TPU v7x, 256 devices: a whole 4x4x8 slice. The times are simulated.
256 devices in a mesh: dp: 64 (over x, z, core), tensor: 4 (over y).
Axes of the slice: x: 4, y: 4, z: 8, core: 2. Of those that a mesh axis runs over, the one named last changes fastest.
Arguments:
- grad_codes: bfloat16 [4, 64, 64, 18432], P(None, 'dp', None, 'tensor'), may hold values from -448 to 448
- exponents: int32 [4, 64, 16], P(None, 'dp'), may hold values from 7 to 10
- accumulated: bfloat16 [64, 18432], P('dp', 'tensor'), may hold values from -12 to 12
- arrival: int32 [64], replicated, may hold values from 0 to 63, each once
- bucket_of_row: int32 [64], replicated, may hold values from 0 to 15, never falling along the last dimension, each value on 1 to 8 neighbouring positions
Outputs:
- unit_codes: bfloat16 [4, 64, 18432], P(None, 'dp', 'tensor')
- bucket_peaks: float32 [4, 16], replicated
- compensated: float32 [64, 18432], P('dp', 'tensor')
Inputs may be any that keep to these rules, and one draw needn't show every extreme that they name: `arrival`: each weight row appears in exactly one slot. `bucket_of_row`: bucket numbers never fall along the rows; each bucket holds 1 to 8 consecutive rows and one holds exactly 8.
All inputs are finite; a program needn't handle non-finite values.
Results may differ from a plain program's by a relative error of at most 0.001.
Values sent between devices are 32-bit elements; how exact they have to be, the bound alone decides.
No kernel may reach another device: no remote copies, remote signals or barrier semaphores. Data moves between devices by JAX's collectives and lax.ppermute only.
A program may use at most 64 MiB of HBM per device.

v0:
```python
import jax
import jax.numpy as jnp
from jax import lax
from jax.sharding import Mesh
from jax.sharding import PartitionSpec as P

NB = 16
DP = ("dp_0", "dp_1", "dp_2")


epsilon = 1e-06


def cut_along(value, dim, peers):
    dims = value.shape
    pieces = value.reshape(*dims[:dim], peers, dims[dim] // peers, *dims[dim + 1 :])
    return jnp.moveaxis(pieces, dim, 0)


def sent_and_summed(value, axis, dim):
    peers = lax.axis_size(axis)
    pieces = lax.all_to_all(cut_along(value, dim, peers), axis, 0, 0, tiled=True)
    return jnp.sum(pieces, axis=0)


def sum_in_two_steps(value, axes, dim):
    far, near = axes
    pieces = cut_along(value, dim, lax.axis_size(far))
    nearer = sent_and_summed(pieces, near, dim + 1)
    arrived = lax.all_to_all(nearer, far, split_axis=0, concat_axis=0, tiled=True)
    return arrived.sum(axis=0)


def copy_for_each(value, axis):
    copies = jnp.broadcast_to(value, (lax.axis_size(axis), *value.shape))
    return lax.all_to_all(copies, axis, split_axis=0, concat_axis=0, tiled=True)


def taken_together(value, axis):
    return copy_for_each(value, axis).max(axis=0)


def by_axis(value, axes):
    far, near = axes
    nearer = taken_together(value, near)
    return taken_together(nearer, far)


def on_device(grad_codes, exponents, accumulated, arrival, bucket_of_row):
    row_count = arrival.shape[0]
    own_rows = accumulated.shape[0]
    step_count = grad_codes.shape[0]
    inverse = (
        jnp.zeros((row_count,), jnp.int32).at[arrival].set(jnp.arange(row_count, dtype=jnp.int32))
    )
    member = bucket_of_row[:, None] == jnp.arange(NB, dtype=jnp.int32)[None, :]
    factors = jnp.exp2(-exponents[:, 0, :].astype(jnp.float32))

    def dequantize(micro_step):
        row_block = jnp.take(grad_codes[micro_step, 0], inverse, axis=0)
        factor_rows = jnp.sum(jnp.where(member, factors[micro_step][None, :], 0.0), axis=1)
        return row_block.astype(jnp.float32) * factor_rows[:, None]

    def all_steps():
        return jnp.stack([dequantize(micro_step) for micro_step in range(step_count)], axis=1)

    stacked = sum_in_two_steps(all_steps(), (("dp_0", "dp_1"), "dp_2"), 0)
    reduced = [stacked[:, micro_step] for micro_step in range(step_count)]
    own_member = lax.dynamic_slice_in_dim(member, lax.axis_index(DP) * own_rows, own_rows, 0)
    running = accumulated
    carried = jnp.zeros(accumulated.shape, jnp.float32)
    exact_sums = []
    local_peaks = []
    for micro_step in range(step_count):
        adjusted = reduced[micro_step] - carried
        previous = running.astype(jnp.float32)
        running = lax.optimization_barrier((previous + adjusted).astype(jnp.bfloat16))
        carried = running.astype(jnp.float32) - previous - adjusted
        exact_sum = running.astype(jnp.float32) - carried
        exact_sums.append(exact_sum)
        row_max = jnp.max(jnp.abs(exact_sum), axis=1)
        local_peak = jnp.max(jnp.where(own_member, row_max[:, None], 0.0), axis=0)
        local_peaks.append(local_peak)
    peak_table = by_axis(jnp.stack(local_peaks), (("dp_0", "dp_1"), ("dp_2", "tensor")))
    scaled_list = []
    for micro_step in range(step_count):
        peak_rows = jnp.sum(jnp.where(own_member, peak_table[micro_step][None, :], 0.0), axis=1)
        scaled_list.append(
            (exact_sums[micro_step] / (peak_rows[:, None] + epsilon)).astype(jnp.bfloat16)
        )
    return (jnp.stack(scaled_list), peak_table, exact_sums[-1])


def solution(mesh):
    finer = Mesh(
        mesh.devices.reshape(4, 8, 2, mesh.shape["tensor"]), ("dp_0", "dp_1", "dp_2", "tensor")
    )
    in_specs = (P(None, DP, None, "tensor"), P(None, DP, None), P(DP, "tensor"), P(), P())
    out_specs = (P(None, DP, "tensor"), P(), P(DP, "tensor"))
    return jax.shard_map(
        on_device, mesh=finer, in_specs=in_specs, out_specs=out_specs, check_vma=False
    )
```

profile of v0, /device:TPU:1, one launch (start us, length us, event | category | flops | bytes accessed | tf_op | source)
XLA Modules:
  0.0 141.9 jit_solution(12415762954318935179)
XLA Ops:
  0.6 0.7 compare_select_fusion.1
  1.3 0.8 scatter_custom_fusion
  2.1 0.5 compare_and_fusion
  2.6 0.7 multiply_exponential_fusion
  3.3 0.5 slice_bitcast_fusion.10
  3.8 1.8 %slice_bitcast_fusion.3 = (bf16[64,4608]{1,0:T(8,128)(2,1)S(1)}, bf16[64,4608]{1,0:T(8,128)(2,1)S(1)}, bf16[64,4608]{1,0:T(8,128)(2,1)S(1)}, bf16[64,4608]{1,0:T(8,128)(2,1)S(1)}) fusion(bf16[4,1,64,4608]{3,2,1,0:T(8,128)(2,1)} %param.7), kind=kLoop, calls=%fused_computation.13 | loop fusion | bytes 4718592 | tf_op jit(solution)/shard_map/squeeze | solution.py:60
  5.6 0.9 gather_fusion
  6.5 0.9 gather_fusion.1
  7.4 0.9 gather_fusion.2
  8.3 0.9 gather_fusion.3
  9.5 2.7 %convert_multiply_fusion.3 = (f32[64,4608]{1,0:T(8,128)S(1)}, f32[64,4608]{1,0:T(8,128)}, f32[64,4608]{1,0:T(8,128)}, f32[64,4608]{1,0:T(8,128)}) fusion(bf16[64,4608]{1,0:T(8,128)(2,1)S(1)} %gather_fusion, f32[64]{0:T(128)S(1)} %get-tuple-element.8, pred[64]{0:T(512)(128)(4,1)} %compare_and_fusion, f32[64]{0:T(128)S(1)} %get-tuple-element.11, ...), kind=kLoop, calls=%fused_computation.9 | loop fusion | flops 3538944 | bytes 7078976 | tf_op jit(solution)/shard_map/mul | solution.py:62
  12.2 0.7 stack.37
  13.2 2.0 %stack.38 = f32[32,2,1,1,4608]{4,1,0,3,2:T(2,128)S(1)} reshape(f32[64,4608]{1,0:T(8,128)} %get-tuple-element.34) | data formatting | bytes 2359296 | tf_op jit(solution)/shard_map/stack | solution.py:65
  15.4 3.0 %stack.39 = f32[32,2,1,1,4608]{4,1,0,3,2:T(2,128)} reshape(f32[64,4608]{1,0:T(8,128)} %get-tuple-element.35) | data formatting | bytes 2359296 | tf_op jit(solution)/shard_map/stack | solution.py:65
  18.4 1.5 %copy.22 = f32[32,2,1,1,4608]{4,0,3,2,1:T(8,128)S(1)} copy(f32[32,2,1,1,4608]{4,1,0,3,2:T(2,128)} %stack.39) | data formatting | bytes 2359296 | tf_op jit(solution)/shard_map/stack | solution.py:65
  19.9 3.0 %stack.40 = f32[32,2,1,1,4608]{4,1,0,3,2:T(2,128)} reshape(f32[64,4608]{1,0:T(8,128)} %get-tuple-element.36) | data formatting | bytes 2359296 | tf_op jit(solution)/shard_map/stack | solution.py:65
  22.9 1.5 %copy.23 = f32[32,2,1,1,4608]{4,0,3,2,1:T(8,128)S(1)} copy(f32[32,2,1,1,4608]{4,1,0,3,2:T(2,128)} %stack.40) | data formatting | bytes 2359296 | tf_op jit(solution)/shard_map/stack | solution.py:65
  24.8 11.4 %all_to_all.20 = f32[2,32,1,4,4608]{4,1,3,2,0:T(8,128)} all-to-all(f32[2,32,1,4,4608]{4,1,3,2,0:T(8,128)S(1)} %maximum_bitcast_fusion), channel_id=1, replica_groups=mesh['dp_0'=4,'dp_1'=8,'dp_2'=2,'tensor'=4] {'dp_2'}, dimensions={0} | all-to-all | bytes 9437184 | tf_op jit(solution)/shard_map/all_to_all | solution.py:22
  36.2 2.9 %reduce_sum.98 = f32[32,4,4608]{2,0,1:T(8,128)S(1)} reduce(f32[2,32,1,4,4608]{4,1,3,2,0:T(8,128)} %all_to_all.20, f32[]{:T(128)} %constant.17.clone.1), dimensions={0,2}, to_apply=%region_5.7 | reduce | flops 589824 | bytes 7077892 | tf_op jit(solution)/shard_map/reduce_sum | solution.py:23
  39.1 2.9 %copy.25 = f32[32,1,4,4608]{3,2,1,0:T(4,128)} copy(f32[32,1,4,4608]{3,0,2,1:T(8,128)S(1)} %bitcast.62) | data formatting | bytes 4718592 | tf_op jit(solution)/shard_map/reduce_sum | solution.py:23
  42.1 9.3 %all-to-all-start.1 = ((f32[32,1,4,4608]{3,2,1,0:T(4,128)}), f32[32,1,4,4608]{3,2,1,0:T(4,128)S(1)}, u32[]{:S(2)}, u32[]{:S(2)}) async-start(f32[32,1,4,4608]{3,2,1,0:T(4,128)} %copy.25), calls=%async_computation.1 | async-start | bytes 4718592 | tf_op jit(solution)/shard_map/all_to_all | solution.py:30
  51.5 54.3 %all-to-all-done.1 = f32[32,1,4,4608]{3,2,1,0:T(4,128)S(1)} async-done(((f32[32,1,4,4608]{3,2,1,0:T(4,128)}), f32[32,1,4,4608]{3,2,1,0:T(4,128)S(1)}, u32[]{:S(2)}, u32[]{:S(2)}) %all-to-all-start.1) | async-done | bytes 2359328 | tf_op jit(solution)/shard_map/all_to_all | solution.py:30
  106.2 0.6 abs_reduce_fusion.3
  106.9 0.7 abs_reduce_fusion.2
  107.6 0.7 abs_reduce_fusion.1
  108.4 0.7 abs_reduce_fusion
  109.0 0.7 broadcast_select_fusion.3
  109.7 1.9 %broadcast_select_fusion.2 = (f32[1,16]{1,0:T(1,128)S(1)}, f32[1,16]{1,0:T(1,128)S(1)}, f32[1,16]{1,0:T(1,128)S(1)}) fusion(pred[1,16]{1,0:T(4,128)(4,1)S(1)} %get-tuple-element.13, f32[]{:T(128)} %get-tuple-element.16, f32[]{:T(128)} %get-tuple-element.20, f32[]{:T(128)} %get-tuple-element.18), kind=kLoop, calls=%fused_computation.62 | loop fusion | flops 48 | bytes 220 | tf_op jit(solution)/shard_map/jit(_where)/select_n | solution.py:82
  111.7 11.2 %all_to_all.21 = f32[8,4,16]{2,1,0:T(4,128)S(1)} all-to-all(f32[8,4,16]{2,1,0:T(4,128)S(1)} %broadcast_in_dim.120), channel_id=1, replica_groups=mesh['dp_0'=4,'dp_1'=8,'dp_2'=2,'tensor'=4] {'dp_2','tensor'}, dimensions={0} | all-to-all | bytes 4096 | tf_op jit(solution)/shard_map/all_to_all | solution.py:36
  122.8 14.9 %all_to_all.22 = f32[32,4,16]{2,1,0:T(4,128)S(1)} all-to-all(f32[32,4,16]{2,1,0:T(4,128)S(1)} %broadcast_in_dim.121), channel_id=1, replica_groups=mesh['dp_0'=4,'dp_1'=8,'dp_2'=2,'tensor'=4] {'dp_0','dp_1'}, dimensions={0} | all-to-all | bytes 16384 | tf_op jit(solution)/shard_map/all_to_all | solution.py:36
  137.8 0.7 select_reduce_fusion.7
  141.2 0.7 pad_maximum_fusion
  (32 shorter events, 1.9 us)
Async XLA Ops:
  8.3 0.9 copy-start.3
  8.3 0.9 copy-start.4
  8.3 0.9 copy-start.5
  42.1 63.7 %all-to-all-start.1 = ((f32[32,1,4,4608]{3,2,1,0:T(4,128)}), f32[32,1,4,4608]{3,2,1,0:T(4,128)S(1)}, u32[]{:S(2)}, u32[]{:S(2)}) async-start(f32[32,1,4,4608]{3,2,1,0:T(4,128)} %copy.25), calls=%async_computation.1 | async-start | bytes 4718592 | tf_op jit(solution)/shard_map/all_to_all | solution.py:30
  51.5 54.7 %copy-start = (bf16[1,4608]{1,0:T(2,128)(2,1)S(1)}, bf16[1,4608]{1,0:T(2,128)(2,1)}, u32[]{:S(2)}) copy-start(bf16[1,4608]{1,0:T(2,128)(2,1)} %param.9) | copy-start | bytes 27652
  109.0 32.8 %copy-start.1 = (f32[1,4608]{1,0:T(1,128)}, f32[1,4608]{1,0:T(1,128)S(1)}, u32[]{:S(2)}) copy-start(f32[1,4608]{1,0:T(1,128)S(1)} %get-tuple-element.21) | copy-start | bytes 55300
  137.8 4.0 %copy-start.2 = (f32[4,16]{1,0:T(4,128)}, f32[4,16]{1,0:T(4,128)S(1)}, u32[]{:S(2)}) copy-start(f32[4,16]{1,0:T(4,128)S(1)} %reduce_max.62) | copy-start | bytes 772
where the time goes:
time: 143 us; the launch traced here: 142 us
  waiting for transfers between devices  54.3 us (38%)
  blocking collectives  37.5 us (26%)
  local copies, waits for them, and re-layouts  21.8 us (15%)
  other arithmetic  15.5 us (11%)
  starting transfers between devices  9.33 us (7%)
  between operations  3.4 us (2%)
    all_to_all x1, waiting for transfers between devices, sum_in_two_steps(): lax.all_to_all(nearer, far, split_axis=0, concat_axis=0, tiled=True)  54.3 us
    all_to_all x2, blocking collectives, copy_for_each(): return lax.all_to_all(copies, axis, split_axis=0, concat_axis=0, tiled=True)  26.1 us
    another operation x8, local copies, waits for them, and re-layouts, all_steps(): jnp.stack([dequantize(micro_step) for micro_step in range(step_count)], a...  12.1 us
    all_to_all x1, blocking collectives, sent_and_summed(): lax.all_to_all(cut_along(value, dim, peers), axis, 0, 0, tiled=True)  11.4 us
    all_to_all x1, starting transfers between devices, sum_in_two_steps(): lax.all_to_all(nearer, far, split_axis=0, concat_axis=0, tiled=True)  9.33 us
    gather x4, local copies, waits for them, and re-layouts, dequantize(): row_block = jnp.take(grad_codes[micro_step, 0], inverse, axis=0)  3.61 us
    reduce_sum x1, local copies, waits for them, and re-layouts, sent_and_summed(): return jnp.sum(pieces, axis=0)  2.93 us
    reduce_sum x1, other arithmetic, sent_and_summed(): return jnp.sum(pieces, axis=0)  2.89 us
  transfers between devices with their start and end apart: 1, of which 1 were waited for; matrix products, arithmetic and copies ran while one was open for 0% of the time, Pallas kernels for 0%

commit v1 on v0

v1 whole, which is shorter than its diff:
```python
import functools

import jax
import jax.numpy as jnp
from jax import lax
from jax.experimental import pallas as pl
from jax.experimental.pallas import tpu as pltpu
from jax.sharding import Mesh
from jax.sharding import PartitionSpec as P

NB = 16
STEPS = 4
ROWS = 64
LANES = 128
EPSILON = 1e-06

NAMES = ("a4", "b3", "a3", "b2", "a2", "b1", "a1")


def where_rows(tiles):
    half = 2 * tiles
    base, at = {}, 0
    for name in NAMES:
        base[name] = at
        at += 8 * half
    for name in ("own_a", "own_b"):
        base[name] = at
        at += 4 * half
    return base, at


def spread_kernel(tiles, place, arrival, bucket, exponents, codes, mine, send, held, sems):
    base, _ = where_rows(tiles)
    half = 2 * tiles
    x, z, c = place[0], place[1], place[2]

    def copy(rel):
        return pltpu.make_async_copy(codes.at[rel ^ (2 * (1 - c))], held.at[rel], sems.at[rel])

    for rel in range(STEPS):
        copy(rel).start()
    row = lax.broadcasted_iota(jnp.int32, (ROWS, ROWS), 0)
    lane = lax.broadcasted_iota(jnp.int32, (ROWS, ROWS), 1)
    k, g = row // 8, row % 8
    to_z = (z + k * (1 - 2 * c)) & 7
    to_x = (x + g % 4) & 3

    def row_ids(own_until):
        owner = jnp.where(k <= own_until, c, 1 - c)
        return (to_x * 8 + to_z) * 2 + (owner ^ (g // 4))

    for rel in range(STEPS):
        ids = row_ids(4 if rel < 2 else 3)
        row_bucket = jnp.sum(jnp.where(ids == lane, bucket[...], 0), axis=1, keepdims=True)
        step = rel ^ (2 * (1 - c))
        power = exponents[pl.ds(step, 1), :]
        mask = row_bucket == lax.broadcasted_iota(jnp.int32, (ROWS, NB), 1)
        power = jnp.sum(jnp.where(mask, power, 0), axis=1, keepdims=True)
        factor = jnp.ones((ROWS, 1), jnp.float32)
        for bit in range(6):
            factor = factor * jnp.where((power >> bit) & 1 == 1, 2.0 ** -(2**bit), 1.0)
        pick = jnp.where(ids == arrival[...], factor, 0.0).astype(jnp.bfloat16)
        copy(rel).wait()
        h = rel % 2
        mine_half, send_half = ("a", "b") if rel < 2 else ("b", "a")
        width = 2 * LANES
        for block in range(tiles * LANES // width):
            part = jnp.dot(
                pick,
                held[rel, :, block * width : (block + 1) * width],
                preferred_element_type=jnp.float32,
            )
            for sub in range(2):
                at = h * tiles + 2 * block + sub
                for group in range(8):
                    piece = part[group * 8 : group * 8 + 8, sub * LANES : (sub + 1) * LANES]
                    if group == 0:
                        mine[pl.ds(base["own_" + mine_half] + at, 4, half), :] = piece[0:4]
                        send[pl.ds(base["own_" + send_half] + at, 4, half), :] = piece[4:8]
                    elif group < 4 or (group == 4 and rel < 2):
                        mine[pl.ds(base[mine_half + str(group)] + at, 8, half), :] = piece
                    else:
                        send[pl.ds(base[send_half + str(8 - group)] + at, 8, half), :] = piece


def spread(place, arrival, bucket, exponents, codes):
    steps, rows, columns = codes.shape
    tiles = columns // LANES
    _, total = where_rows(tiles)
    shape = jax.ShapeDtypeStruct((total, LANES), jnp.float32)
    vmem = pl.BlockSpec(memory_space=pltpu.VMEM)
    return pl.pallas_call(
        functools.partial(spread_kernel, tiles),
        out_shape=(shape, shape),
        in_specs=[
            pl.BlockSpec(memory_space=pltpu.SMEM),
            vmem,
            vmem,
            vmem,
            pl.BlockSpec(memory_space=pl.ANY),
        ],
        out_specs=(vmem, vmem),
        scratch_shapes=[
            pltpu.VMEM((steps, rows, columns), codes.dtype),
            pltpu.SemaphoreType.DMA((steps,)),
        ],
        name="spread",
    )(place, arrival, bucket, exponents, codes)


def join_kernel(half, own_m, own_r, ra, rb, back, *outs):
    both = 4 * half
    for k in range(4):
        rows = slice(k * half, (k + 1) * half)
        other = slice(both + k * half, both + (k + 1) * half)
        outs[k][0:half] = own_m[rows] + own_r[rows] + ra[rows] + back[other]
        outs[k][half : 2 * half] = own_m[other] + own_r[other] + rb[rows] + back[rows]


def chain_kernel(tiles, place, bucket, t0, t1, t2, t3, start, exact, compensated, peaks):
    c = place[2]
    mine = bucket[(place[0] * 8 + place[1]) * 2 + c]
    total = t0[...] + t1[...] + t2[...] + t3[...]
    running = start[...].astype(jnp.float32)
    carried = jnp.zeros_like(running)
    lane = lax.broadcasted_iota(jnp.int32, (1, LANES), 1)
    table = jnp.zeros((1, LANES), jnp.float32)
    for step in range(STEPS):
        first, second = (step ^ 2) * tiles, step * tiles
        reduced = jnp.where(c == 0, total[first : first + tiles], total[second : second + tiles])
        adjusted = reduced - carried
        new = (running + adjusted).astype(jnp.bfloat16).astype(jnp.float32)
        carried = (new - running) - adjusted
        running = new
        value = running - carried
        peak = jnp.max(jnp.max(jnp.abs(value), axis=0, keepdims=True), axis=1, keepdims=True)
        table = jnp.where(lane == step * NB + mine, peak, table)
        for t in range(tiles):
            exact[step : step + 1, t * LANES : (t + 1) * LANES] = value[t : t + 1]
            if step == STEPS - 1:
                compensated[:, t * LANES : (t + 1) * LANES] = value[t : t + 1]
    peaks[...] = table


def scale_kernel(place, bucket, exact, tables, units, peaks):
    mine = bucket[(place[0] * 8 + place[1]) * 2 + place[2]]
    table = jnp.max(tables[...], axis=0, keepdims=True)
    lane = lax.broadcasted_iota(jnp.int32, (STEPS, LANES), 1)
    step = lax.broadcasted_iota(jnp.int32, (STEPS, LANES), 0)
    spot = lane == step * NB + mine
    peak = jnp.max(jnp.where(spot, jnp.broadcast_to(table, spot.shape), 0.0), axis=1, keepdims=True)
    units[...] = (exact[...] / (peak + EPSILON)).astype(units.dtype)
    for s in range(STEPS):
        peaks[s : s + 1, :] = table[:, s * NB : (s + 1) * NB]


def on_device(grad_codes, exponents, accumulated, arrival, bucket_of_row):
    columns = accumulated.shape[1]
    tiles = columns // LANES
    half = 2 * tiles
    base, _ = where_rows(tiles)
    place = jnp.stack([lax.axis_index("x"), lax.axis_index("z"), lax.axis_index("c")])
    nz = lax.axis_size("z")
    vmem = pl.BlockSpec(memory_space=pltpu.VMEM)
    smem = pl.BlockSpec(memory_space=pltpu.SMEM)

    mine, send = spread(
        place, arrival[None, :], bucket_of_row[None, :], exponents[:, 0, :], grad_codes[:, 0]
    )
    swap = [(0, 1), (1, 0)]
    got = lax.ppermute(send, "c", swap)

    def part(name):
        rows = slice(base[name], base[name] + 8 * half)
        return mine[rows] + got[rows]

    turn = []
    for z in range(nz):
        turn.append((2 * z, 2 * ((z + 1) % nz)))
        turn.append((2 * z + 1, 2 * ((z - 1) % nz) + 1))
    ring = functools.partial(lax.ppermute, axis_name=("z", "c"), perm=turn)
    ra = ring(part("a4"))
    rb = ring(part("b3"))
    ra = ring(part("a3") + ra)
    rb = ring(part("b2") + rb)
    ra = ring(part("a2") + ra)
    rb = ring(part("b1") + rb)
    ra = ring(part("a1") + ra)
    cut = 4 * half
    back = lax.ppermute(jnp.concatenate([ra[cut:], rb[cut:]]), "c", swap)
    own = base["own_a"]
    piece = jax.ShapeDtypeStruct((2 * half, LANES), jnp.float32)
    pieces = pl.pallas_call(
        functools.partial(join_kernel, half),
        out_shape=(piece,) * 4,
        in_specs=[vmem] * 5,
        out_specs=(vmem,) * 4,
        name="join",
    )(mine[own:], got[own:], ra[:cut], rb[:cut], back)
    totals = [pieces[0]]
    for k in range(1, 4):
        totals.append(lax.ppermute(pieces[k], "x", [(i, (i + k) % 4) for i in range(4)]))
    exact, compensated, table = pl.pallas_call(
        functools.partial(chain_kernel, tiles),
        out_shape=(
            jax.ShapeDtypeStruct((STEPS, columns), jnp.float32),
            jax.ShapeDtypeStruct((1, columns), jnp.float32),
            jax.ShapeDtypeStruct((1, LANES), jnp.float32),
        ),
        in_specs=[smem, smem] + [vmem] * 5,
        out_specs=(vmem,) * 3,
        name="chain",
    )(place, bucket_of_row, *totals, accumulated.reshape(tiles, LANES))
    table = jnp.maximum(table, lax.ppermute(table, "c", swap))
    count = lax.axis_size(("x", "z", "y"))
    copies = jnp.broadcast_to(table[None], (count, 1, LANES))
    tables = lax.all_to_all(copies, ("x", "z", "y"), 0, 0, tiled=True)
    units, peaks = pl.pallas_call(
        scale_kernel,
        out_shape=(
            jax.ShapeDtypeStruct((STEPS, columns), jnp.bfloat16),
            jax.ShapeDtypeStruct((STEPS, NB), jnp.float32),
        ),
        in_specs=[smem, smem] + [vmem] * 2,
        out_specs=(vmem,) * 2,
        name="scale",
    )(place, bucket_of_row, exact, tables.reshape(count, LANES))
    return units[:, None, :], peaks, compensated


def solution(mesh):
    finer = Mesh(mesh.devices.reshape(4, 8, 2, mesh.shape["tensor"]), ("x", "z", "c", "y"))
    dp = ("x", "z", "c")
    in_specs = (P(None, dp, None, "y"), P(None, dp, None), P(dp, "y"), P(), P())
    out_specs = (P(None, dp, "y"), P(), P(dp, "y"))
    return jax.shard_map(
        on_device, mesh=finer, in_specs=in_specs, out_specs=out_specs, check_vma=False
    )
```

time: 143 us -> 113 us (0.79)
  starting transfers between devices: 9.33 us -> 37 us
  waiting for transfers between devices: 54.3 us -> 31.1 us
  local copies, waits for them, and re-layouts: 21.8 us -> 2.74 us
  blocking collectives: 37.5 us -> 21.4 us
  Pallas kernels: 0 us -> 10.8 us
  other arithmetic: 15.5 us -> 9.1 us
  between operations: 3.4 us -> 0.69 us
    all_to_all x1 -> x0, waiting for transfers between devices: 54.3 us -> none  [sum_in_two_steps(): lax.all_to_all(nearer, far, split_axis=0, concat_axis=0, tiled=True)]
    ppermute x0 -> x13, starting transfers between devices: none -> 37 us  [the longest x1 7.53 us: on_device(): back = lax.ppermute(jnp.concatenate([ra[cut:], rb[cut:]]), 'c', swap)]
    ppermute x0 -> x13, waiting for transfers between devices: none -> 31.1 us  [the longest x1 4.37 us: on_device(): got = lax.ppermute(send, 'c', swap)]
    all_to_all x3 -> x1, blocking collectives: 37.5 us -> 21.4 us  [on_device(): tables = lax.all_to_all(copies, ('x', 'z', 'y'), 0, 0, tiled=True)]
    another operation x8 -> x0, local copies, waits for them, and re-layouts: 12.1 us -> none  [all_steps(): jnp.stack([dequantize(micro_step) for micro_step in range(step_count)], a...]
    pallas_call x0 -> x4, Pallas kernels: none -> 10.8 us  [the longest x1 5.48 us: spread(): pl.pallas_call(functools.partial(spread_kernel, tiles), out_shape=(shape,...]
    all_to_all x1 -> x0, starting transfers between devices: 9.33 us -> none  [sum_in_two_steps(): lax.all_to_all(nearer, far, split_axis=0, concat_axis=0, tiled=True)]
    add x0 -> x6, other arithmetic: none -> 7.15 us  [the longest x1 2.1 us: on_device(): rb = ring(part('b1') + rb)]
  transfers between devices with their start and end apart: 1 -> 13, of which waited for: 1 -> 11; matrix products, arithmetic and copies ran while one was open for 0% -> 2% of each run, Pallas kernels for 0% -> 0%
where the time goes in v1:
time: 113 us
  starting transfers between devices  37 us (33%)
  waiting for transfers between devices  31.1 us (28%)
  blocking collectives  21.4 us (19%)
  Pallas kernels  10.8 us (10%)
  other arithmetic  9.1 us (8%)
  local copies, waits for them, and re-layouts  2.74 us (2%)
    all_to_all x1, blocking collectives, on_device(): tables = lax.all_to_all(copies, ('x', 'z', 'y'), 0, 0, tiled=True)  21.4 us
    ppermute x1, starting transfers between devices, on_device(): back = lax.ppermute(jnp.concatenate([ra[cut:], rb[cut:]]), 'c', swap)  7.53 us
    pallas_call x1, Pallas kernels, spread(): pl.pallas_call(functools.partial(spread_kernel, tiles), out_shape=(shape,...  5.48 us
    ppermute x1, waiting for transfers between devices, on_device(): got = lax.ppermute(send, 'c', swap)  4.37 us
    ppermute x3, starting transfers between devices, on_device(): lax.ppermute(pieces[k], 'x', [(i, (i + k) % 4) for i in range(4)])  4.22 us
    ppermute x1, starting transfers between devices, on_device(): rb = ring(part('b3'))  3.94 us
    ppermute x1, waiting for transfers between devices, on_device(): rb = ring(part('b3'))  3.67 us
    ppermute x1, waiting for transfers between devices, on_device(): rb = ring(part('b2') + rb)  3.67 us
  transfers between devices with their start and end apart: 13, of which 11 were waited for; matrix products, arithmetic and copies ran while one was open for 2% of the time, Pallas kernels for 0%

profile of v1, /device:TPU:1, one launch (start us, length us, event | category | flops | bytes accessed | tf_op | source)
XLA Modules:
  0.0 112.8 jit_solution(9417159022755813639)
XLA Ops:
  1.2 5.5 %spread.1 = (f32[4608,128]{1,0:T(8,128)}, f32[4608,128]{1,0:T(8,128)}) custom-call(s32[3]{0:T(128)} %pad_add_fusion.place, s32[1,64]{1,0:T(1,128)} %bitcast.17, s32[1,64]{1,0:T(1,128)} %bitcast.15, s32[4,16]{1,0:T(4,128)} %bitcast.16, bf16[4,64,4608]{2,1,0:T(8,128)(2,1)} %bitcast.12), custom_call_target="tpu_custom_call" | custom-call | tf_op jit(solution)/shard_map/spread/pallas_call | solution.py:92
  6.7 3.3 %collective-permute-start = (f32[4608,128]{1,0:T(8,128)}, f32[4608,128]{1,0:T(8,128)S(1)}, u32[]{:S(2)}, u32[]{:S(2)}) collective-permute-start(f32[4608,128]{1,0:T(8,128)} %get-tuple-element.15), channel_id=1, source_target_pairs={{0,4},{4,0},{1,5},{5,1},{2,6},{6,2},{3,7},{7,3},{8,12},{12,8},{9,1... | collective-permute-start | bytes 7077896 | tf_op jit(solution)/shard_map/ppermute | solution.py:171
  10.0 4.4 %collective-permute-done = f32[4608,128]{1,0:T(8,128)S(1)} collective-permute-done((f32[4608,128]{1,0:T(8,128)}, f32[4608,128]{1,0:T(8,128)S(1)}, u32[]{:S(2)}, u32[]{:S(2)}) %collective-permute-start) | collective-permute-done | bytes 2359328 | tf_op jit(solution)/shard_map/ppermute | solution.py:171
  14.4 1.0 slice_add_fusion
  15.4 3.9 %collective-permute-start.5 = (f32[576,128]{1,0:T(8,128)S(1)}, f32[576,128]{1,0:T(8,128)S(1)}, u32[]{:S(2)}, u32[]{:S(2)}) collective-permute-start(f32[576,128]{1,0:T(8,128)S(1)} %slice_add_fusion), channel_id=1, source_target_pairs={{0,8},{4,60},{8,16},{12,4},{16,24},{20,12},{24,32},{28,20},{32,40}... | collective-permute-start | bytes 884744 | tf_op jit(solution)/shard_map/ppermute | solution.py:183
  19.3 3.7 %collective-permute-done.5 = f32[576,128]{1,0:T(8,128)S(1)} collective-permute-done((f32[576,128]{1,0:T(8,128)S(1)}, f32[576,128]{1,0:T(8,128)S(1)}, u32[]{:S(2)}, u32[]{:S(2)}) %collective-permute-start.5) | collective-permute-done | bytes 294944 | tf_op jit(solution)/shard_map/ppermute | solution.py:183
  23.0 1.0 fusion
  24.0 3.2 %collective-permute-start.6 = (f32[576,128]{1,0:T(8,128)S(1)}, f32[576,128]{1,0:T(8,128)S(1)}, u32[]{:S(2)}, u32[]{:S(2)}) collective-permute-start(f32[576,128]{1,0:T(8,128)S(1)} %fusion), channel_id=1, source_target_pairs={{0,8},{4,60},{8,16},{12,4},{16,24},{20,12},{24,32},{28,20},{32,40}... | collective-permute-start | bytes 884744 | tf_op jit(solution)/shard_map/ppermute | solution.py:185
  27.2 3.7 %collective-permute-done.6 = f32[576,128]{1,0:T(8,128)S(1)} collective-permute-done((f32[576,128]{1,0:T(8,128)S(1)}, f32[576,128]{1,0:T(8,128)S(1)}, u32[]{:S(2)}, u32[]{:S(2)}) %collective-permute-start.6) | collective-permute-done | bytes 294944 | tf_op jit(solution)/shard_map/ppermute | solution.py:185
  30.9 2.1 %fusion.1 = (f32[576,128]{1,0:T(8,128)S(1)}, f32[576,128]{1,0:T(8,128)S(1)}, f32[576,128]{1,0:T(8,128)}, f32[576,128]{1,0:T(8,128)}) fusion(f32[576,128]{1,0:T(8,128)S(1)} %collective-permute-done.6, f32[4608,128]{1,0:T(8,128)S(1)} %collective-permute-done, f32[4608,128]{1,0:T(8,128)} %get-tuple-element.14), kind=kLoop, calls=%fused_computation.4 | loop fusion | flops 221184 | bytes 3244032 | tf_op jit(solution)/shard_map/add | solution.py:187
  33.0 3.1 %collective-permute-start.1 = (f32[576,128]{1,0:T(8,128)S(1)}, f32[576,128]{1,0:T(8,128)S(1)}, u32[]{:S(2)}, u32[]{:S(2)}) collective-permute-start(f32[576,128]{1,0:T(8,128)S(1)} %get-tuple-element.26), channel_id=1, source_target_pairs={{0,8},{4,60},{8,16},{12,4},{16,24},{20,12},{24,32},{28,20},{32,40}... | collective-permute-start | bytes 884744 | tf_op jit(solution)/shard_map/ppermute | solution.py:182
  36.1 3.7 %collective-permute-done.1 = f32[576,128]{1,0:T(8,128)S(1)} collective-permute-done((f32[576,128]{1,0:T(8,128)S(1)}, f32[576,128]{1,0:T(8,128)S(1)}, u32[]{:S(2)}, u32[]{:S(2)}) %collective-permute-start.1) | collective-permute-done | bytes 294944 | tf_op jit(solution)/shard_map/ppermute | solution.py:182
  39.8 1.0 fusion.2
  40.8 3.2 %collective-permute-start.2 = (f32[576,128]{1,0:T(8,128)S(1)}, f32[576,128]{1,0:T(8,128)S(1)}, u32[]{:S(2)}, u32[]{:S(2)}) collective-permute-start(f32[576,128]{1,0:T(8,128)S(1)} %fusion.2), channel_id=1, source_target_pairs={{0,8},{4,60},{8,16},{12,4},{16,24},{20,12},{24,32},{28,20},{32,40}... | collective-permute-start | bytes 884744 | tf_op jit(solution)/shard_map/ppermute | solution.py:184
  44.0 3.7 %collective-permute-done.2 = f32[576,128]{1,0:T(8,128)S(1)} collective-permute-done((f32[576,128]{1,0:T(8,128)S(1)}, f32[576,128]{1,0:T(8,128)S(1)}, u32[]{:S(2)}, u32[]{:S(2)}) %collective-permute-start.2) | collective-permute-done | bytes 294944 | tf_op jit(solution)/shard_map/ppermute | solution.py:184
  47.6 1.0 fusion.3
  48.7 3.2 %collective-permute-start.3 = (f32[576,128]{1,0:T(8,128)S(1)}, f32[576,128]{1,0:T(8,128)S(1)}, u32[]{:S(2)}, u32[]{:S(2)}) collective-permute-start(f32[576,128]{1,0:T(8,128)S(1)} %fusion.3), channel_id=1, source_target_pairs={{0,8},{4,60},{8,16},{12,4},{16,24},{20,12},{24,32},{28,20},{32,40}... | collective-permute-start | bytes 884744 | tf_op jit(solution)/shard_map/ppermute | solution.py:186
  51.9 3.6 %collective-permute-done.3 = f32[576,128]{1,0:T(8,128)S(1)} collective-permute-done((f32[576,128]{1,0:T(8,128)S(1)}, f32[576,128]{1,0:T(8,128)S(1)}, u32[]{:S(2)}, u32[]{:S(2)}) %collective-permute-start.3) | collective-permute-done | bytes 294944 | tf_op jit(solution)/shard_map/ppermute | solution.py:186
  55.5 1.0 fusion.4
  56.5 3.2 %collective-permute-start.4 = (f32[576,128]{1,0:T(8,128)S(1)}, f32[576,128]{1,0:T(8,128)S(1)}, u32[]{:S(2)}, u32[]{:S(2)}) collective-permute-start(f32[576,128]{1,0:T(8,128)S(1)} %fusion.4), channel_id=1, source_target_pairs={{0,8},{4,60},{8,16},{12,4},{16,24},{20,12},{24,32},{28,20},{32,40}... | collective-permute-start | bytes 884744 | tf_op jit(solution)/shard_map/ppermute | solution.py:188
  60.4 3.0 %collective-permute-done.4 = f32[576,128]{1,0:T(8,128)S(1)} collective-permute-done((f32[576,128]{1,0:T(8,128)S(1)}, f32[576,128]{1,0:T(8,128)S(1)}, u32[]{:S(2)}, u32[]{:S(2)}) %collective-permute-start.4) | collective-permute-done | bytes 294944 | tf_op jit(solution)/shard_map/ppermute | solution.py:188
  64.1 7.5 %collective-permute-start.8 = (f32[576,128]{1,0:T(8,128)S(1)}, f32[576,128]{1,0:T(8,128)S(1)}, u32[]{:S(2)}, u32[]{:S(2)}) collective-permute-start(f32[576,128]{1,0:T(8,128)S(1)} %pad_maximum_fusion), channel_id=1, source_target_pairs={{0,4},{4,0},{1,5},{5,1},{2,6},{6,2},{3,7},{7,3},{8,12},{12,8},{9,1... | collective-permute-start | bytes 884744 | tf_op jit(solution)/shard_map/ppermute | solution.py:190
  71.6 1.2 %collective-permute-done.8.back = f32[576,128]{1,0:T(8,128)S(1)} collective-permute-done((f32[576,128]{1,0:T(8,128)S(1)}, f32[576,128]{1,0:T(8,128)S(1)}, u32[]{:S(2)}, u32[]{:S(2)}) %collective-permute-start.8) | collective-permute-done | bytes 294944 | tf_op jit(solution)/shard_map/ppermute | solution.py:190
  73.6 2.0 %join.1 = (f32[144,128]{1,0:T(8,128)}, f32[144,128]{1,0:T(8,128)}, f32[144,128]{1,0:T(8,128)}, f32[144,128]{1,0:T(8,128)}) custom-call(f32[576,128]{1,0:T(8,128)} %get-tuple-element.27.own_m, f32[576,128]{1,0:T(8,128)} %get-tuple-element.28.own_r, f32[288,128]{1,0:T(8,128)} %get-tuple-element.30.ra, f32[288,128]{1,0:T(8,128)} %get-tuple-element.32.rb, ...), custom_call_target="tpu_custom_call" | custom-call | tf_op jit(solution)/shard_map/join/pallas_call | solution.py:193
  75.6 2.8 %collective-permute-start.10 = (f32[144,128]{1,0:T(8,128)}, f32[144,128]{1,0:T(8,128)S(1)}, u32[]{:S(2)}, u32[]{:S(2)}) collective-permute-start(f32[144,128]{1,0:T(8,128)} %get-tuple-element.18), channel_id=1, source_target_pairs={{0,128},{64,192},{128,0},{192,64},{1,129},{65,193},{129,1},{193,65... | collective-permute-start | bytes 221192 | tf_op jit(solution)/shard_map/ppermute | solution.py:202
  80.5 2.2 %collective-permute-done.11.t3 = f32[144,128]{1,0:T(8,128)S(1)} collective-permute-done((f32[144,128]{1,0:T(8,128)}, f32[144,128]{1,0:T(8,128)S(1)}, u32[]{:S(2)}, u32[]{:S(2)}) %collective-permute-start.11) | collective-permute-done | bytes 73760 | tf_op jit(solution)/shard_map/ppermute | solution.py:202
  82.7 1.1 collective-permute-done.9.t1
  84.4 1.7 %chain.1 = (f32[4,4608]{1,0:T(4,128)}, f32[1,4608]{1,0:T(1,128)}, f32[1,128]{1,0:T(1,128)}) custom-call(s32[3]{0:T(128)} %pad_add_fusion.place, s32[64]{0:T(128)} %bucket.3, f32[144,128]{1,0:T(8,128)} %get-tuple-element.16.t0, f32[144,128]{1,0:T(8,128)} %copy-done.3, f32[144,128]{1,0:T(8,128)} %copy-done.1, f32[144,128]{1,0:T(8,128)} %copy-done.2, ...), custom_call_target="tpu_custom_call" | custom-call | tf_op jit(solution)/shard_map/chain/pallas_call | solution.py:203
  86.1 2.1 %collective-permute-start.12 = (f32[1,128]{1,0:T(1,128)}, f32[1,128]{1,0:T(1,128)S(1)}, u32[]{:S(2)}, u32[]{:S(2)}) collective-permute-start(f32[1,128]{1,0:T(1,128)} %get-tuple-element.21), channel_id=1, source_target_pairs={{0,4},{4,0},{1,5},{5,1},{2,6},{6,2},{3,7},{7,3},{8,12},{12,8},{9,1... | collective-permute-start | bytes 1544 | tf_op jit(solution)/shard_map/ppermute | solution.py:214
  88.2 1.0 collective-permute-done.12
  89.9 21.4 %all_to_all.5 = f32[128,1,128]{2,1,0:T(1,128)} all-to-all(f32[128,1,128]{2,1,0:T(1,128)S(1)} %broadcast_in_dim.20), channel_id=1, replica_groups=mesh['x'=4,'z'=8,'c'=2,'y'=4] {'x','z','y'}, dimensions={0} | all-to-all | bytes 131072 | tf_op jit(solution)/shard_map/all_to_all | solution.py:217
  111.2 1.6 %scale.1 = (bf16[4,4608]{1,0:T(4,128)(2,1)}, f32[4,16]{1,0:T(4,128)}) custom-call(s32[3]{0:T(128)} %pad_add_fusion.place, s32[64]{0:T(128)} %bucket.3, f32[4,4608]{1,0:T(4,128)} %get-tuple-element.20.exact, f32[128,128]{1,0:T(8,128)} %bitcast.13), custom_call_target="tpu_custom_call" | custom-call | tf_op jit(solution)/shard_map/scale/pallas_call | solution.py:218
  (22 shorter events, 6.3 us)
Async XLA Ops:
  6.7 7.7 %collective-permute-start = (f32[4608,128]{1,0:T(8,128)}, f32[4608,128]{1,0:T(8,128)S(1)}, u32[]{:S(2)}, u32[]{:S(2)}) collective-permute-start(f32[4608,128]{1,0:T(8,128)} %get-tuple-element.15), channel_id=1, source_target_pairs={{0,4},{4,0},{1,5},{5,1},{2,6},{6,2},{3,7},{7,3},{8,12},{12,8},{9,1... | collective-permute-start | bytes 7077896 | tf_op jit(solution)/shard_map/ppermute | solution.py:171
  15.4 7.6 %collective-permute-start.5 = (f32[576,128]{1,0:T(8,128)S(1)}, f32[576,128]{1,0:T(8,128)S(1)}, u32[]{:S(2)}, u32[]{:S(2)}) collective-permute-start(f32[576,128]{1,0:T(8,128)S(1)} %slice_add_fusion), channel_id=1, source_target_pairs={{0,8},{4,60},{8,16},{12,4},{16,24},{20,12},{24,32},{28,20},{32,40}... | collective-permute-start | bytes 884744 | tf_op jit(solution)/shard_map/ppermute | solution.py:183
  24.0 6.9 %collective-permute-start.6 = (f32[576,128]{1,0:T(8,128)S(1)}, f32[576,128]{1,0:T(8,128)S(1)}, u32[]{:S(2)}, u32[]{:S(2)}) collective-permute-start(f32[576,128]{1,0:T(8,128)S(1)} %fusion), channel_id=1, source_target_pairs={{0,8},{4,60},{8,16},{12,4},{16,24},{20,12},{24,32},{28,20},{32,40}... | collective-permute-start | bytes 884744 | tf_op jit(solution)/shard_map/ppermute | solution.py:185
  33.0 6.8 %collective-permute-start.1 = (f32[576,128]{1,0:T(8,128)S(1)}, f32[576,128]{1,0:T(8,128)S(1)}, u32[]{:S(2)}, u32[]{:S(2)}) collective-permute-start(f32[576,128]{1,0:T(8,128)S(1)} %get-tuple-element.26), channel_id=1, source_target_pairs={{0,8},{4,60},{8,16},{12,4},{16,24},{20,12},{24,32},{28,20},{32,40}... | collective-permute-start | bytes 884744 | tf_op jit(solution)/shard_map/ppermute | solution.py:182
  40.8 6.9 %collective-permute-start.2 = (f32[576,128]{1,0:T(8,128)S(1)}, f32[576,128]{1,0:T(8,128)S(1)}, u32[]{:S(2)}, u32[]{:S(2)}) collective-permute-start(f32[576,128]{1,0:T(8,128)S(1)} %fusion.2), channel_id=1, source_target_pairs={{0,8},{4,60},{8,16},{12,4},{16,24},{20,12},{24,32},{28,20},{32,40}... | collective-permute-start | bytes 884744 | tf_op jit(solution)/shard_map/ppermute | solution.py:184
  48.7 31.1 %copy-start.4 = (bf16[1,4608]{1,0:T(2,128)(2,1)S(1)}, bf16[1,4608]{1,0:T(2,128)(2,1)}, u32[]{:S(2)}) copy-start(bf16[1,4608]{1,0:T(2,128)(2,1)} %param.7) | copy-start | bytes 27652
  48.7 6.9 %collective-permute-start.3 = (f32[576,128]{1,0:T(8,128)S(1)}, f32[576,128]{1,0:T(8,128)S(1)}, u32[]{:S(2)}, u32[]{:S(2)}) collective-permute-start(f32[576,128]{1,0:T(8,128)S(1)} %fusion.3), channel_id=1, source_target_pairs={{0,8},{4,60},{8,16},{12,4},{16,24},{20,12},{24,32},{28,20},{32,40}... | collective-permute-start | bytes 884744 | tf_op jit(solution)/shard_map/ppermute | solution.py:186
  51.9 7.9 %collective-permute-start.7 = (f32[576,128]{1,0:T(8,128)S(1)}, f32[576,128]{1,0:T(8,128)S(1)}, u32[]{:S(2)}, u32[]{:S(2)}) collective-permute-start(f32[576,128]{1,0:T(8,128)S(1)} %get-tuple-element.25), channel_id=1, source_target_pairs={{0,8},{4,60},{8,16},{12,4},{16,24},{20,12},{24,32},{28,20},{32,40}... | collective-permute-start | bytes 884744 | tf_op jit(solution)/shard_map/ppermute | solution.py:187
  56.5 6.9 %collective-permute-start.4 = (f32[576,128]{1,0:T(8,128)S(1)}, f32[576,128]{1,0:T(8,128)S(1)}, u32[]{:S(2)}, u32[]{:S(2)}) collective-permute-start(f32[576,128]{1,0:T(8,128)S(1)} %fusion.4), channel_id=1, source_target_pairs={{0,8},{4,60},{8,16},{12,4},{16,24},{20,12},{24,32},{28,20},{32,40}... | collective-permute-start | bytes 884744 | tf_op jit(solution)/shard_map/ppermute | solution.py:188
  64.1 8.7 %collective-permute-start.8 = (f32[576,128]{1,0:T(8,128)S(1)}, f32[576,128]{1,0:T(8,128)S(1)}, u32[]{:S(2)}, u32[]{:S(2)}) collective-permute-start(f32[576,128]{1,0:T(8,128)S(1)} %pad_maximum_fusion), channel_id=1, source_target_pairs={{0,4},{4,0},{1,5},{5,1},{2,6},{6,2},{3,7},{7,3},{8,12},{12,8},{9,1... | collective-permute-start | bytes 884744 | tf_op jit(solution)/shard_map/ppermute | solution.py:190
  72.8 0.7 copy-start
  75.6 4.9 %collective-permute-start.10 = (f32[144,128]{1,0:T(8,128)}, f32[144,128]{1,0:T(8,128)S(1)}, u32[]{:S(2)}, u32[]{:S(2)}) collective-permute-start(f32[144,128]{1,0:T(8,128)} %get-tuple-element.18), channel_id=1, source_target_pairs={{0,128},{64,192},{128,0},{192,64},{1,129},{65,193},{129,1},{193,65... | collective-permute-start | bytes 221192 | tf_op jit(solution)/shard_map/ppermute | solution.py:202
  78.3 4.4 %collective-permute-start.11 = (f32[144,128]{1,0:T(8,128)}, f32[144,128]{1,0:T(8,128)S(1)}, u32[]{:S(2)}, u32[]{:S(2)}) collective-permute-start(f32[144,128]{1,0:T(8,128)} %get-tuple-element.19), channel_id=1, source_target_pairs={{0,192},{64,0},{128,64},{192,128},{1,193},{65,1},{129,65},{193,129... | collective-permute-start | bytes 221192 | tf_op jit(solution)/shard_map/ppermute | solution.py:202
  79.2 4.6 %collective-permute-start.9 = (f32[144,128]{1,0:T(8,128)}, f32[144,128]{1,0:T(8,128)S(1)}, u32[]{:S(2)}, u32[]{:S(2)}) collective-permute-start(f32[144,128]{1,0:T(8,128)} %get-tuple-element.17), channel_id=1, source_target_pairs={{0,64},{64,128},{128,192},{192,0},{1,65},{65,129},{129,193},{193,1... | collective-permute-start | bytes 221192 | tf_op jit(solution)/shard_map/ppermute | solution.py:202
  80.5 3.3 %copy-start.1 = (f32[144,128]{1,0:T(8,128)}, f32[144,128]{1,0:T(8,128)S(1)}, u32[]{:S(2)}) copy-start(f32[144,128]{1,0:T(8,128)S(1)} %collective-permute-done.10.t2) | copy-start | bytes 221188
  82.7 1.1 copy-start.2
  83.8 0.6 copy-start.3
  86.1 3.0 %collective-permute-start.12 = (f32[1,128]{1,0:T(1,128)}, f32[1,128]{1,0:T(1,128)S(1)}, u32[]{:S(2)}, u32[]{:S(2)}) collective-permute-start(f32[1,128]{1,0:T(1,128)} %get-tuple-element.21), channel_id=1, source_target_pairs={{0,4},{4,0},{1,5},{5,1},{2,6},{6,2},{3,7},{7,3},{8,12},{12,8},{9,1... | collective-permute-start | bytes 1544 | tf_op jit(solution)/shard_map/ppermute | solution.py:214

commit v2 on v1

--- a/solution.py
+++ b/solution.py
@@ -8,6 +8,7 @@
 from jax.sharding import Mesh
 from jax.sharding import PartitionSpec as P
 
+
 NB = 16
 STEPS = 4
 ROWS = 64
@@ -15,24 +16,33 @@
 EPSILON = 1e-06
 
 NAMES = ("a4", "b3", "a3", "b2", "a2", "b1", "a1")
+EARLY = ("a4", "b3")
+
+
+def room(mib):
+    return pltpu.CompilerParams(vmem_limit_bytes=mib * 2**20)
 
 
 def where_rows(tiles):
     half = 2 * tiles
-    base, at = {}, 0
-    for name in NAMES:
-        base[name] = at
-        at += 8 * half
-    for name in ("own_a", "own_b"):
-        base[name] = at
-        at += 4 * half
-    return base, at
-
-
-def spread_kernel(tiles, place, arrival, bucket, exponents, codes, mine, send, held, sems):
+    base, sizes = {}, [0, 0]
+    for name in NAMES + ("own_a", "own_b"):
+        late = int(name not in EARLY)
+        base[name] = (late, sizes[late])
+        sizes[late] += (4 if name.startswith("own") else 8) * half
+    return base, sizes
+
+
+def spread_kernel(tiles, place, arrival, bucket, exponents, codes, mine0, mine1, send0, send1, held, sems):
     base, _ = where_rows(tiles)
     half = 2 * tiles
     x, z, c = place[0], place[1], place[2]
+
+    def put(outs, name, at, count, value):
+        late, first = base[name]
+        outs[late][pl.ds(first + at, count, half), :] = value
+
+    mine, send = (mine0, mine1), (send0, send1)
 
     def copy(rel):
         return pltpu.make_async_copy(codes.at[rel ^ (2 * (1 - c))], held.at[rel], sems.at[rel])
@@ -75,46 +85,58 @@
                 for group in range(8):
                     piece = part[group * 8 : group * 8 + 8, sub * LANES : (sub + 1) * LANES]
                     if group == 0:
-                        mine[pl.ds(base["own_" + mine_half] + at, 4, half), :] = piece[0:4]
-                        send[pl.ds(base["own_" + send_half] + at, 4, half), :] = piece[4:8]
+                        put(mine, "own_" + mine_half, at, 4, piece[0:4])
+                        put(send, "own_" + send_half, at, 4, piece[4:8])
                     elif group < 4 or (group == 4 and rel < 2):
-                        mine[pl.ds(base[mine_half + str(group)] + at, 8, half), :] = piece
+                        put(mine, mine_half + str(group), at, 8, piece)
                     else:
-                        send[pl.ds(base[send_half + str(8 - group)] + at, 8, half), :] = piece
+                        put(send, send_half + str(8 - group), at, 8, piece)
 
 
 def spread(place, arrival, bucket, exponents, codes):
     steps, rows, columns = codes.shape
     tiles = columns // LANES
-    _, total = where_rows(tiles)
-    shape = jax.ShapeDtypeStruct((total, LANES), jnp.float32)
+    shapes = tuple(
+        jax.ShapeDtypeStruct((size, LANES), jnp.float32) for size in where_rows(tiles)[1]
+    )
     vmem = pl.BlockSpec(memory_space=pltpu.VMEM)
     return pl.pallas_call(
         functools.partial(spread_kernel, tiles),
-        out_shape=(shape, shape),
+        out_shape=shapes + shapes,
         in_specs=[
             pl.BlockSpec(memory_space=pltpu.SMEM),
             vmem,
             vmem,
             vmem,
-            pl.BlockSpec(memory_space=pl.ANY),
+            pl.BlockSpec(memory_space=pltpu.HBM),
         ],
-        out_specs=(vmem, vmem),
+        out_specs=(vmem,) * 4,
         scratch_shapes=[
             pltpu.VMEM((steps, rows, columns), codes.dtype),
             pltpu.SemaphoreType.DMA((steps,)),
         ],
+        compiler_params=room(16),
         name="spread",
     )(place, arrival, bucket, exponents, codes)
 
 
-def join_kernel(half, own_m, own_r, ra, rb, back, *outs):
-    both = 4 * half
+def add_kernel(first, *refs):
+    *ins, out = refs
+    rows = slice(first, first + out.shape[0])
+    total = ins[0][rows] + ins[1][rows]
+    if len(ins) == 3:
+        total = total + ins[2][...]
+    out[...] = total
+
+
+def join_kernel(half, own_a, own_b, mine, got, ra, rb, back_a, back_b, *outs):
     for k in range(4):
         rows = slice(k * half, (k + 1) * half)
-        other = slice(both + k * half, both + (k + 1) * half)
-        outs[k][0:half] = own_m[rows] + own_r[rows] + ra[rows] + back[other]
-        outs[k][half : 2 * half] = own_m[other] + own_r[other] + rb[rows] + back[rows]
+        other = slice((k + 4) * half, (k + 5) * half)
+        at = slice(own_a + k * half, own_a + (k + 1) * half)
+        outs[k][0:half] = mine[at] + got[at] + ra[rows] + back_b[other]
+        at = slice(own_b + k * half, own_b + (k + 1) * half)
+        outs[k][half : 2 * half] = mine[at] + got[at] + rb[rows] + back_a[other]
 
 
 def chain_kernel(tiles, place, bucket, t0, t1, t2, t3, start, exact, compensated, peaks):
@@ -164,39 +186,41 @@
     vmem = pl.BlockSpec(memory_space=pltpu.VMEM)
     smem = pl.BlockSpec(memory_space=pltpu.SMEM)
 
-    mine, send = spread(
+    *mine, send0, send1 = spread(
         place, arrival[None, :], bucket_of_row[None, :], exponents[:, 0, :], grad_codes[:, 0]
     )
     swap = [(0, 1), (1, 0)]
-    got = lax.ppermute(send, "c", swap)
-
-    def part(name):
-        rows = slice(base[name], base[name] + 8 * half)
-        return mine[rows] + got[rows]
-
+    got = [lax.ppermute(send0, "c", swap), lax.ppermute(send1, "c", swap)]
     turn = []
     for z in range(nz):
         turn.append((2 * z, 2 * ((z + 1) % nz)))
         turn.append((2 * z + 1, 2 * ((z - 1) % nz) + 1))
-    ring = functools.partial(lax.ppermute, axis_name=("z", "c"), perm=turn)
-    ra = ring(part("a4"))
-    rb = ring(part("b3"))
-    ra = ring(part("a3") + ra)
-    rb = ring(part("b2") + rb)
-    ra = ring(part("a2") + ra)
-    rb = ring(part("b1") + rb)
-    ra = ring(part("a1") + ra)
-    cut = 4 * half
-    back = lax.ppermute(jnp.concatenate([ra[cut:], rb[cut:]]), "c", swap)
-    own = base["own_a"]
+
+    arrived = {"a": (), "b": ()}
+    for name in NAMES:
+        late, first = base[name]
+        ins = (mine[late], got[late]) + arrived[name[0]]
+        held = pl.pallas_call(
+            functools.partial(add_kernel, first),
+            out_shape=jax.ShapeDtypeStruct((8 * half, LANES), jnp.float32),
+            in_specs=[vmem] * len(ins),
+            out_specs=vmem,
+            compiler_params=room(4),
+            name="add",
+        )(*ins)
+        arrived[name[0]] = (lax.ppermute(held, ("z", "c"), turn),)
+    (ra,), (rb,) = arrived["a"], arrived["b"]
+    back_b = lax.ppermute(rb, "c", swap)
+    back_a = lax.ppermute(ra, "c", swap)
     piece = jax.ShapeDtypeStruct((2 * half, LANES), jnp.float32)
     pieces = pl.pallas_call(
-        functools.partial(join_kernel, half),
+        functools.partial(join_kernel, half, base["own_a"][1], base["own_b"][1]),
         out_shape=(piece,) * 4,
-        in_specs=[vmem] * 5,
+        in_specs=[vmem] * 6,
         out_specs=(vmem,) * 4,
+        compiler_params=room(4),
         name="join",
-    )(mine[own:], got[own:], ra[:cut], rb[:cut], back)
+    )(mine[1], got[1], ra, rb, back_a, back_b)
     totals = [pieces[0]]
     for k in range(1, 4):
         totals.append(lax.ppermute(pieces[k], "x", [(i, (i + k) % 4) for i in range(4)]))
@@ -209,6 +233,7 @@
         ),
         in_specs=[smem, smem] + [vmem] * 5,
         out_specs=(vmem,) * 3,
+        compiler_params=room(4),
         name="chain",
     )(place, bucket_of_row, *totals, accumulated.reshape(tiles, LANES))
     table = jnp.maximum(table, lax.ppermute(table, "c", swap))
@@ -223,6 +248,7 @@
         ),
         in_specs=[smem, smem] + [vmem] * 2,
         out_specs=(vmem,) * 2,
+        compiler_params=room(4),
         name="scale",
     )(place, bucket_of_row, exact, tables.reshape(count, LANES))
     return units[:, None, :], peaks, compensated
@@ -233,6 +259,7 @@
     dp = ("x", "z", "c")
     in_specs = (P(None, dp, None, "y"), P(None, dp, None), P(dp, "y"), P(), P())
     out_specs = (P(None, dp, "y"), P(), P(dp, "y"))
+
     return jax.shard_map(
         on_device, mesh=finer, in_specs=in_specs, out_specs=out_specs, check_vma=False
     )

time: 113 us -> 84.9 us (0.75)
  waiting for transfers between devices: 31.1 us -> 12.2 us
  other arithmetic: 9.1 us -> 0.14 us
  Pallas kernels: 10.8 us -> 5.62 us
  starting transfers between devices: 37 us -> 39.4 us
  blocking collectives: 21.4 us -> 22.9 us
    ppermute x9 -> x11, waiting for transfers between devices: 26.8 us -> 9.13 us  [the longest x2 4.06 us: on_device(): got = [lax.ppermute(send0, 'c', swap), lax.ppermute(send1, 'c', swap)]]
    add x6 -> x0, other arithmetic: 7.15 us -> none  [the longest x1 2.1 us: on_device(): rb = ring(part('b1') + rb)]
    pallas_call x2 -> x9, Pallas kernels: 7.47 us -> 3.12 us  [the longest x1 2.78 us: spread(): pl.pallas_call(functools.partial(spread_kernel, tiles), out_shape=shapes...]
    unnamed x10 -> x12, local copies, waits for them, and re-layouts: 1.36 us -> 3.67 us
    ppermute x9 -> x11, starting transfers between devices: 30.7 us -> 32.7 us  [the longest x7 20.5 us: on_device(): arrived[name[0]] = (lax.ppermute(held, ('z', 'c'), turn),)]
    all_to_all x1, blocking collectives: 21.4 us -> 22.9 us  [on_device(): tables = lax.all_to_all(copies, ('x', 'z', 'y'), 0, 0, tiled=True)]
    slice x2 -> x0, local copies, waits for them, and re-layouts: 1.34 us -> none  [on_device(): back = lax.ppermute(jnp.concatenate([ra[cut:], rb[cut:]]), 'c', swap)]
  transfers between devices with their start and end apart: 13 -> 15, of which waited for: 11 -> 8; matrix products, arithmetic and copies ran while one was open for 2% -> 0% of each run, Pallas kernels for 0% -> 0%
where the time goes in v2:
time: 84.9 us; the launch traced here: 84.7 us
  starting transfers between devices  39.4 us (46%)
  blocking collectives  22.9 us (27%)
  waiting for transfers between devices  12.2 us (14%)
  Pallas kernels  5.62 us (7%)
  local copies, waits for them, and re-layouts  3.71 us (4%)
    all_to_all x1, blocking collectives, on_device(): tables = lax.all_to_all(copies, ('x', 'z', 'y'), 0, 0, tiled=True)  22.9 us
    ppermute x7, starting transfers between devices, on_device(): arrived[name[0]] = (lax.ppermute(held, ('z', 'c'), turn),)  20.5 us
    ppermute x1, starting transfers between devices, on_device(): back_a = lax.ppermute(ra, 'c', swap)  4.92 us
    ppermute x3, starting transfers between devices, on_device(): lax.ppermute(pieces[k], 'x', [(i, (i + k) % 4) for i in range(4)])  4.9 us
    ppermute x2, waiting for transfers between devices, on_device(): got = [lax.ppermute(send0, 'c', swap), lax.ppermute(send1, 'c', swap)]  4.06 us
    ppermute x1, starting transfers between devices, on_device(): back_b = lax.ppermute(rb, 'c', swap)  3.88 us
    ppermute x7, waiting for transfers between devices, on_device(): arrived[name[0]] = (lax.ppermute(held, ('z', 'c'), turn),)  3.86 us
    unnamed x12, local copies, waits for them, and re-layouts  3.67 us
  transfers between devices with their start and end apart: 15, of which 8 were waited for; matrix products, arithmetic and copies ran while one was open for 0% of the time, Pallas kernels for 0%

profile of v2, /device:TPU:1, one launch (start us, length us, event | category | flops | bytes accessed | tf_op | source)
XLA Modules:
  0.0 84.7 jit_solution(14708708727645347775)
XLA Ops:
  0.6 0.1 pad_add_fusion.place
  0.7 1.7 %copy-done = bf16[4,1,64,4608]{3,2,1,0:T(8,128)(2,1)S(1)} copy-done((bf16[4,1,64,4608]{3,2,1,0:T(8,128)(2,1)S(1)}, bf16[4,1,64,4608]{3,2,1,0:T(8,128)(2,1)}, u32[]{:S(2)}) %copy-start) | copy-done | bytes 2359320
  2.4 0.7 copy-done.1
  3.0 0.7 copy-done.3
  3.7 0.7 copy-done.4
  4.4 2.8 %spread.1 = (f32[1152,128]{1,0:T(8,128)S(1)}, f32[3456,128]{1,0:T(8,128)S(1)}, f32[1152,128]{1,0:T(8,128)S(1)}, f32[3456,128]{1,0:T(8,128)S(1)}) custom-call(s32[3]{0:T(128)S(1)} %pad_add_fusion.place, s32[1,64]{1,0:T(1,128)S(1)} %bitcast.17, s32[1,64]{1,0:T(1,128)S(1)} %bitcast.15, s32[4,16]{1,0:T(4,128)S(1)} %bitcast.16, bf16[4,64,4608]{2,1,0:T(8,128)(2,1)S(1)} %bitcast.12), custom_call_target="tpu_custom_call" | custom-call | tf_op jit(solution)/shard_map/spread/pallas_call | solution.py:103
  7.2 3.3 %collective-permute-start = (f32[3456,128]{1,0:T(8,128)S(1)}, f32[3456,128]{1,0:T(8,128)S(1)}, u32[]{:S(2)}, u32[]{:S(2)}) collective-permute-start(f32[3456,128]{1,0:T(8,128)S(1)} %get-tuple-element.17), channel_id=1, source_target_pairs={{0,4},{4,0},{1,5},{5,1},{2,6},{6,2},{3,7},{7,3},{8,12},{12,8},{9,1... | collective-permute-start | bytes 5308424 | tf_op jit(solution)/shard_map/ppermute | solution.py:193
  10.4 0.1 collective-permute-start.1
  10.5 4.1 %collective-permute-done.1.refs_1_ = f32[1152,128]{1,0:T(8,128)S(1)} collective-permute-done((f32[1152,128]{1,0:T(8,128)S(1)}, f32[1152,128]{1,0:T(8,128)S(1)}, u32[]{:S(2)}, u32[]{:S(2)}) %collective-permute-start.1) | collective-permute-done | bytes 589856 | tf_op jit(solution)/shard_map/ppermute | solution.py:193
  14.6 3.9 %collective-permute-start.2 = (f32[576,128]{1,0:T(8,128)S(1)}, f32[576,128]{1,0:T(8,128)S(1)}, u32[]{:S(2)}, u32[]{:S(2)}) collective-permute-start(f32[576,128]{1,0:T(8,128)S(1)} %add.12), channel_id=1, source_target_pairs={{0,8},{4,60},{8,16},{12,4},{16,24},{20,12},{24,32},{28,20},{32,40}... | collective-permute-start | bytes 884744 | tf_op jit(solution)/shard_map/ppermute | solution.py:211
  18.6 0.8 collective-permute-start.6
  19.4 2.8 %collective-permute-done.2.refs_2_ = f32[576,128]{1,0:T(8,128)S(1)} collective-permute-done((f32[576,128]{1,0:T(8,128)S(1)}, f32[576,128]{1,0:T(8,128)S(1)}, u32[]{:S(2)}, u32[]{:S(2)}) %collective-permute-start.2) | collective-permute-done | bytes 294944 | tf_op jit(solution)/shard_map/ppermute | solution.py:211
  22.3 3.2 %collective-permute-start.3 = (f32[576,128]{1,0:T(8,128)S(1)}, f32[576,128]{1,0:T(8,128)S(1)}, u32[]{:S(2)}, u32[]{:S(2)}) collective-permute-start(f32[576,128]{1,0:T(8,128)S(1)} %add.13), channel_id=1, source_target_pairs={{0,8},{4,60},{8,16},{12,4},{16,24},{20,12},{24,32},{28,20},{32,40}... | collective-permute-start | bytes 884744 | tf_op jit(solution)/shard_map/ppermute | solution.py:211
  25.5 3.1 %collective-permute-start.7 = (f32[576,128]{1,0:T(8,128)S(1)}, f32[576,128]{1,0:T(8,128)S(1)}, u32[]{:S(2)}, u32[]{:S(2)}) collective-permute-start(f32[576,128]{1,0:T(8,128)S(1)} %add.17), channel_id=1, source_target_pairs={{0,8},{4,60},{8,16},{12,4},{16,24},{20,12},{24,32},{28,20},{32,40}... | collective-permute-start | bytes 884744 | tf_op jit(solution)/shard_map/ppermute | solution.py:211
  28.6 0.5 collective-permute-done.3.refs_2_
  29.2 3.2 %collective-permute-start.4 = (f32[576,128]{1,0:T(8,128)S(1)}, f32[576,128]{1,0:T(8,128)S(1)}, u32[]{:S(2)}, u32[]{:S(2)}) collective-permute-start(f32[576,128]{1,0:T(8,128)S(1)} %add.14), channel_id=1, source_target_pairs={{0,8},{4,60},{8,16},{12,4},{16,24},{20,12},{24,32},{28,20},{32,40}... | collective-permute-start | bytes 884744 | tf_op jit(solution)/shard_map/ppermute | solution.py:211
  32.4 3.1 %collective-permute-start.8 = (f32[576,128]{1,0:T(8,128)S(1)}, f32[576,128]{1,0:T(8,128)S(1)}, u32[]{:S(2)}, u32[]{:S(2)}) collective-permute-start(f32[576,128]{1,0:T(8,128)S(1)} %add.18), channel_id=1, source_target_pairs={{0,8},{4,60},{8,16},{12,4},{16,24},{20,12},{24,32},{28,20},{32,40}... | collective-permute-start | bytes 884744 | tf_op jit(solution)/shard_map/ppermute | solution.py:211
  35.5 0.5 collective-permute-done.4.refs_2_
  36.1 3.2 %collective-permute-start.5 = (f32[576,128]{1,0:T(8,128)S(1)}, f32[576,128]{1,0:T(8,128)S(1)}, u32[]{:S(2)}, u32[]{:S(2)}) collective-permute-start(f32[576,128]{1,0:T(8,128)S(1)} %add.15), channel_id=1, source_target_pairs={{0,8},{4,60},{8,16},{12,4},{16,24},{20,12},{24,32},{28,20},{32,40}... | collective-permute-start | bytes 884744 | tf_op jit(solution)/shard_map/ppermute | solution.py:211
  39.3 3.9 %collective-permute-start.10 = (f32[576,128]{1,0:T(8,128)S(1)}, f32[576,128]{1,0:T(8,128)S(1)}, u32[]{:S(2)}, u32[]{:S(2)}) collective-permute-start(f32[576,128]{1,0:T(8,128)S(1)} %collective-permute-done.8.rb), channel_id=1, source_target_pairs={{0,4},{4,0},{1,5},{5,1},{2,6},{6,2},{3,7},{7,3},{8,12},{12,8},{9,1... | collective-permute-start | bytes 884744 | tf_op jit(solution)/shard_map/ppermute | solution.py:213
  43.2 4.9 %collective-permute-start.9 = (f32[576,128]{1,0:T(8,128)S(1)}, f32[576,128]{1,0:T(8,128)S(1)}, u32[]{:S(2)}, u32[]{:S(2)}) collective-permute-start(f32[576,128]{1,0:T(8,128)S(1)} %collective-permute-done.5.ra), channel_id=1, source_target_pairs={{0,4},{4,0},{1,5},{5,1},{2,6},{6,2},{3,7},{7,3},{8,12},{12,8},{9,1... | collective-permute-start | bytes 884744 | tf_op jit(solution)/shard_map/ppermute | solution.py:214
  48.1 1.2 %collective-permute-done.9.back_a = f32[576,128]{1,0:T(8,128)S(1)} collective-permute-done((f32[576,128]{1,0:T(8,128)S(1)}, f32[576,128]{1,0:T(8,128)S(1)}, u32[]{:S(2)}, u32[]{:S(2)}) %collective-permute-start.9) | collective-permute-done | bytes 294944 | tf_op jit(solution)/shard_map/ppermute | solution.py:214
  49.4 1.3 %collective-permute-start.11 = (f32[144,128]{1,0:T(8,128)S(1)}, f32[144,128]{1,0:T(8,128)S(1)}, u32[]{:S(2)}, u32[]{:S(2)}) collective-permute-start(f32[144,128]{1,0:T(8,128)S(1)} %get-tuple-element.21), channel_id=1, source_target_pairs={{0,64},{64,128},{128,192},{192,0},{1,65},{65,129},{129,193},{193,1... | collective-permute-start | bytes 221192 | tf_op jit(solution)/shard_map/ppermute | solution.py:226
  50.7 2.4 %collective-permute-start.12 = (f32[144,128]{1,0:T(8,128)S(1)}, f32[144,128]{1,0:T(8,128)S(1)}, u32[]{:S(2)}, u32[]{:S(2)}) collective-permute-start(f32[144,128]{1,0:T(8,128)S(1)} %get-tuple-element.22), channel_id=1, source_target_pairs={{0,128},{64,192},{128,0},{192,64},{1,129},{65,193},{129,1},{193,65... | collective-permute-start | bytes 221192 | tf_op jit(solution)/shard_map/ppermute | solution.py:226
  53.1 1.2 %collective-permute-start.13 = (f32[144,128]{1,0:T(8,128)S(1)}, f32[144,128]{1,0:T(8,128)S(1)}, u32[]{:S(2)}, u32[]{:S(2)}) collective-permute-start(f32[144,128]{1,0:T(8,128)S(1)} %get-tuple-element.23), channel_id=1, source_target_pairs={{0,192},{64,0},{128,64},{192,128},{1,193},{65,1},{129,65},{193,129... | collective-permute-start | bytes 221192 | tf_op jit(solution)/shard_map/ppermute | solution.py:226
  54.4 2.0 %collective-permute-done.12.t2 = f32[144,128]{1,0:T(8,128)S(1)} collective-permute-done((f32[144,128]{1,0:T(8,128)S(1)}, f32[144,128]{1,0:T(8,128)S(1)}, u32[]{:S(2)}, u32[]{:S(2)}) %collective-permute-start.12) | collective-permute-done | bytes 73760 | tf_op jit(solution)/shard_map/ppermute | solution.py:226
  56.4 0.3 collective-permute-done.13.t3
  56.7 1.2 %chain.1 = (f32[4,4608]{1,0:T(4,128)S(1)}, f32[1,4608]{1,0:T(1,128)}, f32[1,128]{1,0:T(1,128)S(1)}) custom-call(s32[3]{0:T(128)S(1)} %pad_add_fusion.place, s32[64]{0:T(128)S(1)} %copy-done.2, f32[144,128]{1,0:T(8,128)S(1)} %get-tuple-element.20.t0, f32[144,128]{1,0:T(8,128)S(1)} %collective-permute-done.11.t1, f32[144,128]{1,0:T(8,128)S(1)} %collective-permute-done.12.t2, ...), custom_call_target="tpu_custom_call" | custom-call | tf_op jit(solution)/shard_map/chain/pallas_call | solution.py:227
  57.9 1.8 %collective-permute-start.14 = (f32[1,128]{1,0:T(1,128)S(1)}, f32[1,128]{1,0:T(1,128)S(1)}, u32[]{:S(2)}, u32[]{:S(2)}) collective-permute-start(f32[1,128]{1,0:T(1,128)S(1)} %get-tuple-element.25), channel_id=1, source_target_pairs={{0,4},{4,0},{1,5},{5,1},{2,6},{6,2},{3,7},{7,3},{8,12},{12,8},{9,1... | collective-permute-start | bytes 1544 | tf_op jit(solution)/shard_map/ppermute | solution.py:239
  59.7 0.8 collective-permute-done.14
  60.5 22.9 %all_to_all.5 = f32[128,1,128]{2,1,0:T(1,128)S(1)} all-to-all(f32[128,1,128]{2,1,0:T(1,128)S(1)} %broadcast_in_dim.20), channel_id=1, replica_groups=mesh['x'=4,'z'=8,'c'=2,'y'=4] {'x','z','y'}, dimensions={0} | all-to-all | bytes 131072 | tf_op jit(solution)/shard_map/all_to_all | solution.py:242
  83.4 1.3 %scale.1 = (bf16[4,4608]{1,0:T(4,128)(2,1)}, f32[4,16]{1,0:T(4,128)}) custom-call(s32[3]{0:T(128)S(1)} %pad_add_fusion.place, s32[64]{0:T(128)S(1)} %copy-done.2, f32[4,4608]{1,0:T(4,128)S(1)} %get-tuple-element.24.exact, f32[128,128]{1,0:T(8,128)S(1)} %bitcast.13), custom_call_target="tpu_custom_call" | custom-call | tf_op jit(solution)/shard_map/scale/pallas_call | solution.py:243
  (26 shorter events, 0.5 us)
Async XLA Ops:
  0.7 1.7 %copy-start = (bf16[4,1,64,4608]{3,2,1,0:T(8,128)(2,1)S(1)}, bf16[4,1,64,4608]{3,2,1,0:T(8,128)(2,1)}, u32[]{:S(2)}) copy-start(bf16[4,1,64,4608]{3,2,1,0:T(8,128)(2,1)} %param.5) | copy-start | bytes 7077892
  2.4 0.7 copy-start.1
  3.0 0.7 copy-start.3
  3.7 0.7 copy-start.4
  7.2 15.1 %collective-permute-start = (f32[3456,128]{1,0:T(8,128)S(1)}, f32[3456,128]{1,0:T(8,128)S(1)}, u32[]{:S(2)}, u32[]{:S(2)}) collective-permute-start(f32[3456,128]{1,0:T(8,128)S(1)} %get-tuple-element.17), channel_id=1, source_target_pairs={{0,4},{4,0},{1,5},{5,1},{2,6},{6,2},{3,7},{7,3},{8,12},{12,8},{9,1... | collective-permute-start | bytes 5308424 | tf_op jit(solution)/shard_map/ppermute | solution.py:193
  10.4 4.2 %collective-permute-start.1 = (f32[1152,128]{1,0:T(8,128)S(1)}, f32[1152,128]{1,0:T(8,128)S(1)}, u32[]{:S(2)}, u32[]{:S(2)}) collective-permute-start(f32[1152,128]{1,0:T(8,128)S(1)} %get-tuple-element.19), channel_id=1, source_target_pairs={{0,4},{4,0},{1,5},{5,1},{2,6},{6,2},{3,7},{7,3},{8,12},{12,8},{9,1... | collective-permute-start | bytes 1769480 | tf_op jit(solution)/shard_map/ppermute | solution.py:193
  14.6 7.6 %collective-permute-start.2 = (f32[576,128]{1,0:T(8,128)S(1)}, f32[576,128]{1,0:T(8,128)S(1)}, u32[]{:S(2)}, u32[]{:S(2)}) collective-permute-start(f32[576,128]{1,0:T(8,128)S(1)} %add.12), channel_id=1, source_target_pairs={{0,8},{4,60},{8,16},{12,4},{16,24},{20,12},{24,32},{28,20},{32,40}... | collective-permute-start | bytes 884744 | tf_op jit(solution)/shard_map/ppermute | solution.py:211
  18.6 6.9 %collective-permute-start.6 = (f32[576,128]{1,0:T(8,128)S(1)}, f32[576,128]{1,0:T(8,128)S(1)}, u32[]{:S(2)}, u32[]{:S(2)}) collective-permute-start(f32[576,128]{1,0:T(8,128)S(1)} %add.16), channel_id=1, source_target_pairs={{0,8},{4,60},{8,16},{12,4},{16,24},{20,12},{24,32},{28,20},{32,40}... | collective-permute-start | bytes 884744 | tf_op jit(solution)/shard_map/ppermute | solution.py:211
  22.3 6.9 %collective-permute-start.3 = (f32[576,128]{1,0:T(8,128)S(1)}, f32[576,128]{1,0:T(8,128)S(1)}, u32[]{:S(2)}, u32[]{:S(2)}) collective-permute-start(f32[576,128]{1,0:T(8,128)S(1)} %add.13), channel_id=1, source_target_pairs={{0,8},{4,60},{8,16},{12,4},{16,24},{20,12},{24,32},{28,20},{32,40}... | collective-permute-start | bytes 884744 | tf_op jit(solution)/shard_map/ppermute | solution.py:211
  25.5 6.9 %collective-permute-start.7 = (f32[576,128]{1,0:T(8,128)S(1)}, f32[576,128]{1,0:T(8,128)S(1)}, u32[]{:S(2)}, u32[]{:S(2)}) collective-permute-start(f32[576,128]{1,0:T(8,128)S(1)} %add.17), channel_id=1, source_target_pairs={{0,8},{4,60},{8,16},{12,4},{16,24},{20,12},{24,32},{28,20},{32,40}... | collective-permute-start | bytes 884744 | tf_op jit(solution)/shard_map/ppermute | solution.py:211
  29.2 6.9 %collective-permute-start.4 = (f32[576,128]{1,0:T(8,128)S(1)}, f32[576,128]{1,0:T(8,128)S(1)}, u32[]{:S(2)}, u32[]{:S(2)}) collective-permute-start(f32[576,128]{1,0:T(8,128)S(1)} %add.14), channel_id=1, source_target_pairs={{0,8},{4,60},{8,16},{12,4},{16,24},{20,12},{24,32},{28,20},{32,40}... | collective-permute-start | bytes 884744 | tf_op jit(solution)/shard_map/ppermute | solution.py:211
  32.4 6.9 %collective-permute-start.8 = (f32[576,128]{1,0:T(8,128)S(1)}, f32[576,128]{1,0:T(8,128)S(1)}, u32[]{:S(2)}, u32[]{:S(2)}) collective-permute-start(f32[576,128]{1,0:T(8,128)S(1)} %add.18), channel_id=1, source_target_pairs={{0,8},{4,60},{8,16},{12,4},{16,24},{20,12},{24,32},{28,20},{32,40}... | collective-permute-start | bytes 884744 | tf_op jit(solution)/shard_map/ppermute | solution.py:211
  36.1 18.2 %copy-start.5 = (bf16[1,4608]{1,0:T(2,128)(2,1)S(1)}, bf16[1,4608]{1,0:T(2,128)(2,1)}, u32[]{:S(2)}) copy-start(bf16[1,4608]{1,0:T(2,128)(2,1)} %param.7) | copy-start | bytes 27652
  36.1 20.6 %copy-start.2 = (s32[64]{0:T(128)S(1)}, s32[64]{0:T(128)}, u32[]{:S(2)}) copy-start(s32[64]{0:T(128)} %bucket.3) | copy-start | bytes 772
  36.1 7.1 %collective-permute-start.5 = (f32[576,128]{1,0:T(8,128)S(1)}, f32[576,128]{1,0:T(8,128)S(1)}, u32[]{:S(2)}, u32[]{:S(2)}) collective-permute-start(f32[576,128]{1,0:T(8,128)S(1)} %add.15), channel_id=1, source_target_pairs={{0,8},{4,60},{8,16},{12,4},{16,24},{20,12},{24,32},{28,20},{32,40}... | collective-permute-start | bytes 884744 | tf_op jit(solution)/shard_map/ppermute | solution.py:211
  39.3 8.8 %collective-permute-start.10 = (f32[576,128]{1,0:T(8,128)S(1)}, f32[576,128]{1,0:T(8,128)S(1)}, u32[]{:S(2)}, u32[]{:S(2)}) collective-permute-start(f32[576,128]{1,0:T(8,128)S(1)} %collective-permute-done.8.rb), channel_id=1, source_target_pairs={{0,4},{4,0},{1,5},{5,1},{2,6},{6,2},{3,7},{7,3},{8,12},{12,8},{9,1... | collective-permute-start | bytes 884744 | tf_op jit(solution)/shard_map/ppermute | solution.py:213
  43.2 6.1 %collective-permute-start.9 = (f32[576,128]{1,0:T(8,128)S(1)}, f32[576,128]{1,0:T(8,128)S(1)}, u32[]{:S(2)}, u32[]{:S(2)}) collective-permute-start(f32[576,128]{1,0:T(8,128)S(1)} %collective-permute-done.5.ra), channel_id=1, source_target_pairs={{0,4},{4,0},{1,5},{5,1},{2,6},{6,2},{3,7},{7,3},{8,12},{12,8},{9,1... | collective-permute-start | bytes 884744 | tf_op jit(solution)/shard_map/ppermute | solution.py:214
  49.4 5.0 %collective-permute-start.11 = (f32[144,128]{1,0:T(8,128)S(1)}, f32[144,128]{1,0:T(8,128)S(1)}, u32[]{:S(2)}, u32[]{:S(2)}) collective-permute-start(f32[144,128]{1,0:T(8,128)S(1)} %get-tuple-element.21), channel_id=1, source_target_pairs={{0,64},{64,128},{128,192},{192,0},{1,65},{65,129},{129,193},{193,1... | collective-permute-start | bytes 221192 | tf_op jit(solution)/shard_map/ppermute | solution.py:226
  50.7 5.7 %collective-permute-start.12 = (f32[144,128]{1,0:T(8,128)S(1)}, f32[144,128]{1,0:T(8,128)S(1)}, u32[]{:S(2)}, u32[]{:S(2)}) collective-permute-start(f32[144,128]{1,0:T(8,128)S(1)} %get-tuple-element.22), channel_id=1, source_target_pairs={{0,128},{64,192},{128,0},{192,64},{1,129},{65,193},{129,1},{193,65... | collective-permute-start | bytes 221192 | tf_op jit(solution)/shard_map/ppermute | solution.py:226
  53.1 3.5 %collective-permute-start.13 = (f32[144,128]{1,0:T(8,128)S(1)}, f32[144,128]{1,0:T(8,128)S(1)}, u32[]{:S(2)}, u32[]{:S(2)}) collective-permute-start(f32[144,128]{1,0:T(8,128)S(1)} %get-tuple-element.23), channel_id=1, source_target_pairs={{0,192},{64,0},{128,64},{192,128},{1,193},{65,1},{129,65},{193,129... | collective-permute-start | bytes 221192 | tf_op jit(solution)/shard_map/ppermute | solution.py:226
  57.9 2.6 %collective-permute-start.14 = (f32[1,128]{1,0:T(1,128)S(1)}, f32[1,128]{1,0:T(1,128)S(1)}, u32[]{:S(2)}, u32[]{:S(2)}) collective-permute-start(f32[1,128]{1,0:T(1,128)S(1)} %get-tuple-element.25), channel_id=1, source_target_pairs={{0,4},{4,0},{1,5},{5,1},{2,6},{6,2},{3,7},{7,3},{8,12},{12,8},{9,1... | collective-permute-start | bytes 1544 | tf_op jit(solution)/shard_map/ppermute | solution.py:239

commit v3 on v2

v3 whole, which is shorter than its diff:
```python
import functools

import jax
import jax.numpy as jnp
from jax import lax
from jax.experimental import pallas as pl
from jax.experimental.pallas import tpu as pltpu
from jax.sharding import Mesh
from jax.sharding import PartitionSpec as P


NB = 16
STEPS = 4
ROWS = 64
LANES = 128
EPSILON = 1e-06

PIECES = tuple(
    (hops - (rel >= 2), rel) for hops in (4, 3, 2, 1) for rel in range(STEPS) if hops - (rel >= 2) > 0
)
EARLY = PIECES[:STEPS]


def room(mib):
    return pltpu.CompilerParams(vmem_limit_bytes=mib * 2**20)


def where_rows(tiles):
    base, sizes = {}, [0, 0]
    for piece in PIECES + tuple((0, rel) for rel in range(STEPS)):
        late = int(piece not in EARLY)
        base[piece] = (late, sizes[late])
        sizes[late] += (8 if piece[0] else 4) * tiles
    return base, sizes


def group_order(rel):
    first = [4, 5] if rel < 2 else [3, 4]
    return first + [k for k in range(8) if k not in first]


def picks_kernel(place, table, picks):
    x, z, c = place[0], place[1], place[2]
    shape = (ROWS, ROWS)
    group = lax.broadcasted_iota(jnp.int32, shape, 0) // 8
    g = lax.broadcasted_iota(jnp.int32, shape, 0) % 8
    lane = lax.broadcasted_iota(jnp.int32, shape, 1)
    arrival, bucket = table[0:1, 0:ROWS], table[0:1, ROWS : 2 * ROWS]
    exponents = table[1:2, 0:ROWS]
    to_x = x ^ (g % 4)
    for rel in range(STEPS):
        k = jnp.zeros(shape, jnp.int32)
        for index, value in enumerate(group_order(rel)):
            k = jnp.where(group == index, value, k)
        to_z = (z + k * (1 - 2 * c)) & 7
        owner = jnp.where(k <= (4 if rel < 2 else 3), c, 1 - c)
        ids = (to_x * 8 + to_z) * 2 + (owner ^ (g // 4))
        row_bucket = jnp.sum(jnp.where(ids == lane, bucket, 0), axis=1, keepdims=True)
        step = rel ^ (2 * (1 - c))
        power = jnp.sum(
            jnp.where(row_bucket + step * NB == lane, exponents, 0), axis=1, keepdims=True
        )
        factor = jnp.ones((ROWS, 1), jnp.float32)
        for bit in range(6):
            factor = factor * jnp.where((power >> bit) & 1 == 1, 2.0 ** -(2**bit), 1.0)
        picks[rel] = jnp.where(ids == arrival, factor, 0.0).astype(jnp.bfloat16)


def spread_kernel(tiles, late, place, picks, codes, mine, send):
    base, _ = where_rows(tiles)
    c = place[2]
    width = 2 * LANES
    rows = slice(16, ROWS) if late else slice(0, 16)

    def put(out, piece, at, value):
        assert base[piece][0] == late
        out[pl.ds(base[piece][1] + at, value.shape[0], tiles), :] = value

    for rel in range(STEPS):
        order = group_order(rel)[2:] if late else group_order(rel)[:2]
        pick = picks[rel, rows, :]
        step = rel ^ (2 * (1 - c))
        for block in range(tiles * LANES // width):
            part = jnp.dot(
                pick,
                codes[step, :, block * width : (block + 1) * width],
                preferred_element_type=jnp.float32,
            )
            for sub in range(2):
                at = 2 * block + sub
                for index, k in enumerate(order):
                    piece = part[index * 8 : index * 8 + 8, sub * LANES : (sub + 1) * LANES]
                    if k == 0:
                        put(mine, (0, rel), at, piece[0:4])
                        put(send, (0, rel ^ 2), at, piece[4:8])
                    elif (k, rel) in base:
                        put(mine, (k, rel), at, piece)
                    else:
                        put(send, (8 - k, rel ^ 2), at, piece)


def spread(late, place, picks, codes):
    tiles = codes.shape[2] // LANES
    shape = jax.ShapeDtypeStruct((where_rows(tiles)[1][late], LANES), jnp.float32)
    vmem = pl.BlockSpec(memory_space=pltpu.VMEM)
    return pl.pallas_call(
        functools.partial(spread_kernel, tiles, late),
        out_shape=(shape, shape),
        in_specs=[pl.BlockSpec(memory_space=pltpu.SMEM), vmem, vmem],
        out_specs=(vmem, vmem),
        compiler_params=room(8),
        name="spread",
    )(place, picks, codes)


def add_kernel(first, *refs):
    *ins, out = refs
    rows = slice(first, first + out.shape[0])
    total = ins[0][rows] + ins[1][rows]
    if len(ins) == 3:
        total = total + ins[2][...]
    out[...] = total


def join_kernel(tiles, own, mine, got, r0, r1, r2, r3, b0, b1, b2, b3, *outs):
    ring, back = (r0, r1, r2, r3), (b0, b1, b2, b3)
    for k in range(4):
        rows = slice(k * tiles, (k + 1) * tiles)
        other = slice((k + 4) * tiles, (k + 5) * tiles)
        for rel in range(STEPS):
            at = slice(own[rel] + k * tiles, own[rel] + (k + 1) * tiles)
            outs[k][rel * tiles : (rel + 1) * tiles] = (
                mine[at] + got[at] + ring[rel][rows] + back[rel ^ 2][other]
            )


def chain_kernel(tiles, place, bucket, t0, t1, t2, t3, start, exact, peaks):
    c = place[2]
    mine = bucket[(place[0] * 8 + place[1]) * 2 + c]
    total = t0[...] + t1[...] + t2[...] + t3[...]
    running = start[...].astype(jnp.float32)
    carried = jnp.zeros_like(running)
    lane = lax.broadcasted_iota(jnp.int32, (1, LANES), 1)
    table = jnp.zeros((1, LANES), jnp.float32)
    for step in range(STEPS):
        first, second = (step ^ 2) * tiles, step * tiles
        reduced = jnp.where(c == 0, total[first : first + tiles], total[second : second + tiles])
        adjusted = reduced - carried
        new = (running + adjusted).astype(jnp.bfloat16).astype(jnp.float32)
        carried = (new - running) - adjusted
        running = new
        value = running - carried
        peak = jnp.max(jnp.max(jnp.abs(value), axis=0, keepdims=True), axis=1, keepdims=True)
        table = jnp.where(lane == step * NB + mine, peak, table)
        for t in range(tiles):
            exact[step : step + 1, t * LANES : (t + 1) * LANES] = value[t : t + 1]
    peaks[...] = table


def scale_kernel(place, bucket, exact, tables, units, peaks, compensated):
    mine = bucket[(place[0] * 8 + place[1]) * 2 + place[2]]
    table = jnp.max(tables[...], axis=0, keepdims=True)
    lane = lax.broadcasted_iota(jnp.int32, (STEPS, LANES), 1)
    step = lax.broadcasted_iota(jnp.int32, (STEPS, LANES), 0)
    spot = lane == step * NB + mine
    peak = jnp.max(jnp.where(spot, jnp.broadcast_to(table, spot.shape), 0.0), axis=1, keepdims=True)
    compensated[...] = exact[STEPS - 1 : STEPS, :]
    units[...] = (exact[...] / (peak + EPSILON)).astype(units.dtype)
    for s in range(STEPS):
        peaks[s : s + 1, :] = table[:, s * NB : (s + 1) * NB]


def on_device(grad_codes, exponents, accumulated, arrival, bucket_of_row):
    columns = accumulated.shape[1]
    tiles = columns // LANES
    base, _ = where_rows(tiles)
    place = jnp.stack([lax.axis_index("x"), lax.axis_index("z"), lax.axis_index("c")])
    nz = lax.axis_size("z")
    vmem = pl.BlockSpec(memory_space=pltpu.VMEM)
    smem = pl.BlockSpec(memory_space=pltpu.SMEM)
    codes = grad_codes[:, 0]

    words = jnp.concatenate([arrival, bucket_of_row, exponents.reshape(-1), jnp.zeros_like(arrival)])
    picks = pl.pallas_call(
        picks_kernel,
        out_shape=jax.ShapeDtypeStruct((STEPS, ROWS, ROWS), jnp.bfloat16),
        in_specs=[smem, vmem],
        out_specs=vmem,
        compiler_params=room(4),
        name="picks",
    )(place, words.reshape(2, LANES))

    swap = [(0, 1), (1, 0)]
    mine0, send0 = spread(0, place, picks, codes)
    got0 = lax.ppermute(send0, "c", swap)
    mine1, send1 = spread(1, place, picks, codes)
    got1 = lax.ppermute(send1, "c", swap)
    mine, got = (mine0, mine1), (got0, got1)
    turn = []
    for z in range(nz):
        turn.append((2 * z, 2 * ((z + 1) % nz)))
        turn.append((2 * z + 1, 2 * ((z - 1) % nz) + 1))

    ring = [()] * STEPS
    for hops, rel in PIECES:
        late, first = base[hops, rel]
        ins = (mine[late], got[late]) + ring[rel]
        held = pl.pallas_call(
            functools.partial(add_kernel, first),
            out_shape=jax.ShapeDtypeStruct((8 * tiles, LANES), jnp.float32),
            in_specs=[vmem] * len(ins),
            out_specs=vmem,
            compiler_params=room(4),
            name="add",
        )(*ins)
        ring[rel] = (lax.ppermute(held, ("z", "c"), turn),)
    ring = [arrived for (arrived,) in ring]
    back = [lax.ppermute(arrived, "c", swap) for arrived in ring]
    piece = jax.ShapeDtypeStruct((STEPS * tiles, LANES), jnp.float32)
    own = tuple(base[0, rel][1] for rel in range(STEPS))
    pieces = pl.pallas_call(
        functools.partial(join_kernel, tiles, own),
        out_shape=(piece,) * 4,
        in_specs=[vmem] * 10,
        out_specs=(vmem,) * 4,
        compiler_params=room(4),
        name="join",
    )(mine1, got1, *ring, *back)
    totals = [pieces[0]]
    for k in range(1, 4):
        totals.append(lax.ppermute(pieces[k], "x", [(i, i ^ k) for i in range(4)]))
    exact, table = pl.pallas_call(
        functools.partial(chain_kernel, tiles),
        out_shape=(
            jax.ShapeDtypeStruct((STEPS, columns), jnp.float32),
            jax.ShapeDtypeStruct((1, LANES), jnp.float32),
        ),
        in_specs=[smem, smem] + [vmem] * 5,
        out_specs=(vmem,) * 2,
        compiler_params=room(4),
        name="chain",
    )(place, bucket_of_row, *totals, accumulated.reshape(tiles, LANES))
    table = jnp.maximum(table, lax.ppermute(table, "c", swap))
    count = lax.axis_size(("x", "z", "y"))
    copies = jnp.broadcast_to(table[None], (count, 1, LANES))
    tables = lax.all_to_all(copies, ("x", "z", "y"), 0, 0, tiled=True)
    units, peaks, compensated = pl.pallas_call(
        scale_kernel,
        out_shape=(
            jax.ShapeDtypeStruct((STEPS, columns), jnp.bfloat16),
            jax.ShapeDtypeStruct((STEPS, NB), jnp.float32),
            jax.ShapeDtypeStruct((1, columns), jnp.float32),
        ),
        in_specs=[smem, smem] + [vmem] * 2,
        out_specs=(vmem,) * 3,
        compiler_params=room(4),
        name="scale",
    )(place, bucket_of_row, exact, tables.reshape(count, LANES))
    return units[:, None, :], peaks, compensated


def solution(mesh):
    finer = Mesh(mesh.devices.reshape(4, 8, 2, mesh.shape["tensor"]), ("x", "z", "c", "y"))
    dp = ("x", "z", "c")
    in_specs = (P(None, dp, None, "y"), P(None, dp, None), P(dp, "y"), P(), P())
    out_specs = (P(None, dp, "y"), P(), P(dp, "y"))

    return jax.shard_map(
        on_device, mesh=finer, in_specs=in_specs, out_specs=out_specs, check_vma=False
    )
```

time: 84.9 us -> 79 us (0.931)
  waiting for transfers between devices: 12.2 us -> 9.68 us
  other arithmetic: 0.14 us -> 2.16 us
  blocking collectives: 22.9 us -> 20.9 us
  starting transfers between devices: 39.4 us -> 37.6 us
  local copies, waits for them, and re-layouts: 3.71 us -> 2.31 us
    ppermute x14 -> x23, waiting for transfers between devices: 11.4 us -> 8.87 us  [the longest x3 4.63 us: on_device(): totals.append(lax.ppermute(pieces[k], 'x', [(i, i ^ k) for i in range(4)]))]
    all_to_all x1, blocking collectives: 22.9 us -> 20.9 us  [on_device(): tables = lax.all_to_all(copies, ('x', 'z', 'y'), 0, 0, tiled=True)]
    ppermute x14 -> x23, starting transfers between devices: 37.6 us -> 35.9 us  [the longest x14 23.1 us: on_device(): ring[rel] = (lax.ppermute(held, ('z', 'c'), turn),)]
    unnamed x12 -> x7, local copies, waits for them, and re-layouts: 3.67 us -> 2.19 us
    unnamed x1 -> x2, other arithmetic: 0.06 us -> 1.33 us
    pallas_call x2 -> x4, Pallas kernels: 2.83 us -> 3.13 us  [the longest x2 2.11 us: spread(): pl.pallas_call(functools.partial(spread_kernel, tiles, late), out_shape=(...]
  transfers between devices with their start and end apart: 15 -> 24, of which waited for: 8 -> 6; matrix products, arithmetic and copies ran while one was open for 0% -> 0% of each run, Pallas kernels for 0% -> 2%
where the time goes in v3:
time: 79 us; the launch traced here: 78.8 us
  starting transfers between devices  37.6 us (48%)
  blocking collectives  20.9 us (26%)
  waiting for transfers between devices  9.68 us (12%)
  Pallas kernels  5.4 us (7%)
  local copies, waits for them, and re-layouts  2.31 us (3%)
  other arithmetic  2.16 us (3%)
    ppermute x14, starting transfers between devices, on_device(): ring[rel] = (lax.ppermute(held, ('z', 'c'), turn),)  23.1 us
    all_to_all x1, blocking collectives, on_device(): tables = lax.all_to_all(copies, ('x', 'z', 'y'), 0, 0, tiled=True)  20.9 us
    ppermute x4, starting transfers between devices, on_device(): back = [lax.ppermute(arrived, 'c', swap) for arrived in ring]  5.52 us
    ppermute x3, waiting for transfers between devices, on_device(): totals.append(lax.ppermute(pieces[k], 'x', [(i, i ^ k) for i in range(4)]))  4.63 us
    ppermute x3, starting transfers between devices, on_device(): totals.append(lax.ppermute(pieces[k], 'x', [(i, i ^ k) for i in range(4)]))  3.94 us
    ppermute x1, starting transfers between devices, on_device(): got1 = lax.ppermute(send1, 'c', swap)  3.29 us
    ppermute x1, waiting for transfers between devices, on_device(): got0 = lax.ppermute(send0, 'c', swap)  3.1 us
    unnamed x7, local copies, waits for them, and re-layouts  2.19 us
  transfers between devices with their start and end apart: 24, of which 6 were waited for; matrix products, arithmetic and copies ran while one was open for 0% of the time, Pallas kernels for 2%

profile of v3, /device:TPU:1, one launch (start us, length us, event | category | flops | bytes accessed | tf_op | source)
XLA Modules:
  0.0 78.8 jit_solution(18190381709402966300)
XLA Ops:
  1.2 1.3 %reduce.4 = s32[4,16]{1,0:T(4,128)S(1)} reduce(s32[4,1,16]{2,1,0:T(1,128)} %param.6, s32[]{:T(128)} %broadcast.5), dimensions={1}, to_apply=%param.6.reduce_sub_computation.3 | reduce | bytes 516 | tf_op args[1]
  3.3 0.9 %picks.1 = bf16[4,64,64]{2,1,0:T(8,128)(2,1)S(1)} custom-call(s32[3]{0:T(128)S(1)} %pad_add_fusion.place, s32[2,128]{1,0:T(2,128)S(1)} %add_bitcast_fusion.table), custom_call_target="tpu_custom_call" | custom-call | tf_op jit(solution)/shard_map/picks/pallas_call | solution.py:184
  4.3 1.7 %copy-done = bf16[4,1,64,4608]{3,2,1,0:T(8,128)(2,1)S(1)} copy-done((bf16[4,1,64,4608]{3,2,1,0:T(8,128)(2,1)S(1)}, bf16[4,1,64,4608]{3,2,1,0:T(8,128)(2,1)}, u32[]{:S(2)}) %copy-start) | copy-done | bytes 2359320
  5.9 1.1 %spread.2 = (f32[3456,128]{1,0:T(8,128)S(1)}, f32[3456,128]{1,0:T(8,128)S(1)}) custom-call(s32[3]{0:T(128)S(1)} %pad_add_fusion.place, bf16[4,64,64]{2,1,0:T(8,128)(2,1)S(1)} %picks.1, bf16[4,64,4608]{2,1,0:T(8,128)(2,1)S(1)} %bitcast.11), custom_call_target="tpu_custom_call" | custom-call | tf_op jit(solution)/shard_map/spread/pallas_call | solution.py:106
  7.1 3.3 %collective-permute-start = (f32[3456,128]{1,0:T(8,128)S(1)}, f32[3456,128]{1,0:T(8,128)S(1)}, u32[]{:S(2)}, u32[]{:S(2)}) collective-permute-start(f32[3456,128]{1,0:T(8,128)S(1)} %get-tuple-element.17), channel_id=1, source_target_pairs={{0,4},{4,0},{1,5},{5,1},{2,6},{6,2},{3,7},{7,3},{8,12},{12,8},{9,1... | collective-permute-start | bytes 5308424 | tf_op jit(solution)/shard_map/ppermute | solution.py:197
  10.4 1.0 %spread.3 = (f32[1152,128]{1,0:T(8,128)S(1)}, f32[1152,128]{1,0:T(8,128)S(1)}) custom-call(s32[3]{0:T(128)S(1)} %pad_add_fusion.place, bf16[4,64,64]{2,1,0:T(8,128)(2,1)S(1)} %picks.1, bf16[4,64,4608]{2,1,0:T(8,128)(2,1)S(1)} %bitcast.12), custom_call_target="tpu_custom_call" | custom-call | tf_op jit(solution)/shard_map/spread/pallas_call | solution.py:106
  11.4 3.1 %collective-permute-done.1.refs_1_ = f32[1152,128]{1,0:T(8,128)S(1)} collective-permute-done((f32[1152,128]{1,0:T(8,128)S(1)}, f32[1152,128]{1,0:T(8,128)S(1)}, u32[]{:S(2)}, u32[]{:S(2)}) %collective-permute-start.1) | collective-permute-done | bytes 589856 | tf_op jit(solution)/shard_map/ppermute | solution.py:195
  14.6 3.9 %collective-permute-start.2 = (f32[288,128]{1,0:T(8,128)S(1)}, f32[288,128]{1,0:T(8,128)S(1)}, u32[]{:S(2)}, u32[]{:S(2)}) collective-permute-start(f32[288,128]{1,0:T(8,128)S(1)} %add.29), channel_id=1, source_target_pairs={{0,8},{4,60},{8,16},{12,4},{16,24},{20,12},{24,32},{28,20},{32,40}... | collective-permute-start | bytes 442376 | tf_op jit(solution)/shard_map/ppermute | solution.py:216
  19.4 0.8 %collective-permute-start.10 = (f32[288,128]{1,0:T(8,128)S(1)}, f32[288,128]{1,0:T(8,128)S(1)}, u32[]{:S(2)}, u32[]{:S(2)}) collective-permute-start(f32[288,128]{1,0:T(8,128)S(1)} %add.37), channel_id=1, source_target_pairs={{0,8},{4,60},{8,16},{12,4},{16,24},{20,12},{24,32},{28,20},{32,40}... | collective-permute-start | bytes 442376 | tf_op jit(solution)/shard_map/ppermute | solution.py:216
  20.2 0.8 %collective-permute-start.13 = (f32[288,128]{1,0:T(8,128)S(1)}, f32[288,128]{1,0:T(8,128)S(1)}, u32[]{:S(2)}, u32[]{:S(2)}) collective-permute-start(f32[288,128]{1,0:T(8,128)S(1)} %add.40), channel_id=1, source_target_pairs={{0,8},{4,60},{8,16},{12,4},{16,24},{20,12},{24,32},{28,20},{32,40}... | collective-permute-start | bytes 442376 | tf_op jit(solution)/shard_map/ppermute | solution.py:216
  21.0 2.8 %collective-permute-start.3 = (f32[288,128]{1,0:T(8,128)S(1)}, f32[288,128]{1,0:T(8,128)S(1)}, u32[]{:S(2)}, u32[]{:S(2)}) collective-permute-start(f32[288,128]{1,0:T(8,128)S(1)} %add.30), channel_id=1, source_target_pairs={{0,8},{4,60},{8,16},{12,4},{16,24},{20,12},{24,32},{28,20},{32,40}... | collective-permute-start | bytes 442376 | tf_op jit(solution)/shard_map/ppermute | solution.py:216
  23.9 1.5 %collective-permute-start.7 = (f32[288,128]{1,0:T(8,128)S(1)}, f32[288,128]{1,0:T(8,128)S(1)}, u32[]{:S(2)}, u32[]{:S(2)}) collective-permute-start(f32[288,128]{1,0:T(8,128)S(1)} %add.34), channel_id=1, source_target_pairs={{0,8},{4,60},{8,16},{12,4},{16,24},{20,12},{24,32},{28,20},{32,40}... | collective-permute-start | bytes 442376 | tf_op jit(solution)/shard_map/ppermute | solution.py:216
  25.4 1.5 %collective-permute-start.11 = (f32[288,128]{1,0:T(8,128)S(1)}, f32[288,128]{1,0:T(8,128)S(1)}, u32[]{:S(2)}, u32[]{:S(2)}) collective-permute-start(f32[288,128]{1,0:T(8,128)S(1)} %add.38), channel_id=1, source_target_pairs={{0,8},{4,60},{8,16},{12,4},{16,24},{20,12},{24,32},{28,20},{32,40}... | collective-permute-start | bytes 442376 | tf_op jit(solution)/shard_map/ppermute | solution.py:216
  27.0 1.5 %collective-permute-start.14 = (f32[288,128]{1,0:T(8,128)S(1)}, f32[288,128]{1,0:T(8,128)S(1)}, u32[]{:S(2)}, u32[]{:S(2)}) collective-permute-start(f32[288,128]{1,0:T(8,128)S(1)} %add.41), channel_id=1, source_target_pairs={{0,8},{4,60},{8,16},{12,4},{16,24},{20,12},{24,32},{28,20},{32,40}... | collective-permute-start | bytes 442376 | tf_op jit(solution)/shard_map/ppermute | solution.py:216
  28.6 1.5 %collective-permute-start.4 = (f32[288,128]{1,0:T(8,128)S(1)}, f32[288,128]{1,0:T(8,128)S(1)}, u32[]{:S(2)}, u32[]{:S(2)}) collective-permute-start(f32[288,128]{1,0:T(8,128)S(1)} %add.31), channel_id=1, source_target_pairs={{0,8},{4,60},{8,16},{12,4},{16,24},{20,12},{24,32},{28,20},{32,40}... | collective-permute-start | bytes 442376 | tf_op jit(solution)/shard_map/ppermute | solution.py:216
  30.2 1.5 %collective-permute-start.8 = (f32[288,128]{1,0:T(8,128)S(1)}, f32[288,128]{1,0:T(8,128)S(1)}, u32[]{:S(2)}, u32[]{:S(2)}) collective-permute-start(f32[288,128]{1,0:T(8,128)S(1)} %add.35), channel_id=1, source_target_pairs={{0,8},{4,60},{8,16},{12,4},{16,24},{20,12},{24,32},{28,20},{32,40}... | collective-permute-start | bytes 442376 | tf_op jit(solution)/shard_map/ppermute | solution.py:216
  31.8 1.5 %collective-permute-start.12 = (f32[288,128]{1,0:T(8,128)S(1)}, f32[288,128]{1,0:T(8,128)S(1)}, u32[]{:S(2)}, u32[]{:S(2)}) collective-permute-start(f32[288,128]{1,0:T(8,128)S(1)} %add.39), channel_id=1, source_target_pairs={{0,8},{4,60},{8,16},{12,4},{16,24},{20,12},{24,32},{28,20},{32,40}... | collective-permute-start | bytes 442376 | tf_op jit(solution)/shard_map/ppermute | solution.py:216
  33.3 1.5 %collective-permute-start.15 = (f32[288,128]{1,0:T(8,128)S(1)}, f32[288,128]{1,0:T(8,128)S(1)}, u32[]{:S(2)}, u32[]{:S(2)}) collective-permute-start(f32[288,128]{1,0:T(8,128)S(1)} %add.42), channel_id=1, source_target_pairs={{0,8},{4,60},{8,16},{12,4},{16,24},{20,12},{24,32},{28,20},{32,40}... | collective-permute-start | bytes 442376 | tf_op jit(solution)/shard_map/ppermute | solution.py:216
  34.9 1.7 %collective-permute-start.5 = (f32[288,128]{1,0:T(8,128)S(1)}, f32[288,128]{1,0:T(8,128)S(1)}, u32[]{:S(2)}, u32[]{:S(2)}) collective-permute-start(f32[288,128]{1,0:T(8,128)S(1)} %add.32), channel_id=1, source_target_pairs={{0,8},{4,60},{8,16},{12,4},{16,24},{20,12},{24,32},{28,20},{32,40}... | collective-permute-start | bytes 442376 | tf_op jit(solution)/shard_map/ppermute | solution.py:216
  36.7 1.4 %collective-permute-start.9 = (f32[288,128]{1,0:T(8,128)S(1)}, f32[288,128]{1,0:T(8,128)S(1)}, u32[]{:S(2)}, u32[]{:S(2)}) collective-permute-start(f32[288,128]{1,0:T(8,128)S(1)} %add.36), channel_id=1, source_target_pairs={{0,8},{4,60},{8,16},{12,4},{16,24},{20,12},{24,32},{28,20},{32,40}... | collective-permute-start | bytes 442376 | tf_op jit(solution)/shard_map/ppermute | solution.py:216
  38.8 1.4 %collective-permute-start.19 = (f32[288,128]{1,0:T(8,128)S(1)}, f32[288,128]{1,0:T(8,128)S(1)}, u32[]{:S(2)}, u32[]{:S(2)}) collective-permute-start(f32[288,128]{1,0:T(8,128)S(1)} %collective-permute-done.15.r3), channel_id=1, source_target_pairs={{0,4},{4,0},{1,5},{5,1},{2,6},{6,2},{3,7},{7,3},{8,12},{12,8},{9,1... | collective-permute-start | bytes 442376 | tf_op jit(solution)/shard_map/ppermute | solution.py:218
  40.3 1.8 %collective-permute-start.16 = (f32[288,128]{1,0:T(8,128)S(1)}, f32[288,128]{1,0:T(8,128)S(1)}, u32[]{:S(2)}, u32[]{:S(2)}) collective-permute-start(f32[288,128]{1,0:T(8,128)S(1)} %collective-permute-done.5.r0), channel_id=1, source_target_pairs={{0,4},{4,0},{1,5},{5,1},{2,6},{6,2},{3,7},{7,3},{8,12},{12,8},{9,1... | collective-permute-start | bytes 442376 | tf_op jit(solution)/shard_map/ppermute | solution.py:218
  42.1 1.6 %collective-permute-start.17 = (f32[288,128]{1,0:T(8,128)S(1)}, f32[288,128]{1,0:T(8,128)S(1)}, u32[]{:S(2)}, u32[]{:S(2)}) collective-permute-start(f32[288,128]{1,0:T(8,128)S(1)} %collective-permute-done.9.r1), channel_id=1, source_target_pairs={{0,4},{4,0},{1,5},{5,1},{2,6},{6,2},{3,7},{7,3},{8,12},{12,8},{9,1... | collective-permute-start | bytes 442376 | tf_op jit(solution)/shard_map/ppermute | solution.py:218
  43.7 1.0 %collective-permute-done.17.b1 = f32[288,128]{1,0:T(8,128)S(1)} collective-permute-done((f32[288,128]{1,0:T(8,128)S(1)}, f32[288,128]{1,0:T(8,128)S(1)}, u32[]{:S(2)}, u32[]{:S(2)}) %collective-permute-start.17) | collective-permute-done | bytes 147488 | tf_op jit(solution)/shard_map/ppermute | solution.py:218
  44.8 1.3 %collective-permute-start.20 = (f32[144,128]{1,0:T(8,128)S(1)}, f32[144,128]{1,0:T(8,128)S(1)}, u32[]{:S(2)}, u32[]{:S(2)}) collective-permute-start(f32[144,128]{1,0:T(8,128)S(1)} %get-tuple-element.21), channel_id=1, source_target_pairs={{0,64},{64,0},{128,192},{192,128},{1,65},{65,1},{129,193},{193,129... | collective-permute-start | bytes 221192 | tf_op jit(solution)/shard_map/ppermute | solution.py:231
  46.1 2.5 %collective-permute-start.21 = (f32[144,128]{1,0:T(8,128)S(1)}, f32[144,128]{1,0:T(8,128)S(1)}, u32[]{:S(2)}, u32[]{:S(2)}) collective-permute-start(f32[144,128]{1,0:T(8,128)S(1)} %get-tuple-element.22), channel_id=1, source_target_pairs={{0,128},{64,192},{128,0},{192,64},{1,129},{65,193},{129,1},{193,65... | collective-permute-start | bytes 221192 | tf_op jit(solution)/shard_map/ppermute | solution.py:231
  48.8 3.0 %collective-permute-done.21.t2 = f32[144,128]{1,0:T(8,128)S(1)} collective-permute-done((f32[144,128]{1,0:T(8,128)S(1)}, f32[144,128]{1,0:T(8,128)S(1)}, u32[]{:S(2)}, u32[]{:S(2)}) %collective-permute-start.21) | collective-permute-done | bytes 73760 | tf_op jit(solution)/shard_map/ppermute | solution.py:231
  51.8 1.6 %collective-permute-done.22.t3 = f32[144,128]{1,0:T(8,128)S(1)} collective-permute-done((f32[144,128]{1,0:T(8,128)S(1)}, f32[144,128]{1,0:T(8,128)S(1)}, u32[]{:S(2)}, u32[]{:S(2)}) %collective-permute-start.22) | collective-permute-done | bytes 73760 | tf_op jit(solution)/shard_map/ppermute | solution.py:231
  54.1 1.6 %collective-permute-start.23 = (f32[1,128]{1,0:T(1,128)S(1)}, f32[1,128]{1,0:T(1,128)S(1)}, u32[]{:S(2)}, u32[]{:S(2)}) collective-permute-start(f32[1,128]{1,0:T(1,128)S(1)} %get-tuple-element.25), channel_id=1, source_target_pairs={{0,4},{4,0},{1,5},{5,1},{2,6},{6,2},{3,7},{7,3},{8,12},{12,8},{9,1... | collective-permute-start | bytes 1544 | tf_op jit(solution)/shard_map/ppermute | solution.py:243
  55.7 0.8 %collective-permute-done.23 = f32[1,128]{1,0:T(1,128)S(1)} collective-permute-done((f32[1,128]{1,0:T(1,128)S(1)}, f32[1,128]{1,0:T(1,128)S(1)}, u32[]{:S(2)}, u32[]{:S(2)}) %collective-permute-start.23) | collective-permute-done | bytes 544 | tf_op jit(solution)/shard_map/ppermute | solution.py:243
  56.6 20.9 %all_to_all.5 = f32[128,1,128]{2,1,0:T(1,128)S(1)} all-to-all(f32[128,1,128]{2,1,0:T(1,128)S(1)} %broadcast_in_dim.16), channel_id=1, replica_groups=mesh['x'=4,'z'=8,'c'=2,'y'=4] {'x','z','y'}, dimensions={0} | all-to-all | bytes 131072 | tf_op jit(solution)/shard_map/all_to_all | solution.py:246
  77.5 1.3 %scale.1 = (bf16[4,4608]{1,0:T(4,128)(2,1)}, f32[4,16]{1,0:T(4,128)}, f32[1,4608]{1,0:T(1,128)}) custom-call(s32[3]{0:T(128)S(1)} %pad_add_fusion.place, s32[64]{0:T(128)S(1)} %copy-done.1, f32[4,4608]{1,0:T(4,128)S(1)} %get-tuple-element.24.exact, f32[128,128]{1,0:T(8,128)S(1)} %bitcast.13), custom_call_target="tpu_custom_call" | custom-call | tf_op jit(solution)/shard_map/scale/pallas_call | solution.py:247
  (52 shorter events, 4.6 us)
Async XLA Ops:
  4.3 1.7 %copy-start = (bf16[4,1,64,4608]{3,2,1,0:T(8,128)(2,1)S(1)}, bf16[4,1,64,4608]{3,2,1,0:T(8,128)(2,1)}, u32[]{:S(2)}) copy-start(bf16[4,1,64,4608]{3,2,1,0:T(8,128)(2,1)} %param.5) | copy-start | bytes 7077892
  7.1 13.9 %collective-permute-start = (f32[3456,128]{1,0:T(8,128)S(1)}, f32[3456,128]{1,0:T(8,128)S(1)}, u32[]{:S(2)}, u32[]{:S(2)}) collective-permute-start(f32[3456,128]{1,0:T(8,128)S(1)} %get-tuple-element.17), channel_id=1, source_target_pairs={{0,4},{4,0},{1,5},{5,1},{2,6},{6,2},{3,7},{7,3},{8,12},{12,8},{9,1... | collective-permute-start | bytes 5308424 | tf_op jit(solution)/shard_map/ppermute | solution.py:197
  11.3 3.2 %collective-permute-start.1 = (f32[1152,128]{1,0:T(8,128)S(1)}, f32[1152,128]{1,0:T(8,128)S(1)}, u32[]{:S(2)}, u32[]{:S(2)}) collective-permute-start(f32[1152,128]{1,0:T(8,128)S(1)} %get-tuple-element.19), channel_id=1, source_target_pairs={{0,4},{4,0},{1,5},{5,1},{2,6},{6,2},{3,7},{7,3},{8,12},{12,8},{9,1... | collective-permute-start | bytes 1769480 | tf_op jit(solution)/shard_map/ppermute | solution.py:195
  14.6 6.4 %collective-permute-start.2 = (f32[288,128]{1,0:T(8,128)S(1)}, f32[288,128]{1,0:T(8,128)S(1)}, u32[]{:S(2)}, u32[]{:S(2)}) collective-permute-start(f32[288,128]{1,0:T(8,128)S(1)} %add.29), channel_id=1, source_target_pairs={{0,8},{4,60},{8,16},{12,4},{16,24},{20,12},{24,32},{28,20},{32,40}... | collective-permute-start | bytes 442376 | tf_op jit(solution)/shard_map/ppermute | solution.py:216
  18.5 5.3 %collective-permute-start.6 = (f32[288,128]{1,0:T(8,128)S(1)}, f32[288,128]{1,0:T(8,128)S(1)}, u32[]{:S(2)}, u32[]{:S(2)}) collective-permute-start(f32[288,128]{1,0:T(8,128)S(1)} %add.33), channel_id=1, source_target_pairs={{0,8},{4,60},{8,16},{12,4},{16,24},{20,12},{24,32},{28,20},{32,40}... | collective-permute-start | bytes 442376 | tf_op jit(solution)/shard_map/ppermute | solution.py:216
  19.4 6.0 %collective-permute-start.10 = (f32[288,128]{1,0:T(8,128)S(1)}, f32[288,128]{1,0:T(8,128)S(1)}, u32[]{:S(2)}, u32[]{:S(2)}) collective-permute-start(f32[288,128]{1,0:T(8,128)S(1)} %add.37), channel_id=1, source_target_pairs={{0,8},{4,60},{8,16},{12,4},{16,24},{20,12},{24,32},{28,20},{32,40}... | collective-permute-start | bytes 442376 | tf_op jit(solution)/shard_map/ppermute | solution.py:216
  20.2 6.8 %collective-permute-start.13 = (f32[288,128]{1,0:T(8,128)S(1)}, f32[288,128]{1,0:T(8,128)S(1)}, u32[]{:S(2)}, u32[]{:S(2)}) collective-permute-start(f32[288,128]{1,0:T(8,128)S(1)} %add.40), channel_id=1, source_target_pairs={{0,8},{4,60},{8,16},{12,4},{16,24},{20,12},{24,32},{28,20},{32,40}... | collective-permute-start | bytes 442376 | tf_op jit(solution)/shard_map/ppermute | solution.py:216
  21.0 7.5 %collective-permute-start.3 = (f32[288,128]{1,0:T(8,128)S(1)}, f32[288,128]{1,0:T(8,128)S(1)}, u32[]{:S(2)}, u32[]{:S(2)}) collective-permute-start(f32[288,128]{1,0:T(8,128)S(1)} %add.30), channel_id=1, source_target_pairs={{0,8},{4,60},{8,16},{12,4},{16,24},{20,12},{24,32},{28,20},{32,40}... | collective-permute-start | bytes 442376 | tf_op jit(solution)/shard_map/ppermute | solution.py:216
  23.9 6.3 %collective-permute-start.7 = (f32[288,128]{1,0:T(8,128)S(1)}, f32[288,128]{1,0:T(8,128)S(1)}, u32[]{:S(2)}, u32[]{:S(2)}) collective-permute-start(f32[288,128]{1,0:T(8,128)S(1)} %add.34), channel_id=1, source_target_pairs={{0,8},{4,60},{8,16},{12,4},{16,24},{20,12},{24,32},{28,20},{32,40}... | collective-permute-start | bytes 442376 | tf_op jit(solution)/shard_map/ppermute | solution.py:216
  25.4 6.3 %collective-permute-start.11 = (f32[288,128]{1,0:T(8,128)S(1)}, f32[288,128]{1,0:T(8,128)S(1)}, u32[]{:S(2)}, u32[]{:S(2)}) collective-permute-start(f32[288,128]{1,0:T(8,128)S(1)} %add.38), channel_id=1, source_target_pairs={{0,8},{4,60},{8,16},{12,4},{16,24},{20,12},{24,32},{28,20},{32,40}... | collective-permute-start | bytes 442376 | tf_op jit(solution)/shard_map/ppermute | solution.py:216
  27.0 6.3 %collective-permute-start.14 = (f32[288,128]{1,0:T(8,128)S(1)}, f32[288,128]{1,0:T(8,128)S(1)}, u32[]{:S(2)}, u32[]{:S(2)}) collective-permute-start(f32[288,128]{1,0:T(8,128)S(1)} %add.41), channel_id=1, source_target_pairs={{0,8},{4,60},{8,16},{12,4},{16,24},{20,12},{24,32},{28,20},{32,40}... | collective-permute-start | bytes 442376 | tf_op jit(solution)/shard_map/ppermute | solution.py:216
  28.6 6.3 %collective-permute-start.4 = (f32[288,128]{1,0:T(8,128)S(1)}, f32[288,128]{1,0:T(8,128)S(1)}, u32[]{:S(2)}, u32[]{:S(2)}) collective-permute-start(f32[288,128]{1,0:T(8,128)S(1)} %add.31), channel_id=1, source_target_pairs={{0,8},{4,60},{8,16},{12,4},{16,24},{20,12},{24,32},{28,20},{32,40}... | collective-permute-start | bytes 442376 | tf_op jit(solution)/shard_map/ppermute | solution.py:216
  30.2 6.5 %collective-permute-start.8 = (f32[288,128]{1,0:T(8,128)S(1)}, f32[288,128]{1,0:T(8,128)S(1)}, u32[]{:S(2)}, u32[]{:S(2)}) collective-permute-start(f32[288,128]{1,0:T(8,128)S(1)} %add.35), channel_id=1, source_target_pairs={{0,8},{4,60},{8,16},{12,4},{16,24},{20,12},{24,32},{28,20},{32,40}... | collective-permute-start | bytes 442376 | tf_op jit(solution)/shard_map/ppermute | solution.py:216
  31.8 6.3 %collective-permute-start.12 = (f32[288,128]{1,0:T(8,128)S(1)}, f32[288,128]{1,0:T(8,128)S(1)}, u32[]{:S(2)}, u32[]{:S(2)}) collective-permute-start(f32[288,128]{1,0:T(8,128)S(1)} %add.39), channel_id=1, source_target_pairs={{0,8},{4,60},{8,16},{12,4},{16,24},{20,12},{24,32},{28,20},{32,40}... | collective-permute-start | bytes 442376 | tf_op jit(solution)/shard_map/ppermute | solution.py:216
  33.3 5.5 %collective-permute-start.15 = (f32[288,128]{1,0:T(8,128)S(1)}, f32[288,128]{1,0:T(8,128)S(1)}, u32[]{:S(2)}, u32[]{:S(2)}) collective-permute-start(f32[288,128]{1,0:T(8,128)S(1)} %add.42), channel_id=1, source_target_pairs={{0,8},{4,60},{8,16},{12,4},{16,24},{20,12},{24,32},{28,20},{32,40}... | collective-permute-start | bytes 442376 | tf_op jit(solution)/shard_map/ppermute | solution.py:216
  34.9 5.4 %collective-permute-start.5 = (f32[288,128]{1,0:T(8,128)S(1)}, f32[288,128]{1,0:T(8,128)S(1)}, u32[]{:S(2)}, u32[]{:S(2)}) collective-permute-start(f32[288,128]{1,0:T(8,128)S(1)} %add.32), channel_id=1, source_target_pairs={{0,8},{4,60},{8,16},{12,4},{16,24},{20,12},{24,32},{28,20},{32,40}... | collective-permute-start | bytes 442376 | tf_op jit(solution)/shard_map/ppermute | solution.py:216
  36.7 12.1 %copy-start.2 = (bf16[1,4608]{1,0:T(2,128)(2,1)S(1)}, bf16[1,4608]{1,0:T(2,128)(2,1)}, u32[]{:S(2)}) copy-start(bf16[1,4608]{1,0:T(2,128)(2,1)} %param.7) | copy-start | bytes 27652
  36.7 16.8 %copy-start.1 = (s32[64]{0:T(128)S(1)}, s32[64]{0:T(128)}, u32[]{:S(2)}) copy-start(s32[64]{0:T(128)} %bucket.3) | copy-start | bytes 772
  36.7 5.4 %collective-permute-start.9 = (f32[288,128]{1,0:T(8,128)S(1)}, f32[288,128]{1,0:T(8,128)S(1)}, u32[]{:S(2)}, u32[]{:S(2)}) collective-permute-start(f32[288,128]{1,0:T(8,128)S(1)} %add.36), channel_id=1, source_target_pairs={{0,8},{4,60},{8,16},{12,4},{16,24},{20,12},{24,32},{28,20},{32,40}... | collective-permute-start | bytes 442376 | tf_op jit(solution)/shard_map/ppermute | solution.py:216
  38.1 5.6 %collective-permute-start.18 = (f32[288,128]{1,0:T(8,128)S(1)}, f32[288,128]{1,0:T(8,128)S(1)}, u32[]{:S(2)}, u32[]{:S(2)}) collective-permute-start(f32[288,128]{1,0:T(8,128)S(1)} %collective-permute-done.12.r2), channel_id=1, source_target_pairs={{0,4},{4,0},{1,5},{5,1},{2,6},{6,2},{3,7},{7,3},{8,12},{12,8},{9,1... | collective-permute-start | bytes 442376 | tf_op jit(solution)/shard_map/ppermute | solution.py:218
  38.8 4.9 %collective-permute-start.19 = (f32[288,128]{1,0:T(8,128)S(1)}, f32[288,128]{1,0:T(8,128)S(1)}, u32[]{:S(2)}, u32[]{:S(2)}) collective-permute-start(f32[288,128]{1,0:T(8,128)S(1)} %collective-permute-done.15.r3), channel_id=1, source_target_pairs={{0,4},{4,0},{1,5},{5,1},{2,6},{6,2},{3,7},{7,3},{8,12},{12,8},{9,1... | collective-permute-start | bytes 442376 | tf_op jit(solution)/shard_map/ppermute | solution.py:218
  40.3 3.4 %collective-permute-start.16 = (f32[288,128]{1,0:T(8,128)S(1)}, f32[288,128]{1,0:T(8,128)S(1)}, u32[]{:S(2)}, u32[]{:S(2)}) collective-permute-start(f32[288,128]{1,0:T(8,128)S(1)} %collective-permute-done.5.r0), channel_id=1, source_target_pairs={{0,4},{4,0},{1,5},{5,1},{2,6},{6,2},{3,7},{7,3},{8,12},{12,8},{9,1... | collective-permute-start | bytes 442376 | tf_op jit(solution)/shard_map/ppermute | solution.py:218
  42.1 2.6 %collective-permute-start.17 = (f32[288,128]{1,0:T(8,128)S(1)}, f32[288,128]{1,0:T(8,128)S(1)}, u32[]{:S(2)}, u32[]{:S(2)}) collective-permute-start(f32[288,128]{1,0:T(8,128)S(1)} %collective-permute-done.9.r1), channel_id=1, source_target_pairs={{0,4},{4,0},{1,5},{5,1},{2,6},{6,2},{3,7},{7,3},{8,12},{12,8},{9,1... | collective-permute-start | bytes 442376 | tf_op jit(solution)/shard_map/ppermute | solution.py:218
  44.8 4.0 %collective-permute-start.20 = (f32[144,128]{1,0:T(8,128)S(1)}, f32[144,128]{1,0:T(8,128)S(1)}, u32[]{:S(2)}, u32[]{:S(2)}) collective-permute-start(f32[144,128]{1,0:T(8,128)S(1)} %get-tuple-element.21), channel_id=1, source_target_pairs={{0,64},{64,0},{128,192},{192,128},{1,65},{65,1},{129,193},{193,129... | collective-permute-start | bytes 221192 | tf_op jit(solution)/shard_map/ppermute | solution.py:231
  46.1 5.7 %collective-permute-start.21 = (f32[144,128]{1,0:T(8,128)S(1)}, f32[144,128]{1,0:T(8,128)S(1)}, u32[]{:S(2)}, u32[]{:S(2)}) collective-permute-start(f32[144,128]{1,0:T(8,128)S(1)} %get-tuple-element.22), channel_id=1, source_target_pairs={{0,128},{64,192},{128,0},{192,64},{1,129},{65,193},{129,1},{193,65... | collective-permute-start | bytes 221192 | tf_op jit(solution)/shard_map/ppermute | solution.py:231
  48.5 4.9 %collective-permute-start.22 = (f32[144,128]{1,0:T(8,128)S(1)}, f32[144,128]{1,0:T(8,128)S(1)}, u32[]{:S(2)}, u32[]{:S(2)}) collective-permute-start(f32[144,128]{1,0:T(8,128)S(1)} %get-tuple-element.23), channel_id=1, source_target_pairs={{0,192},{64,128},{128,64},{192,0},{1,193},{65,129},{129,65},{193,1... | collective-permute-start | bytes 221192 | tf_op jit(solution)/shard_map/ppermute | solution.py:231
  54.1 2.4 %collective-permute-start.23 = (f32[1,128]{1,0:T(1,128)S(1)}, f32[1,128]{1,0:T(1,128)S(1)}, u32[]{:S(2)}, u32[]{:S(2)}) collective-permute-start(f32[1,128]{1,0:T(1,128)S(1)} %get-tuple-element.25), channel_id=1, source_target_pairs={{0,4},{4,0},{1,5},{5,1},{2,6},{6,2},{3,7},{7,3},{8,12},{12,8},{9,1... | collective-permute-start | bytes 1544 | tf_op jit(solution)/shard_map/ppermute | solution.py:243

commit v4 on v3

--- a/solution.py
+++ b/solution.py
@@ -45,8 +45,7 @@
     group = lax.broadcasted_iota(jnp.int32, shape, 0) // 8
     g = lax.broadcasted_iota(jnp.int32, shape, 0) % 8
     lane = lax.broadcasted_iota(jnp.int32, shape, 1)
-    arrival, bucket = table[0:1, 0:ROWS], table[0:1, ROWS : 2 * ROWS]
-    exponents = table[1:2, 0:ROWS]
+    arrival, bucket = table[STEPS : STEPS + 1, 0:ROWS], table[STEPS + 1 : STEPS + 2, 0:ROWS]
     to_x = x ^ (g % 4)
     for rel in range(STEPS):
         k = jnp.zeros(shape, jnp.int32)
@@ -56,10 +55,8 @@
         owner = jnp.where(k <= (4 if rel < 2 else 3), c, 1 - c)
         ids = (to_x * 8 + to_z) * 2 + (owner ^ (g // 4))
         row_bucket = jnp.sum(jnp.where(ids == lane, bucket, 0), axis=1, keepdims=True)
-        step = rel ^ (2 * (1 - c))
-        power = jnp.sum(
-            jnp.where(row_bucket + step * NB == lane, exponents, 0), axis=1, keepdims=True
-        )
+        exponents = jnp.where(c == 0, table[rel ^ 2, 0:ROWS][None], table[rel, 0:ROWS][None])
+        power = jnp.sum(jnp.where(row_bucket == lane, exponents, 0), axis=1, keepdims=True)
         factor = jnp.ones((ROWS, 1), jnp.float32)
         for bit in range(6):
             factor = factor * jnp.where((power >> bit) & 1 == 1, 2.0 ** -(2**bit), 1.0)
@@ -180,15 +177,19 @@
     smem = pl.BlockSpec(memory_space=pltpu.SMEM)
     codes = grad_codes[:, 0]
 
-    words = jnp.concatenate([arrival, bucket_of_row, exponents.reshape(-1), jnp.zeros_like(arrival)])
+    def wide(rows):
+        return jnp.pad(rows, ((0, 0), (0, LANES - rows.shape[1])))
+
+    words = jnp.concatenate([wide(exponents[:, 0]), wide(arrival[None]), wide(bucket_of_row[None])])
     picks = pl.pallas_call(
         picks_kernel,
         out_shape=jax.ShapeDtypeStruct((STEPS, ROWS, ROWS), jnp.bfloat16),
         in_specs=[smem, vmem],
         out_specs=vmem,
         compiler_params=room(4),
+        cost_estimate=pl.CostEstimate(flops=3 * 10**9, bytes_accessed=10**5, transcendentals=0),
         name="picks",
-    )(place, words.reshape(2, LANES))
+    )(place, words)
 
     swap = [(0, 1), (1, 0)]
     mine0, send0 = spread(0, place, picks, codes)

time: 79 us -> 76.1 us (0.963)
  local copies, waits for them, and re-layouts: 2.31 us -> 0.82 us
  other arithmetic: 2.16 us -> 0.86 us
    unnamed x7 -> x6, local copies, waits for them, and re-layouts: 2.19 us -> 0.78 us
    unnamed x2 -> x1, other arithmetic: 1.33 us -> 0.06 us
where the time goes in v4:
time: 76.1 us; the launch traced here: 76 us
  starting transfers between devices  37.6 us (49%)
  blocking collectives  20.9 us (27%)
  waiting for transfers between devices  9.68 us (13%)
  Pallas kernels  5.36 us (7%)
  other arithmetic  0.86 us (1%)
  local copies, waits for them, and re-layouts  0.82 us (1%)
    ppermute x14, starting transfers between devices, on_device(): ring[rel] = (lax.ppermute(held, ('z', 'c'), turn),)  23.1 us
    all_to_all x1, blocking collectives, on_device(): tables = lax.all_to_all(copies, ('x', 'z', 'y'), 0, 0, tiled=True)  20.9 us
    ppermute x4, starting transfers between devices, on_device(): back = [lax.ppermute(arrived, 'c', swap) for arrived in ring]  5.52 us
    ppermute x3, waiting for transfers between devices, on_device(): totals.append(lax.ppermute(pieces[k], 'x', [(i, i ^ k) for i in range(4)]))  4.63 us
    ppermute x3, starting transfers between devices, on_device(): totals.append(lax.ppermute(pieces[k], 'x', [(i, i ^ k) for i in range(4)]))  3.94 us
    ppermute x1, starting transfers between devices, on_device(): got1 = lax.ppermute(send1, 'c', swap)  3.29 us
    ppermute x1, waiting for transfers between devices, on_device(): got0 = lax.ppermute(send0, 'c', swap)  3.1 us
    pallas_call x2, Pallas kernels, spread(): pl.pallas_call(functools.partial(spread_kernel, tiles, late), out_shape=(...  2.11 us
  transfers between devices with their start and end apart: 24, of which 6 were waited for; matrix products, arithmetic and copies ran while one was open for 0% of the time, Pallas kernels for 2%

profile of v4, /device:TPU:1, one launch (start us, length us, event | category | flops | bytes accessed | tf_op | source)
XLA Modules:
  0.0 76.0 jit_solution(1595376118423884546)
XLA Ops:
  1.4 0.9 %picks.1 = bf16[4,64,64]{2,1,0:T(8,128)(2,1)S(1)} custom-call(s32[3]{0:T(128)S(1)} %pad_add_fusion.2.place, s32[6,128]{1,0:T(8,128)S(1)} %pad_add_fusion.table), custom_call_target="tpu_custom_call" | custom-call | flops 3000000000 | bytes 100000 | tf_op jit(solution)/shard_map/picks/pallas_call | solution.py:184
  2.3 0.8 %copy-done = bf16[4,1,64,4608]{3,2,1,0:T(8,128)(2,1)S(1)} copy-done((bf16[4,1,64,4608]{3,2,1,0:T(8,128)(2,1)S(1)}, bf16[4,1,64,4608]{3,2,1,0:T(8,128)(2,1)}, u32[]{:S(2)}) %copy-start) | copy-done | bytes 2359320
  3.1 1.1 %spread.2 = (f32[3456,128]{1,0:T(8,128)S(1)}, f32[3456,128]{1,0:T(8,128)S(1)}) custom-call(s32[3]{0:T(128)S(1)} %pad_add_fusion.2.place, bf16[4,64,64]{2,1,0:T(8,128)(2,1)S(1)} %picks.1, bf16[4,64,4608]{2,1,0:T(8,128)(2,1)S(1)} %bitcast.12), custom_call_target="tpu_custom_call" | custom-call | tf_op jit(solution)/shard_map/spread/pallas_call | solution.py:103
  4.2 3.3 %collective-permute-start = (f32[3456,128]{1,0:T(8,128)S(1)}, f32[3456,128]{1,0:T(8,128)S(1)}, u32[]{:S(2)}, u32[]{:S(2)}) collective-permute-start(f32[3456,128]{1,0:T(8,128)S(1)} %get-tuple-element.17), channel_id=1, source_target_pairs={{0,4},{4,0},{1,5},{5,1},{2,6},{6,2},{3,7},{7,3},{8,12},{12,8},{9,1... | collective-permute-start | bytes 5308424 | tf_op jit(solution)/shard_map/ppermute | solution.py:198
  7.5 1.0 %spread.3 = (f32[1152,128]{1,0:T(8,128)S(1)}, f32[1152,128]{1,0:T(8,128)S(1)}) custom-call(s32[3]{0:T(128)S(1)} %pad_add_fusion.2.place, bf16[4,64,64]{2,1,0:T(8,128)(2,1)S(1)} %picks.1, bf16[4,64,4608]{2,1,0:T(8,128)(2,1)S(1)} %bitcast.13), custom_call_target="tpu_custom_call" | custom-call | tf_op jit(solution)/shard_map/spread/pallas_call | solution.py:103
  8.6 3.1 %collective-permute-done.1.refs_1_ = f32[1152,128]{1,0:T(8,128)S(1)} collective-permute-done((f32[1152,128]{1,0:T(8,128)S(1)}, f32[1152,128]{1,0:T(8,128)S(1)}, u32[]{:S(2)}, u32[]{:S(2)}) %collective-permute-start.1) | collective-permute-done | bytes 589856 | tf_op jit(solution)/shard_map/ppermute | solution.py:196
  11.7 3.9 %collective-permute-start.2 = (f32[288,128]{1,0:T(8,128)S(1)}, f32[288,128]{1,0:T(8,128)S(1)}, u32[]{:S(2)}, u32[]{:S(2)}) collective-permute-start(f32[288,128]{1,0:T(8,128)S(1)} %add.31), channel_id=1, source_target_pairs={{0,8},{4,60},{8,16},{12,4},{16,24},{20,12},{24,32},{28,20},{32,40}... | collective-permute-start | bytes 442376 | tf_op jit(solution)/shard_map/ppermute | solution.py:217
  15.7 0.8 %collective-permute-start.6 = (f32[288,128]{1,0:T(8,128)S(1)}, f32[288,128]{1,0:T(8,128)S(1)}, u32[]{:S(2)}, u32[]{:S(2)}) collective-permute-start(f32[288,128]{1,0:T(8,128)S(1)} %add.35), channel_id=1, source_target_pairs={{0,8},{4,60},{8,16},{12,4},{16,24},{20,12},{24,32},{28,20},{32,40}... | collective-permute-start | bytes 442376 | tf_op jit(solution)/shard_map/ppermute | solution.py:217
  16.5 0.8 %collective-permute-start.10 = (f32[288,128]{1,0:T(8,128)S(1)}, f32[288,128]{1,0:T(8,128)S(1)}, u32[]{:S(2)}, u32[]{:S(2)}) collective-permute-start(f32[288,128]{1,0:T(8,128)S(1)} %add.39), channel_id=1, source_target_pairs={{0,8},{4,60},{8,16},{12,4},{16,24},{20,12},{24,32},{28,20},{32,40}... | collective-permute-start | bytes 442376 | tf_op jit(solution)/shard_map/ppermute | solution.py:217
  17.3 0.8 %collective-permute-start.13 = (f32[288,128]{1,0:T(8,128)S(1)}, f32[288,128]{1,0:T(8,128)S(1)}, u32[]{:S(2)}, u32[]{:S(2)}) collective-permute-start(f32[288,128]{1,0:T(8,128)S(1)} %add.42), channel_id=1, source_target_pairs={{0,8},{4,60},{8,16},{12,4},{16,24},{20,12},{24,32},{28,20},{32,40}... | collective-permute-start | bytes 442376 | tf_op jit(solution)/shard_map/ppermute | solution.py:217
  18.2 2.8 %collective-permute-start.3 = (f32[288,128]{1,0:T(8,128)S(1)}, f32[288,128]{1,0:T(8,128)S(1)}, u32[]{:S(2)}, u32[]{:S(2)}) collective-permute-start(f32[288,128]{1,0:T(8,128)S(1)} %add.32), channel_id=1, source_target_pairs={{0,8},{4,60},{8,16},{12,4},{16,24},{20,12},{24,32},{28,20},{32,40}... | collective-permute-start | bytes 442376 | tf_op jit(solution)/shard_map/ppermute | solution.py:217
  21.0 1.5 %collective-permute-start.7 = (f32[288,128]{1,0:T(8,128)S(1)}, f32[288,128]{1,0:T(8,128)S(1)}, u32[]{:S(2)}, u32[]{:S(2)}) collective-permute-start(f32[288,128]{1,0:T(8,128)S(1)} %add.36), channel_id=1, source_target_pairs={{0,8},{4,60},{8,16},{12,4},{16,24},{20,12},{24,32},{28,20},{32,40}... | collective-permute-start | bytes 442376 | tf_op jit(solution)/shard_map/ppermute | solution.py:217
  22.6 1.5 %collective-permute-start.11 = (f32[288,128]{1,0:T(8,128)S(1)}, f32[288,128]{1,0:T(8,128)S(1)}, u32[]{:S(2)}, u32[]{:S(2)}) collective-permute-start(f32[288,128]{1,0:T(8,128)S(1)} %add.40), channel_id=1, source_target_pairs={{0,8},{4,60},{8,16},{12,4},{16,24},{20,12},{24,32},{28,20},{32,40}... | collective-permute-start | bytes 442376 | tf_op jit(solution)/shard_map/ppermute | solution.py:217
  24.2 1.5 %collective-permute-start.14 = (f32[288,128]{1,0:T(8,128)S(1)}, f32[288,128]{1,0:T(8,128)S(1)}, u32[]{:S(2)}, u32[]{:S(2)}) collective-permute-start(f32[288,128]{1,0:T(8,128)S(1)} %add.43), channel_id=1, source_target_pairs={{0,8},{4,60},{8,16},{12,4},{16,24},{20,12},{24,32},{28,20},{32,40}... | collective-permute-start | bytes 442376 | tf_op jit(solution)/shard_map/ppermute | solution.py:217
  25.7 1.5 %collective-permute-start.4 = (f32[288,128]{1,0:T(8,128)S(1)}, f32[288,128]{1,0:T(8,128)S(1)}, u32[]{:S(2)}, u32[]{:S(2)}) collective-permute-start(f32[288,128]{1,0:T(8,128)S(1)} %add.33), channel_id=1, source_target_pairs={{0,8},{4,60},{8,16},{12,4},{16,24},{20,12},{24,32},{28,20},{32,40}... | collective-permute-start | bytes 442376 | tf_op jit(solution)/shard_map/ppermute | solution.py:217
  27.3 1.5 %collective-permute-start.8 = (f32[288,128]{1,0:T(8,128)S(1)}, f32[288,128]{1,0:T(8,128)S(1)}, u32[]{:S(2)}, u32[]{:S(2)}) collective-permute-start(f32[288,128]{1,0:T(8,128)S(1)} %add.37), channel_id=1, source_target_pairs={{0,8},{4,60},{8,16},{12,4},{16,24},{20,12},{24,32},{28,20},{32,40}... | collective-permute-start | bytes 442376 | tf_op jit(solution)/shard_map/ppermute | solution.py:217
  28.9 1.5 %collective-permute-start.12 = (f32[288,128]{1,0:T(8,128)S(1)}, f32[288,128]{1,0:T(8,128)S(1)}, u32[]{:S(2)}, u32[]{:S(2)}) collective-permute-start(f32[288,128]{1,0:T(8,128)S(1)} %add.41), channel_id=1, source_target_pairs={{0,8},{4,60},{8,16},{12,4},{16,24},{20,12},{24,32},{28,20},{32,40}... | collective-permute-start | bytes 442376 | tf_op jit(solution)/shard_map/ppermute | solution.py:217
  30.5 1.5 %collective-permute-start.15 = (f32[288,128]{1,0:T(8,128)S(1)}, f32[288,128]{1,0:T(8,128)S(1)}, u32[]{:S(2)}, u32[]{:S(2)}) collective-permute-start(f32[288,128]{1,0:T(8,128)S(1)} %add.44), channel_id=1, source_target_pairs={{0,8},{4,60},{8,16},{12,4},{16,24},{20,12},{24,32},{28,20},{32,40}... | collective-permute-start | bytes 442376 | tf_op jit(solution)/shard_map/ppermute | solution.py:217
  32.1 1.7 %collective-permute-start.5 = (f32[288,128]{1,0:T(8,128)S(1)}, f32[288,128]{1,0:T(8,128)S(1)}, u32[]{:S(2)}, u32[]{:S(2)}) collective-permute-start(f32[288,128]{1,0:T(8,128)S(1)} %add.34), channel_id=1, source_target_pairs={{0,8},{4,60},{8,16},{12,4},{16,24},{20,12},{24,32},{28,20},{32,40}... | collective-permute-start | bytes 442376 | tf_op jit(solution)/shard_map/ppermute | solution.py:217
  33.8 1.4 %collective-permute-start.9 = (f32[288,128]{1,0:T(8,128)S(1)}, f32[288,128]{1,0:T(8,128)S(1)}, u32[]{:S(2)}, u32[]{:S(2)}) collective-permute-start(f32[288,128]{1,0:T(8,128)S(1)} %add.38), channel_id=1, source_target_pairs={{0,8},{4,60},{8,16},{12,4},{16,24},{20,12},{24,32},{28,20},{32,40}... | collective-permute-start | bytes 442376 | tf_op jit(solution)/shard_map/ppermute | solution.py:217
  36.0 1.4 %collective-permute-start.19 = (f32[288,128]{1,0:T(8,128)S(1)}, f32[288,128]{1,0:T(8,128)S(1)}, u32[]{:S(2)}, u32[]{:S(2)}) collective-permute-start(f32[288,128]{1,0:T(8,128)S(1)} %collective-permute-done.15.r3), channel_id=1, source_target_pairs={{0,4},{4,0},{1,5},{5,1},{2,6},{6,2},{3,7},{7,3},{8,12},{12,8},{9,1... | collective-permute-start | bytes 442376 | tf_op jit(solution)/shard_map/ppermute | solution.py:219
  37.4 1.8 %collective-permute-start.16 = (f32[288,128]{1,0:T(8,128)S(1)}, f32[288,128]{1,0:T(8,128)S(1)}, u32[]{:S(2)}, u32[]{:S(2)}) collective-permute-start(f32[288,128]{1,0:T(8,128)S(1)} %collective-permute-done.5.r0), channel_id=1, source_target_pairs={{0,4},{4,0},{1,5},{5,1},{2,6},{6,2},{3,7},{7,3},{8,12},{12,8},{9,1... | collective-permute-start | bytes 442376 | tf_op jit(solution)/shard_map/ppermute | solution.py:219
  39.2 1.6 %collective-permute-start.17 = (f32[288,128]{1,0:T(8,128)S(1)}, f32[288,128]{1,0:T(8,128)S(1)}, u32[]{:S(2)}, u32[]{:S(2)}) collective-permute-start(f32[288,128]{1,0:T(8,128)S(1)} %collective-permute-done.9.r1), channel_id=1, source_target_pairs={{0,4},{4,0},{1,5},{5,1},{2,6},{6,2},{3,7},{7,3},{8,12},{12,8},{9,1... | collective-permute-start | bytes 442376 | tf_op jit(solution)/shard_map/ppermute | solution.py:219
  40.9 1.0 %collective-permute-done.17.b1 = f32[288,128]{1,0:T(8,128)S(1)} collective-permute-done((f32[288,128]{1,0:T(8,128)S(1)}, f32[288,128]{1,0:T(8,128)S(1)}, u32[]{:S(2)}, u32[]{:S(2)}) %collective-permute-start.17) | collective-permute-done | bytes 147488 | tf_op jit(solution)/shard_map/ppermute | solution.py:219
  41.9 1.3 %collective-permute-start.20 = (f32[144,128]{1,0:T(8,128)S(1)}, f32[144,128]{1,0:T(8,128)S(1)}, u32[]{:S(2)}, u32[]{:S(2)}) collective-permute-start(f32[144,128]{1,0:T(8,128)S(1)} %get-tuple-element.21), channel_id=1, source_target_pairs={{0,64},{64,0},{128,192},{192,128},{1,65},{65,1},{129,193},{193,129... | collective-permute-start | bytes 221192 | tf_op jit(solution)/shard_map/ppermute | solution.py:232
  43.2 2.5 %collective-permute-start.21 = (f32[144,128]{1,0:T(8,128)S(1)}, f32[144,128]{1,0:T(8,128)S(1)}, u32[]{:S(2)}, u32[]{:S(2)}) collective-permute-start(f32[144,128]{1,0:T(8,128)S(1)} %get-tuple-element.22), channel_id=1, source_target_pairs={{0,128},{64,192},{128,0},{192,64},{1,129},{65,193},{129,1},{193,65... | collective-permute-start | bytes 221192 | tf_op jit(solution)/shard_map/ppermute | solution.py:232
  46.0 3.0 %collective-permute-done.21.t2 = f32[144,128]{1,0:T(8,128)S(1)} collective-permute-done((f32[144,128]{1,0:T(8,128)S(1)}, f32[144,128]{1,0:T(8,128)S(1)}, u32[]{:S(2)}, u32[]{:S(2)}) %collective-permute-start.21) | collective-permute-done | bytes 73760 | tf_op jit(solution)/shard_map/ppermute | solution.py:232
  49.0 1.6 %collective-permute-done.22.t3 = f32[144,128]{1,0:T(8,128)S(1)} collective-permute-done((f32[144,128]{1,0:T(8,128)S(1)}, f32[144,128]{1,0:T(8,128)S(1)}, u32[]{:S(2)}, u32[]{:S(2)}) %collective-permute-start.22) | collective-permute-done | bytes 73760 | tf_op jit(solution)/shard_map/ppermute | solution.py:232
  51.3 1.6 %collective-permute-start.23 = (f32[1,128]{1,0:T(1,128)S(1)}, f32[1,128]{1,0:T(1,128)S(1)}, u32[]{:S(2)}, u32[]{:S(2)}) collective-permute-start(f32[1,128]{1,0:T(1,128)S(1)} %get-tuple-element.25), channel_id=1, source_target_pairs={{0,4},{4,0},{1,5},{5,1},{2,6},{6,2},{3,7},{7,3},{8,12},{12,8},{9,1... | collective-permute-start | bytes 1544 | tf_op jit(solution)/shard_map/ppermute | solution.py:244
  52.9 0.8 %collective-permute-done.23 = f32[1,128]{1,0:T(1,128)S(1)} collective-permute-done((f32[1,128]{1,0:T(1,128)S(1)}, f32[1,128]{1,0:T(1,128)S(1)}, u32[]{:S(2)}, u32[]{:S(2)}) %collective-permute-start.23) | collective-permute-done | bytes 544 | tf_op jit(solution)/shard_map/ppermute | solution.py:244
  53.8 20.9 %all_to_all.5 = f32[128,1,128]{2,1,0:T(1,128)S(1)} all-to-all(f32[128,1,128]{2,1,0:T(1,128)S(1)} %broadcast_in_dim.20), channel_id=1, replica_groups=mesh['x'=4,'z'=8,'c'=2,'y'=4] {'x','z','y'}, dimensions={0} | all-to-all | bytes 131072 | tf_op jit(solution)/shard_map/all_to_all | solution.py:247
  74.7 1.3 %scale.1 = (bf16[4,4608]{1,0:T(4,128)(2,1)}, f32[4,16]{1,0:T(4,128)}, f32[1,4608]{1,0:T(1,128)}) custom-call(s32[3]{0:T(128)S(1)} %pad_add_fusion.2.place, s32[64]{0:T(128)S(1)} %copy-done.1, f32[4,4608]{1,0:T(4,128)S(1)} %get-tuple-element.24.exact, f32[128,128]{1,0:T(8,128)S(1)} %bitcast.14), custom_call_target="tpu_custom_call" | custom-call | tf_op jit(solution)/shard_map/scale/pallas_call | solution.py:248
  (48 shorter events, 3.2 us)
Async XLA Ops:
  1.4 1.7 %copy-start = (bf16[4,1,64,4608]{3,2,1,0:T(8,128)(2,1)S(1)}, bf16[4,1,64,4608]{3,2,1,0:T(8,128)(2,1)}, u32[]{:S(2)}) copy-start(bf16[4,1,64,4608]{3,2,1,0:T(8,128)(2,1)} %param.5) | copy-start | bytes 7077892
  4.2 13.9 %collective-permute-start = (f32[3456,128]{1,0:T(8,128)S(1)}, f32[3456,128]{1,0:T(8,128)S(1)}, u32[]{:S(2)}, u32[]{:S(2)}) collective-permute-start(f32[3456,128]{1,0:T(8,128)S(1)} %get-tuple-element.17), channel_id=1, source_target_pairs={{0,4},{4,0},{1,5},{5,1},{2,6},{6,2},{3,7},{7,3},{8,12},{12,8},{9,1... | collective-permute-start | bytes 5308424 | tf_op jit(solution)/shard_map/ppermute | solution.py:198
  8.5 3.2 %collective-permute-start.1 = (f32[1152,128]{1,0:T(8,128)S(1)}, f32[1152,128]{1,0:T(8,128)S(1)}, u32[]{:S(2)}, u32[]{:S(2)}) collective-permute-start(f32[1152,128]{1,0:T(8,128)S(1)} %get-tuple-element.19), channel_id=1, source_target_pairs={{0,4},{4,0},{1,5},{5,1},{2,6},{6,2},{3,7},{7,3},{8,12},{12,8},{9,1... | collective-permute-start | bytes 1769480 | tf_op jit(solution)/shard_map/ppermute | solution.py:196
  11.7 6.4 %collective-permute-start.2 = (f32[288,128]{1,0:T(8,128)S(1)}, f32[288,128]{1,0:T(8,128)S(1)}, u32[]{:S(2)}, u32[]{:S(2)}) collective-permute-start(f32[288,128]{1,0:T(8,128)S(1)} %add.31), channel_id=1, source_target_pairs={{0,8},{4,60},{8,16},{12,4},{16,24},{20,12},{24,32},{28,20},{32,40}... | collective-permute-start | bytes 442376 | tf_op jit(solution)/shard_map/ppermute | solution.py:217
  15.7 5.3 %collective-permute-start.6 = (f32[288,128]{1,0:T(8,128)S(1)}, f32[288,128]{1,0:T(8,128)S(1)}, u32[]{:S(2)}, u32[]{:S(2)}) collective-permute-start(f32[288,128]{1,0:T(8,128)S(1)} %add.35), channel_id=1, source_target_pairs={{0,8},{4,60},{8,16},{12,4},{16,24},{20,12},{24,32},{28,20},{32,40}... | collective-permute-start | bytes 442376 | tf_op jit(solution)/shard_map/ppermute | solution.py:217
  16.5 6.0 %collective-permute-start.10 = (f32[288,128]{1,0:T(8,128)S(1)}, f32[288,128]{1,0:T(8,128)S(1)}, u32[]{:S(2)}, u32[]{:S(2)}) collective-permute-start(f32[288,128]{1,0:T(8,128)S(1)} %add.39), channel_id=1, source_target_pairs={{0,8},{4,60},{8,16},{12,4},{16,24},{20,12},{24,32},{28,20},{32,40}... | collective-permute-start | bytes 442376 | tf_op jit(solution)/shard_map/ppermute | solution.py:217
  17.3 6.8 %collective-permute-start.13 = (f32[288,128]{1,0:T(8,128)S(1)}, f32[288,128]{1,0:T(8,128)S(1)}, u32[]{:S(2)}, u32[]{:S(2)}) collective-permute-start(f32[288,128]{1,0:T(8,128)S(1)} %add.42), channel_id=1, source_target_pairs={{0,8},{4,60},{8,16},{12,4},{16,24},{20,12},{24,32},{28,20},{32,40}... | collective-permute-start | bytes 442376 | tf_op jit(solution)/shard_map/ppermute | solution.py:217
  18.2 7.5 %collective-permute-start.3 = (f32[288,128]{1,0:T(8,128)S(1)}, f32[288,128]{1,0:T(8,128)S(1)}, u32[]{:S(2)}, u32[]{:S(2)}) collective-permute-start(f32[288,128]{1,0:T(8,128)S(1)} %add.32), channel_id=1, source_target_pairs={{0,8},{4,60},{8,16},{12,4},{16,24},{20,12},{24,32},{28,20},{32,40}... | collective-permute-start | bytes 442376 | tf_op jit(solution)/shard_map/ppermute | solution.py:217
  21.0 6.3 %collective-permute-start.7 = (f32[288,128]{1,0:T(8,128)S(1)}, f32[288,128]{1,0:T(8,128)S(1)}, u32[]{:S(2)}, u32[]{:S(2)}) collective-permute-start(f32[288,128]{1,0:T(8,128)S(1)} %add.36), channel_id=1, source_target_pairs={{0,8},{4,60},{8,16},{12,4},{16,24},{20,12},{24,32},{28,20},{32,40}... | collective-permute-start | bytes 442376 | tf_op jit(solution)/shard_map/ppermute | solution.py:217
  22.6 6.3 %collective-permute-start.11 = (f32[288,128]{1,0:T(8,128)S(1)}, f32[288,128]{1,0:T(8,128)S(1)}, u32[]{:S(2)}, u32[]{:S(2)}) collective-permute-start(f32[288,128]{1,0:T(8,128)S(1)} %add.40), channel_id=1, source_target_pairs={{0,8},{4,60},{8,16},{12,4},{16,24},{20,12},{24,32},{28,20},{32,40}... | collective-permute-start | bytes 442376 | tf_op jit(solution)/shard_map/ppermute | solution.py:217
  24.2 6.3 %collective-permute-start.14 = (f32[288,128]{1,0:T(8,128)S(1)}, f32[288,128]{1,0:T(8,128)S(1)}, u32[]{:S(2)}, u32[]{:S(2)}) collective-permute-start(f32[288,128]{1,0:T(8,128)S(1)} %add.43), channel_id=1, source_target_pairs={{0,8},{4,60},{8,16},{12,4},{16,24},{20,12},{24,32},{28,20},{32,40}... | collective-permute-start | bytes 442376 | tf_op jit(solution)/shard_map/ppermute | solution.py:217
  25.7 6.3 %collective-permute-start.4 = (f32[288,128]{1,0:T(8,128)S(1)}, f32[288,128]{1,0:T(8,128)S(1)}, u32[]{:S(2)}, u32[]{:S(2)}) collective-permute-start(f32[288,128]{1,0:T(8,128)S(1)} %add.33), channel_id=1, source_target_pairs={{0,8},{4,60},{8,16},{12,4},{16,24},{20,12},{24,32},{28,20},{32,40}... | collective-permute-start | bytes 442376 | tf_op jit(solution)/shard_map/ppermute | solution.py:217
  27.3 6.5 %collective-permute-start.8 = (f32[288,128]{1,0:T(8,128)S(1)}, f32[288,128]{1,0:T(8,128)S(1)}, u32[]{:S(2)}, u32[]{:S(2)}) collective-permute-start(f32[288,128]{1,0:T(8,128)S(1)} %add.37), channel_id=1, source_target_pairs={{0,8},{4,60},{8,16},{12,4},{16,24},{20,12},{24,32},{28,20},{32,40}... | collective-permute-start | bytes 442376 | tf_op jit(solution)/shard_map/ppermute | solution.py:217
  28.9 6.3 %collective-permute-start.12 = (f32[288,128]{1,0:T(8,128)S(1)}, f32[288,128]{1,0:T(8,128)S(1)}, u32[]{:S(2)}, u32[]{:S(2)}) collective-permute-start(f32[288,128]{1,0:T(8,128)S(1)} %add.41), channel_id=1, source_target_pairs={{0,8},{4,60},{8,16},{12,4},{16,24},{20,12},{24,32},{28,20},{32,40}... | collective-permute-start | bytes 442376 | tf_op jit(solution)/shard_map/ppermute | solution.py:217
  30.5 5.5 %collective-permute-start.15 = (f32[288,128]{1,0:T(8,128)S(1)}, f32[288,128]{1,0:T(8,128)S(1)}, u32[]{:S(2)}, u32[]{:S(2)}) collective-permute-start(f32[288,128]{1,0:T(8,128)S(1)} %add.44), channel_id=1, source_target_pairs={{0,8},{4,60},{8,16},{12,4},{16,24},{20,12},{24,32},{28,20},{32,40}... | collective-permute-start | bytes 442376 | tf_op jit(solution)/shard_map/ppermute | solution.py:217
  32.1 5.4 %collective-permute-start.5 = (f32[288,128]{1,0:T(8,128)S(1)}, f32[288,128]{1,0:T(8,128)S(1)}, u32[]{:S(2)}, u32[]{:S(2)}) collective-permute-start(f32[288,128]{1,0:T(8,128)S(1)} %add.34), channel_id=1, source_target_pairs={{0,8},{4,60},{8,16},{12,4},{16,24},{20,12},{24,32},{28,20},{32,40}... | collective-permute-start | bytes 442376 | tf_op jit(solution)/shard_map/ppermute | solution.py:217
  33.8 12.1 %copy-start.2 = (bf16[1,4608]{1,0:T(2,128)(2,1)S(1)}, bf16[1,4608]{1,0:T(2,128)(2,1)}, u32[]{:S(2)}) copy-start(bf16[1,4608]{1,0:T(2,128)(2,1)} %param.7) | copy-start | bytes 27652
  33.8 16.8 %copy-start.1 = (s32[64]{0:T(128)S(1)}, s32[64]{0:T(128)}, u32[]{:S(2)}) copy-start(s32[64]{0:T(128)} %bucket.3) | copy-start | bytes 772
  33.8 5.4 %collective-permute-start.9 = (f32[288,128]{1,0:T(8,128)S(1)}, f32[288,128]{1,0:T(8,128)S(1)}, u32[]{:S(2)}, u32[]{:S(2)}) collective-permute-start(f32[288,128]{1,0:T(8,128)S(1)} %add.38), channel_id=1, source_target_pairs={{0,8},{4,60},{8,16},{12,4},{16,24},{20,12},{24,32},{28,20},{32,40}... | collective-permute-start | bytes 442376 | tf_op jit(solution)/shard_map/ppermute | solution.py:217
  35.2 5.6 %collective-permute-start.18 = (f32[288,128]{1,0:T(8,128)S(1)}, f32[288,128]{1,0:T(8,128)S(1)}, u32[]{:S(2)}, u32[]{:S(2)}) collective-permute-start(f32[288,128]{1,0:T(8,128)S(1)} %collective-permute-done.12.r2), channel_id=1, source_target_pairs={{0,4},{4,0},{1,5},{5,1},{2,6},{6,2},{3,7},{7,3},{8,12},{12,8},{9,1... | collective-permute-start | bytes 442376 | tf_op jit(solution)/shard_map/ppermute | solution.py:219
  36.0 4.9 %collective-permute-start.19 = (f32[288,128]{1,0:T(8,128)S(1)}, f32[288,128]{1,0:T(8,128)S(1)}, u32[]{:S(2)}, u32[]{:S(2)}) collective-permute-start(f32[288,128]{1,0:T(8,128)S(1)} %collective-permute-done.15.r3), channel_id=1, source_target_pairs={{0,4},{4,0},{1,5},{5,1},{2,6},{6,2},{3,7},{7,3},{8,12},{12,8},{9,1... | collective-permute-start | bytes 442376 | tf_op jit(solution)/shard_map/ppermute | solution.py:219
  37.4 3.4 %collective-permute-start.16 = (f32[288,128]{1,0:T(8,128)S(1)}, f32[288,128]{1,0:T(8,128)S(1)}, u32[]{:S(2)}, u32[]{:S(2)}) collective-permute-start(f32[288,128]{1,0:T(8,128)S(1)} %collective-permute-done.5.r0), channel_id=1, source_target_pairs={{0,4},{4,0},{1,5},{5,1},{2,6},{6,2},{3,7},{7,3},{8,12},{12,8},{9,1... | collective-permute-start | bytes 442376 | tf_op jit(solution)/shard_map/ppermute | solution.py:219
  39.2 2.6 %collective-permute-start.17 = (f32[288,128]{1,0:T(8,128)S(1)}, f32[288,128]{1,0:T(8,128)S(1)}, u32[]{:S(2)}, u32[]{:S(2)}) collective-permute-start(f32[288,128]{1,0:T(8,128)S(1)} %collective-permute-done.9.r1), channel_id=1, source_target_pairs={{0,4},{4,0},{1,5},{5,1},{2,6},{6,2},{3,7},{7,3},{8,12},{12,8},{9,1... | collective-permute-start | bytes 442376 | tf_op jit(solution)/shard_map/ppermute | solution.py:219
  41.9 4.0 %collective-permute-start.20 = (f32[144,128]{1,0:T(8,128)S(1)}, f32[144,128]{1,0:T(8,128)S(1)}, u32[]{:S(2)}, u32[]{:S(2)}) collective-permute-start(f32[144,128]{1,0:T(8,128)S(1)} %get-tuple-element.21), channel_id=1, source_target_pairs={{0,64},{64,0},{128,192},{192,128},{1,65},{65,1},{129,193},{193,129... | collective-permute-start | bytes 221192 | tf_op jit(solution)/shard_map/ppermute | solution.py:232
  43.2 5.7 %collective-permute-start.21 = (f32[144,128]{1,0:T(8,128)S(1)}, f32[144,128]{1,0:T(8,128)S(1)}, u32[]{:S(2)}, u32[]{:S(2)}) collective-permute-start(f32[144,128]{1,0:T(8,128)S(1)} %get-tuple-element.22), channel_id=1, source_target_pairs={{0,128},{64,192},{128,0},{192,64},{1,129},{65,193},{129,1},{193,65... | collective-permute-start | bytes 221192 | tf_op jit(solution)/shard_map/ppermute | solution.py:232
  45.7 4.9 %collective-permute-start.22 = (f32[144,128]{1,0:T(8,128)S(1)}, f32[144,128]{1,0:T(8,128)S(1)}, u32[]{:S(2)}, u32[]{:S(2)}) collective-permute-start(f32[144,128]{1,0:T(8,128)S(1)} %get-tuple-element.23), channel_id=1, source_target_pairs={{0,192},{64,128},{128,64},{192,0},{1,193},{65,129},{129,65},{193,1... | collective-permute-start | bytes 221192 | tf_op jit(solution)/shard_map/ppermute | solution.py:232
  51.3 2.4 %collective-permute-start.23 = (f32[1,128]{1,0:T(1,128)S(1)}, f32[1,128]{1,0:T(1,128)S(1)}, u32[]{:S(2)}, u32[]{:S(2)}) collective-permute-start(f32[1,128]{1,0:T(1,128)S(1)} %get-tuple-element.25), channel_id=1, source_target_pairs={{0,4},{4,0},{1,5},{5,1},{2,6},{6,2},{3,7},{7,3},{8,12},{12,8},{9,1... | collective-permute-start | bytes 1544 | tf_op jit(solution)/shard_map/ppermute | solution.py:244

commit v5 on v4

--- a/solution.py
+++ b/solution.py
@@ -18,7 +18,7 @@
 PIECES = tuple(
     (hops - (rel >= 2), rel) for hops in (4, 3, 2, 1) for rel in range(STEPS) if hops - (rel >= 2) > 0
 )
-EARLY = PIECES[:STEPS]
+FIRST, SECOND = PIECES[:2], PIECES[2:STEPS]
 
 
 def room(mib):
@@ -26,11 +26,11 @@
 
 
 def where_rows(tiles):
-    base, sizes = {}, [0, 0]
+    base, sizes = {}, [0, 0, 0]
     for piece in PIECES + tuple((0, rel) for rel in range(STEPS)):
-        late = int(piece not in EARLY)
-        base[piece] = (late, sizes[late])
-        sizes[late] += (8 if piece[0] else 4) * tiles
+        kind = 0 if piece in FIRST else 1 if piece in SECOND else 2
+        base[piece] = (kind, sizes[kind])
+        sizes[kind] += (8 if piece[0] else 4) * tiles
     return base, sizes
 
 
@@ -39,13 +39,11 @@
     return first + [k for k in range(8) if k not in first]
 
 
-def picks_kernel(place, table, picks):
+def rows_kernel(place, rows):
     x, z, c = place[0], place[1], place[2]
     shape = (ROWS, ROWS)
     group = lax.broadcasted_iota(jnp.int32, shape, 0) // 8
     g = lax.broadcasted_iota(jnp.int32, shape, 0) % 8
-    lane = lax.broadcasted_iota(jnp.int32, shape, 1)
-    arrival, bucket = table[STEPS : STEPS + 1, 0:ROWS], table[STEPS + 1 : STEPS + 2, 0:ROWS]
     to_x = x ^ (g % 4)
     for rel in range(STEPS):
         k = jnp.zeros(shape, jnp.int32)
@@ -53,7 +51,15 @@
             k = jnp.where(group == index, value, k)
         to_z = (z + k * (1 - 2 * c)) & 7
         owner = jnp.where(k <= (4 if rel < 2 else 3), c, 1 - c)
-        ids = (to_x * 8 + to_z) * 2 + (owner ^ (g // 4))
+        rows[rel] = (to_x * 8 + to_z) * 2 + (owner ^ (g // 4))
+
+
+def picks_kernel(place, rows, table, picks):
+    c = place[2]
+    lane = lax.broadcasted_iota(jnp.int32, (ROWS, ROWS), 1)
+    arrival, bucket = table[STEPS : STEPS + 1, 0:ROWS], table[STEPS + 1 : STEPS + 2, 0:ROWS]
+    for rel in range(STEPS):
+        ids = rows[rel]
         row_bucket = jnp.sum(jnp.where(ids == lane, bucket, 0), axis=1, keepdims=True)
         exponents = jnp.where(c == 0, table[rel ^ 2, 0:ROWS][None], table[rel, 0:ROWS][None])
         power = jnp.sum(jnp.where(row_bucket == lane, exponents, 0), axis=1, keepdims=True)
@@ -63,15 +69,18 @@
         picks[rel] = jnp.where(ids == arrival, factor, 0.0).astype(jnp.bfloat16)
 
 
-def spread_kernel(tiles, late, place, picks, codes, mine, send):
+def spread_kernel(tiles, late, place, picks, codes, *outs):
     base, _ = where_rows(tiles)
     c = place[2]
     width = 2 * LANES
     rows = slice(16, ROWS) if late else slice(0, 16)
 
-    def put(out, piece, at, value):
-        assert base[piece][0] == late
-        out[pl.ds(base[piece][1] + at, value.shape[0], tiles), :] = value
+    kinds = (2,) if late else (0, 1)
+    mine, send = dict(zip(kinds, outs[: len(kinds)])), dict(zip(kinds, outs[len(kinds) :]))
+
+    def put(arrays, piece, at, value):
+        kind, first = base[piece]
+        arrays[kind][pl.ds(first + at, value.shape[0], tiles), :] = value
 
     for rel in range(STEPS):
         order = group_order(rel)[2:] if late else group_order(rel)[:2]
@@ -98,13 +107,16 @@
 
 def spread(late, place, picks, codes):
     tiles = codes.shape[2] // LANES
-    shape = jax.ShapeDtypeStruct((where_rows(tiles)[1][late], LANES), jnp.float32)
+    sizes = where_rows(tiles)[1]
+    shapes = tuple(
+        jax.ShapeDtypeStruct((size, LANES), jnp.float32) for size in (sizes[2:] if late else sizes[:2])
+    )
     vmem = pl.BlockSpec(memory_space=pltpu.VMEM)
     return pl.pallas_call(
         functools.partial(spread_kernel, tiles, late),
-        out_shape=(shape, shape),
+        out_shape=shapes + shapes,
         in_specs=[pl.BlockSpec(memory_space=pltpu.SMEM), vmem, vmem],
-        out_specs=(vmem, vmem),
+        out_specs=(vmem,) * (2 * len(shapes)),
         compiler_params=room(8),
         name="spread",
     )(place, picks, codes)
@@ -181,22 +193,31 @@
         return jnp.pad(rows, ((0, 0), (0, LANES - rows.shape[1])))
 
     words = jnp.concatenate([wide(exponents[:, 0]), wide(arrival[None]), wide(bucket_of_row[None])])
+    rows = pl.pallas_call(
+        rows_kernel,
+        out_shape=jax.ShapeDtypeStruct((STEPS, ROWS, ROWS), jnp.int32),
+        in_specs=[smem],
+        out_specs=vmem,
+        compiler_params=room(4),
+        cost_estimate=pl.CostEstimate(flops=3 * 10**9, bytes_accessed=10**5, transcendentals=0),
+        name="rows",
+    )(place)
     picks = pl.pallas_call(
         picks_kernel,
         out_shape=jax.ShapeDtypeStruct((STEPS, ROWS, ROWS), jnp.bfloat16),
-        in_specs=[smem, vmem],
+        in_specs=[smem, vmem, vmem],
         out_specs=vmem,
         compiler_params=room(4),
-        cost_estimate=pl.CostEstimate(flops=3 * 10**9, bytes_accessed=10**5, transcendentals=0),
         name="picks",
-    )(place, words)
+    )(place, rows, words)
 
     swap = [(0, 1), (1, 0)]
-    mine0, send0 = spread(0, place, picks, codes)
+    mine0, mine1, send0, send1 = spread(0, place, picks, codes)
     got0 = lax.ppermute(send0, "c", swap)
-    mine1, send1 = spread(1, place, picks, codes)
     got1 = lax.ppermute(send1, "c", swap)
-    mine, got = (mine0, mine1), (got0, got1)
+    mine2, send2 = spread(1, place, picks, codes)
+    got2 = lax.ppermute(send2, "c", swap)
+    mine, got = (mine0, mine1, mine2), (got0, got1, got2)
     turn = []
     for z in range(nz):
         turn.append((2 * z, 2 * ((z + 1) % nz)))
@@ -226,7 +247,7 @@
         out_specs=(vmem,) * 4,
         compiler_params=room(4),
         name="join",
-    )(mine1, got1, *ring, *back)
+    )(mine2, got2, *ring, *back)
     totals = [pieces[0]]
     for k in range(1, 4):
         totals.append(lax.ppermute(pieces[k], "x", [(i, i ^ k) for i in range(4)]))
@@ -266,6 +287,4 @@
     in_specs = (P(None, dp, None, "y"), P(None, dp, None), P(dp, "y"), P(), P())
     out_specs = (P(None, dp, "y"), P(), P(dp, "y"))
 
-    return jax.shard_map(
-        on_device, mesh=finer, in_specs=in_specs, out_specs=out_specs, check_vma=False
-    )
+    return jax.shard_map(on_device, mesh=finer, in_specs=in_specs, out_specs=out_specs, check_vma=False)

time: 76.1 us -> 74.9 us (0.984)
  waiting for transfers between devices: 9.68 us -> 8.68 us
    ppermute x0 -> x1, starting transfers between devices: none -> 3.28 us  [on_device(): got2 = lax.ppermute(send2, 'c', swap)]
    ppermute x1, starting transfers between devices: 3.29 us -> 0.49 us  [on_device(): got1 = lax.ppermute(send1, 'c', swap)]
    ppermute x1, waiting for transfers between devices: 3.1 us -> 2.18 us  [on_device(): got0 = lax.ppermute(send0, 'c', swap)]
    pallas_call x2 -> x3, Pallas kernels: 2.11 us -> 2.68 us  [the longest x2 2.11 us: spread(): pl.pallas_call(functools.partial(spread_kernel, tiles, late), out_shape=s...]
  transfers between devices with their start and end apart: 24 -> 25, of which waited for: 6 -> 5; matrix products, arithmetic and copies ran while one was open for 0% -> 0% of each run, Pallas kernels for 2% -> 2%
where the time goes in v5:
time: 74.9 us; the launch traced here: 74.7 us
  starting transfers between devices  38.1 us (51%)
  blocking collectives  20.8 us (28%)
  waiting for transfers between devices  8.68 us (12%)
  Pallas kernels  5.92 us (8%)
  between operations  0.77 us (1%)
    ppermute x14, starting transfers between devices, on_device(): ring[rel] = (lax.ppermute(held, ('z', 'c'), turn),)  23.1 us
    all_to_all x1, blocking collectives, on_device(): tables = lax.all_to_all(copies, ('x', 'z', 'y'), 0, 0, tiled=True)  20.8 us
    ppermute x4, starting transfers between devices, on_device(): back = [lax.ppermute(arrived, 'c', swap) for arrived in ring]  5.61 us
    ppermute x3, waiting for transfers between devices, on_device(): totals.append(lax.ppermute(pieces[k], 'x', [(i, i ^ k) for i in range(4)]))  4.63 us
    ppermute x3, starting transfers between devices, on_device(): totals.append(lax.ppermute(pieces[k], 'x', [(i, i ^ k) for i in range(4)]))  3.94 us
    ppermute x1, starting transfers between devices, on_device(): got2 = lax.ppermute(send2, 'c', swap)  3.28 us
    ppermute x1, waiting for transfers between devices, on_device(): got0 = lax.ppermute(send0, 'c', swap)  2.18 us
    pallas_call x2, Pallas kernels, spread(): pl.pallas_call(functools.partial(spread_kernel, tiles, late), out_shape=s...  2.11 us
  transfers between devices with their start and end apart: 25, of which 5 were waited for; matrix products, arithmetic and copies ran while one was open for 0% of the time, Pallas kernels for 2%

profile of v5, /device:TPU:1, one launch (start us, length us, event | category | flops | bytes accessed | tf_op | source)
XLA Modules:
  0.0 74.7 jit_solution(18342712217268928857)
XLA Ops:
  1.4 0.9 %picks.1 = bf16[4,64,64]{2,1,0:T(8,128)(2,1)S(1)} custom-call(s32[3]{0:T(128)S(1)} %pad_add_fusion.2.place, s32[4,64,64]{2,1,0:T(8,128)S(1)} %rows.1, s32[6,128]{1,0:T(8,128)S(1)} %pad_add_fusion.table), custom_call_target="tpu_custom_call" | custom-call | tf_op jit(solution)/shard_map/picks/pallas_call | solution.py:205
  2.4 1.1 %spread.2 = (f32[3456,128]{1,0:T(8,128)S(1)}, f32[3456,128]{1,0:T(8,128)S(1)}) custom-call(s32[3]{0:T(128)S(1)} %pad_add_fusion.2.place, bf16[4,64,64]{2,1,0:T(8,128)(2,1)S(1)} %picks.1, bf16[4,64,4608]{2,1,0:T(8,128)(2,1)S(1)} %bitcast.12), custom_call_target="tpu_custom_call" | custom-call | tf_op jit(solution)/shard_map/spread/pallas_call | solution.py:115
  3.6 3.3 %collective-permute-start = (f32[3456,128]{1,0:T(8,128)S(1)}, f32[3456,128]{1,0:T(8,128)S(1)}, u32[]{:S(2)}, u32[]{:S(2)}) collective-permute-start(f32[3456,128]{1,0:T(8,128)S(1)} %get-tuple-element.19), channel_id=1, source_target_pairs={{0,4},{4,0},{1,5},{5,1},{2,6},{6,2},{3,7},{7,3},{8,12},{12,8},{9,1... | collective-permute-start | bytes 5308424 | tf_op jit(solution)/shard_map/ppermute | solution.py:219
  6.9 1.0 %spread.3 = (f32[576,128]{1,0:T(8,128)S(1)}, f32[576,128]{1,0:T(8,128)S(1)}, f32[576,128]{1,0:T(8,128)S(1)}, f32[576,128]{1,0:T(8,128)S(1)}) custom-call(s32[3]{0:T(128)S(1)} %pad_add_fusion.2.place, bf16[4,64,64]{2,1,0:T(8,128)(2,1)S(1)} %picks.1, bf16[4,64,4608]{2,1,0:T(8,128)(2,1)S(1)} %bitcast.13), custom_call_target="tpu_custom_call" | custom-call | tf_op jit(solution)/shard_map/spread/pallas_call | solution.py:115
  8.4 2.2 %collective-permute-done.1.refs_1_ = f32[576,128]{1,0:T(8,128)S(1)} collective-permute-done((f32[576,128]{1,0:T(8,128)S(1)}, f32[576,128]{1,0:T(8,128)S(1)}, u32[]{:S(2)}, u32[]{:S(2)}) %collective-permute-start.1) | collective-permute-done | bytes 294944 | tf_op jit(solution)/shard_map/ppermute | solution.py:216
  10.6 4.0 %collective-permute-start.2 = (f32[288,128]{1,0:T(8,128)S(1)}, f32[288,128]{1,0:T(8,128)S(1)}, u32[]{:S(2)}, u32[]{:S(2)}) collective-permute-start(f32[288,128]{1,0:T(8,128)S(1)} %add.31), channel_id=1, source_target_pairs={{0,8},{4,60},{8,16},{12,4},{16,24},{20,12},{24,32},{28,20},{32,40}... | collective-permute-start | bytes 442376 | tf_op jit(solution)/shard_map/ppermute | solution.py:238
  14.6 0.8 %collective-permute-start.6 = (f32[288,128]{1,0:T(8,128)S(1)}, f32[288,128]{1,0:T(8,128)S(1)}, u32[]{:S(2)}, u32[]{:S(2)}) collective-permute-start(f32[288,128]{1,0:T(8,128)S(1)} %add.35), channel_id=1, source_target_pairs={{0,8},{4,60},{8,16},{12,4},{16,24},{20,12},{24,32},{28,20},{32,40}... | collective-permute-start | bytes 442376 | tf_op jit(solution)/shard_map/ppermute | solution.py:238
  15.4 0.8 %collective-permute-start.11 = (f32[288,128]{1,0:T(8,128)S(1)}, f32[288,128]{1,0:T(8,128)S(1)}, u32[]{:S(2)}, u32[]{:S(2)}) collective-permute-start(f32[288,128]{1,0:T(8,128)S(1)} %add.39), channel_id=1, source_target_pairs={{0,8},{4,60},{8,16},{12,4},{16,24},{20,12},{24,32},{28,20},{32,40}... | collective-permute-start | bytes 442376 | tf_op jit(solution)/shard_map/ppermute | solution.py:238
  16.2 0.8 %collective-permute-start.14 = (f32[288,128]{1,0:T(8,128)S(1)}, f32[288,128]{1,0:T(8,128)S(1)}, u32[]{:S(2)}, u32[]{:S(2)}) collective-permute-start(f32[288,128]{1,0:T(8,128)S(1)} %add.42), channel_id=1, source_target_pairs={{0,8},{4,60},{8,16},{12,4},{16,24},{20,12},{24,32},{28,20},{32,40}... | collective-permute-start | bytes 442376 | tf_op jit(solution)/shard_map/ppermute | solution.py:238
  17.1 2.8 %collective-permute-start.3 = (f32[288,128]{1,0:T(8,128)S(1)}, f32[288,128]{1,0:T(8,128)S(1)}, u32[]{:S(2)}, u32[]{:S(2)}) collective-permute-start(f32[288,128]{1,0:T(8,128)S(1)} %add.32), channel_id=1, source_target_pairs={{0,8},{4,60},{8,16},{12,4},{16,24},{20,12},{24,32},{28,20},{32,40}... | collective-permute-start | bytes 442376 | tf_op jit(solution)/shard_map/ppermute | solution.py:238
  19.9 1.5 %collective-permute-start.7 = (f32[288,128]{1,0:T(8,128)S(1)}, f32[288,128]{1,0:T(8,128)S(1)}, u32[]{:S(2)}, u32[]{:S(2)}) collective-permute-start(f32[288,128]{1,0:T(8,128)S(1)} %add.36), channel_id=1, source_target_pairs={{0,8},{4,60},{8,16},{12,4},{16,24},{20,12},{24,32},{28,20},{32,40}... | collective-permute-start | bytes 442376 | tf_op jit(solution)/shard_map/ppermute | solution.py:238
  21.5 1.5 %collective-permute-start.12 = (f32[288,128]{1,0:T(8,128)S(1)}, f32[288,128]{1,0:T(8,128)S(1)}, u32[]{:S(2)}, u32[]{:S(2)}) collective-permute-start(f32[288,128]{1,0:T(8,128)S(1)} %add.40), channel_id=1, source_target_pairs={{0,8},{4,60},{8,16},{12,4},{16,24},{20,12},{24,32},{28,20},{32,40}... | collective-permute-start | bytes 442376 | tf_op jit(solution)/shard_map/ppermute | solution.py:238
  23.1 1.5 %collective-permute-start.15 = (f32[288,128]{1,0:T(8,128)S(1)}, f32[288,128]{1,0:T(8,128)S(1)}, u32[]{:S(2)}, u32[]{:S(2)}) collective-permute-start(f32[288,128]{1,0:T(8,128)S(1)} %add.43), channel_id=1, source_target_pairs={{0,8},{4,60},{8,16},{12,4},{16,24},{20,12},{24,32},{28,20},{32,40}... | collective-permute-start | bytes 442376 | tf_op jit(solution)/shard_map/ppermute | solution.py:238
  24.6 1.5 %collective-permute-start.4 = (f32[288,128]{1,0:T(8,128)S(1)}, f32[288,128]{1,0:T(8,128)S(1)}, u32[]{:S(2)}, u32[]{:S(2)}) collective-permute-start(f32[288,128]{1,0:T(8,128)S(1)} %add.33), channel_id=1, source_target_pairs={{0,8},{4,60},{8,16},{12,4},{16,24},{20,12},{24,32},{28,20},{32,40}... | collective-permute-start | bytes 442376 | tf_op jit(solution)/shard_map/ppermute | solution.py:238
  26.2 1.5 %collective-permute-start.8 = (f32[288,128]{1,0:T(8,128)S(1)}, f32[288,128]{1,0:T(8,128)S(1)}, u32[]{:S(2)}, u32[]{:S(2)}) collective-permute-start(f32[288,128]{1,0:T(8,128)S(1)} %add.37), channel_id=1, source_target_pairs={{0,8},{4,60},{8,16},{12,4},{16,24},{20,12},{24,32},{28,20},{32,40}... | collective-permute-start | bytes 442376 | tf_op jit(solution)/shard_map/ppermute | solution.py:238
  27.8 1.5 %collective-permute-start.13 = (f32[288,128]{1,0:T(8,128)S(1)}, f32[288,128]{1,0:T(8,128)S(1)}, u32[]{:S(2)}, u32[]{:S(2)}) collective-permute-start(f32[288,128]{1,0:T(8,128)S(1)} %add.41), channel_id=1, source_target_pairs={{0,8},{4,60},{8,16},{12,4},{16,24},{20,12},{24,32},{28,20},{32,40}... | collective-permute-start | bytes 442376 | tf_op jit(solution)/shard_map/ppermute | solution.py:238
  29.4 1.7 %collective-permute-start.16 = (f32[288,128]{1,0:T(8,128)S(1)}, f32[288,128]{1,0:T(8,128)S(1)}, u32[]{:S(2)}, u32[]{:S(2)}) collective-permute-start(f32[288,128]{1,0:T(8,128)S(1)} %add.44), channel_id=1, source_target_pairs={{0,8},{4,60},{8,16},{12,4},{16,24},{20,12},{24,32},{28,20},{32,40}... | collective-permute-start | bytes 442376 | tf_op jit(solution)/shard_map/ppermute | solution.py:238
  31.1 1.4 %collective-permute-start.5 = (f32[288,128]{1,0:T(8,128)S(1)}, f32[288,128]{1,0:T(8,128)S(1)}, u32[]{:S(2)}, u32[]{:S(2)}) collective-permute-start(f32[288,128]{1,0:T(8,128)S(1)} %add.34), channel_id=1, source_target_pairs={{0,8},{4,60},{8,16},{12,4},{16,24},{20,12},{24,32},{28,20},{32,40}... | collective-permute-start | bytes 442376 | tf_op jit(solution)/shard_map/ppermute | solution.py:238
  32.6 1.5 %collective-permute-start.9 = (f32[288,128]{1,0:T(8,128)S(1)}, f32[288,128]{1,0:T(8,128)S(1)}, u32[]{:S(2)}, u32[]{:S(2)}) collective-permute-start(f32[288,128]{1,0:T(8,128)S(1)} %add.38), channel_id=1, source_target_pairs={{0,8},{4,60},{8,16},{12,4},{16,24},{20,12},{24,32},{28,20},{32,40}... | collective-permute-start | bytes 442376 | tf_op jit(solution)/shard_map/ppermute | solution.py:238
  34.1 0.7 collective-permute-start.19
  34.9 1.6 %collective-permute-start.20 = (f32[288,128]{1,0:T(8,128)S(1)}, f32[288,128]{1,0:T(8,128)S(1)}, u32[]{:S(2)}, u32[]{:S(2)}) collective-permute-start(f32[288,128]{1,0:T(8,128)S(1)} %collective-permute-done.16.r3), channel_id=1, source_target_pairs={{0,4},{4,0},{1,5},{5,1},{2,6},{6,2},{3,7},{7,3},{8,12},{12,8},{9,1... | collective-permute-start | bytes 442376 | tf_op jit(solution)/shard_map/ppermute | solution.py:240
  36.4 1.7 %collective-permute-start.17 = (f32[288,128]{1,0:T(8,128)S(1)}, f32[288,128]{1,0:T(8,128)S(1)}, u32[]{:S(2)}, u32[]{:S(2)}) collective-permute-start(f32[288,128]{1,0:T(8,128)S(1)} %collective-permute-done.5.r0), channel_id=1, source_target_pairs={{0,4},{4,0},{1,5},{5,1},{2,6},{6,2},{3,7},{7,3},{8,12},{12,8},{9,1... | collective-permute-start | bytes 442376 | tf_op jit(solution)/shard_map/ppermute | solution.py:240
  38.1 1.6 %collective-permute-start.18 = (f32[288,128]{1,0:T(8,128)S(1)}, f32[288,128]{1,0:T(8,128)S(1)}, u32[]{:S(2)}, u32[]{:S(2)}) collective-permute-start(f32[288,128]{1,0:T(8,128)S(1)} %collective-permute-done.9.r1), channel_id=1, source_target_pairs={{0,4},{4,0},{1,5},{5,1},{2,6},{6,2},{3,7},{7,3},{8,12},{12,8},{9,1... | collective-permute-start | bytes 442376 | tf_op jit(solution)/shard_map/ppermute | solution.py:240
  39.7 1.0 %collective-permute-done.18.b1 = f32[288,128]{1,0:T(8,128)S(1)} collective-permute-done((f32[288,128]{1,0:T(8,128)S(1)}, f32[288,128]{1,0:T(8,128)S(1)}, u32[]{:S(2)}, u32[]{:S(2)}) %collective-permute-start.18) | collective-permute-done | bytes 147488 | tf_op jit(solution)/shard_map/ppermute | solution.py:240
  40.8 1.3 %collective-permute-start.21 = (f32[144,128]{1,0:T(8,128)S(1)}, f32[144,128]{1,0:T(8,128)S(1)}, u32[]{:S(2)}, u32[]{:S(2)}) collective-permute-start(f32[144,128]{1,0:T(8,128)S(1)} %get-tuple-element.25), channel_id=1, source_target_pairs={{0,64},{64,0},{128,192},{192,128},{1,65},{65,1},{129,193},{193,129... | collective-permute-start | bytes 221192 | tf_op jit(solution)/shard_map/ppermute | solution.py:253
  42.1 2.5 %collective-permute-start.22 = (f32[144,128]{1,0:T(8,128)S(1)}, f32[144,128]{1,0:T(8,128)S(1)}, u32[]{:S(2)}, u32[]{:S(2)}) collective-permute-start(f32[144,128]{1,0:T(8,128)S(1)} %get-tuple-element.26), channel_id=1, source_target_pairs={{0,128},{64,192},{128,0},{192,64},{1,129},{65,193},{129,1},{193,65... | collective-permute-start | bytes 221192 | tf_op jit(solution)/shard_map/ppermute | solution.py:253
  44.8 3.0 %collective-permute-done.22.t2 = f32[144,128]{1,0:T(8,128)S(1)} collective-permute-done((f32[144,128]{1,0:T(8,128)S(1)}, f32[144,128]{1,0:T(8,128)S(1)}, u32[]{:S(2)}, u32[]{:S(2)}) %collective-permute-start.22) | collective-permute-done | bytes 73760 | tf_op jit(solution)/shard_map/ppermute | solution.py:253
  47.9 1.6 %collective-permute-done.23.t3 = f32[144,128]{1,0:T(8,128)S(1)} collective-permute-done((f32[144,128]{1,0:T(8,128)S(1)}, f32[144,128]{1,0:T(8,128)S(1)}, u32[]{:S(2)}, u32[]{:S(2)}) %collective-permute-start.23) | collective-permute-done | bytes 73760 | tf_op jit(solution)/shard_map/ppermute | solution.py:253
  50.2 1.6 %collective-permute-start.24 = (f32[1,128]{1,0:T(1,128)S(1)}, f32[1,128]{1,0:T(1,128)S(1)}, u32[]{:S(2)}, u32[]{:S(2)}) collective-permute-start(f32[1,128]{1,0:T(1,128)S(1)} %get-tuple-element.29), channel_id=1, source_target_pairs={{0,4},{4,0},{1,5},{5,1},{2,6},{6,2},{3,7},{7,3},{8,12},{12,8},{9,1... | collective-permute-start | bytes 1544 | tf_op jit(solution)/shard_map/ppermute | solution.py:265
  51.8 0.8 %collective-permute-done.24 = f32[1,128]{1,0:T(1,128)S(1)} collective-permute-done((f32[1,128]{1,0:T(1,128)S(1)}, f32[1,128]{1,0:T(1,128)S(1)}, u32[]{:S(2)}, u32[]{:S(2)}) %collective-permute-start.24) | collective-permute-done | bytes 544 | tf_op jit(solution)/shard_map/ppermute | solution.py:265
  52.7 20.8 %all_to_all.5 = f32[128,1,128]{2,1,0:T(1,128)S(1)} all-to-all(f32[128,1,128]{2,1,0:T(1,128)S(1)} %broadcast_in_dim.20), channel_id=1, replica_groups=mesh['x'=4,'z'=8,'c'=2,'y'=4] {'x','z','y'}, dimensions={0} | all-to-all | bytes 131072 | tf_op jit(solution)/shard_map/all_to_all | solution.py:268
  73.4 1.3 %scale.1 = (bf16[4,4608]{1,0:T(4,128)(2,1)}, f32[4,16]{1,0:T(4,128)}, f32[1,4608]{1,0:T(1,128)}) custom-call(s32[3]{0:T(128)S(1)} %pad_add_fusion.2.place, s32[64]{0:T(128)S(1)} %copy-done.1, f32[4,4608]{1,0:T(4,128)S(1)} %get-tuple-element.28.exact, f32[128,128]{1,0:T(8,128)S(1)} %bitcast.14), custom_call_target="tpu_custom_call" | custom-call | tf_op jit(solution)/shard_map/scale/pallas_call | solution.py:269
  (55 shorter events, 2.9 us)
Async XLA Ops:
  0.7 0.7 copy-start.1
  0.7 0.7 copy-start.3
  0.7 0.7 copy-start.4
  0.7 1.7 %copy-start = (bf16[4,1,64,4608]{3,2,1,0:T(8,128)(2,1)S(1)}, bf16[4,1,64,4608]{3,2,1,0:T(8,128)(2,1)}, u32[]{:S(2)}) copy-start(bf16[4,1,64,4608]{3,2,1,0:T(8,128)(2,1)} %param.5) | copy-start | bytes 7077892
  3.6 13.5 %collective-permute-start = (f32[3456,128]{1,0:T(8,128)S(1)}, f32[3456,128]{1,0:T(8,128)S(1)}, u32[]{:S(2)}, u32[]{:S(2)}) collective-permute-start(f32[3456,128]{1,0:T(8,128)S(1)} %get-tuple-element.19), channel_id=1, source_target_pairs={{0,4},{4,0},{1,5},{5,1},{2,6},{6,2},{3,7},{7,3},{8,12},{12,8},{9,1... | collective-permute-start | bytes 5308424 | tf_op jit(solution)/shard_map/ppermute | solution.py:219
  7.8 2.8 %collective-permute-start.1 = (f32[576,128]{1,0:T(8,128)S(1)}, f32[576,128]{1,0:T(8,128)S(1)}, u32[]{:S(2)}, u32[]{:S(2)}) collective-permute-start(f32[576,128]{1,0:T(8,128)S(1)} %get-tuple-element.21), channel_id=1, source_target_pairs={{0,4},{4,0},{1,5},{5,1},{2,6},{6,2},{3,7},{7,3},{8,12},{12,8},{9,1... | collective-permute-start | bytes 884744 | tf_op jit(solution)/shard_map/ppermute | solution.py:216
  7.9 7.5 %collective-permute-start.10 = (f32[576,128]{1,0:T(8,128)S(1)}, f32[576,128]{1,0:T(8,128)S(1)}, u32[]{:S(2)}, u32[]{:S(2)}) collective-permute-start(f32[576,128]{1,0:T(8,128)S(1)} %get-tuple-element.23), channel_id=1, source_target_pairs={{0,4},{4,0},{1,5},{5,1},{2,6},{6,2},{3,7},{7,3},{8,12},{12,8},{9,1... | collective-permute-start | bytes 884744 | tf_op jit(solution)/shard_map/ppermute | solution.py:217
  10.6 6.4 %collective-permute-start.2 = (f32[288,128]{1,0:T(8,128)S(1)}, f32[288,128]{1,0:T(8,128)S(1)}, u32[]{:S(2)}, u32[]{:S(2)}) collective-permute-start(f32[288,128]{1,0:T(8,128)S(1)} %add.31), channel_id=1, source_target_pairs={{0,8},{4,60},{8,16},{12,4},{16,24},{20,12},{24,32},{28,20},{32,40}... | collective-permute-start | bytes 442376 | tf_op jit(solution)/shard_map/ppermute | solution.py:238
  14.6 5.3 %collective-permute-start.6 = (f32[288,128]{1,0:T(8,128)S(1)}, f32[288,128]{1,0:T(8,128)S(1)}, u32[]{:S(2)}, u32[]{:S(2)}) collective-permute-start(f32[288,128]{1,0:T(8,128)S(1)} %add.35), channel_id=1, source_target_pairs={{0,8},{4,60},{8,16},{12,4},{16,24},{20,12},{24,32},{28,20},{32,40}... | collective-permute-start | bytes 442376 | tf_op jit(solution)/shard_map/ppermute | solution.py:238
  15.4 6.0 %collective-permute-start.11 = (f32[288,128]{1,0:T(8,128)S(1)}, f32[288,128]{1,0:T(8,128)S(1)}, u32[]{:S(2)}, u32[]{:S(2)}) collective-permute-start(f32[288,128]{1,0:T(8,128)S(1)} %add.39), channel_id=1, source_target_pairs={{0,8},{4,60},{8,16},{12,4},{16,24},{20,12},{24,32},{28,20},{32,40}... | collective-permute-start | bytes 442376 | tf_op jit(solution)/shard_map/ppermute | solution.py:238
  16.2 6.8 %collective-permute-start.14 = (f32[288,128]{1,0:T(8,128)S(1)}, f32[288,128]{1,0:T(8,128)S(1)}, u32[]{:S(2)}, u32[]{:S(2)}) collective-permute-start(f32[288,128]{1,0:T(8,128)S(1)} %add.42), channel_id=1, source_target_pairs={{0,8},{4,60},{8,16},{12,4},{16,24},{20,12},{24,32},{28,20},{32,40}... | collective-permute-start | bytes 442376 | tf_op jit(solution)/shard_map/ppermute | solution.py:238
  17.1 7.5 %collective-permute-start.3 = (f32[288,128]{1,0:T(8,128)S(1)}, f32[288,128]{1,0:T(8,128)S(1)}, u32[]{:S(2)}, u32[]{:S(2)}) collective-permute-start(f32[288,128]{1,0:T(8,128)S(1)} %add.32), channel_id=1, source_target_pairs={{0,8},{4,60},{8,16},{12,4},{16,24},{20,12},{24,32},{28,20},{32,40}... | collective-permute-start | bytes 442376 | tf_op jit(solution)/shard_map/ppermute | solution.py:238
  19.9 6.3 %collective-permute-start.7 = (f32[288,128]{1,0:T(8,128)S(1)}, f32[288,128]{1,0:T(8,128)S(1)}, u32[]{:S(2)}, u32[]{:S(2)}) collective-permute-start(f32[288,128]{1,0:T(8,128)S(1)} %add.36), channel_id=1, source_target_pairs={{0,8},{4,60},{8,16},{12,4},{16,24},{20,12},{24,32},{28,20},{32,40}... | collective-permute-start | bytes 442376 | tf_op jit(solution)/shard_map/ppermute | solution.py:238
  21.5 6.3 %collective-permute-start.12 = (f32[288,128]{1,0:T(8,128)S(1)}, f32[288,128]{1,0:T(8,128)S(1)}, u32[]{:S(2)}, u32[]{:S(2)}) collective-permute-start(f32[288,128]{1,0:T(8,128)S(1)} %add.40), channel_id=1, source_target_pairs={{0,8},{4,60},{8,16},{12,4},{16,24},{20,12},{24,32},{28,20},{32,40}... | collective-permute-start | bytes 442376 | tf_op jit(solution)/shard_map/ppermute | solution.py:238
  23.1 6.3 %collective-permute-start.15 = (f32[288,128]{1,0:T(8,128)S(1)}, f32[288,128]{1,0:T(8,128)S(1)}, u32[]{:S(2)}, u32[]{:S(2)}) collective-permute-start(f32[288,128]{1,0:T(8,128)S(1)} %add.43), channel_id=1, source_target_pairs={{0,8},{4,60},{8,16},{12,4},{16,24},{20,12},{24,32},{28,20},{32,40}... | collective-permute-start | bytes 442376 | tf_op jit(solution)/shard_map/ppermute | solution.py:238
  24.6 6.5 %collective-permute-start.4 = (f32[288,128]{1,0:T(8,128)S(1)}, f32[288,128]{1,0:T(8,128)S(1)}, u32[]{:S(2)}, u32[]{:S(2)}) collective-permute-start(f32[288,128]{1,0:T(8,128)S(1)} %add.33), channel_id=1, source_target_pairs={{0,8},{4,60},{8,16},{12,4},{16,24},{20,12},{24,32},{28,20},{32,40}... | collective-permute-start | bytes 442376 | tf_op jit(solution)/shard_map/ppermute | solution.py:238
  26.2 6.3 %collective-permute-start.8 = (f32[288,128]{1,0:T(8,128)S(1)}, f32[288,128]{1,0:T(8,128)S(1)}, u32[]{:S(2)}, u32[]{:S(2)}) collective-permute-start(f32[288,128]{1,0:T(8,128)S(1)} %add.37), channel_id=1, source_target_pairs={{0,8},{4,60},{8,16},{12,4},{16,24},{20,12},{24,32},{28,20},{32,40}... | collective-permute-start | bytes 442376 | tf_op jit(solution)/shard_map/ppermute | solution.py:238
  27.8 6.3 %collective-permute-start.13 = (f32[288,128]{1,0:T(8,128)S(1)}, f32[288,128]{1,0:T(8,128)S(1)}, u32[]{:S(2)}, u32[]{:S(2)}) collective-permute-start(f32[288,128]{1,0:T(8,128)S(1)} %add.41), channel_id=1, source_target_pairs={{0,8},{4,60},{8,16},{12,4},{16,24},{20,12},{24,32},{28,20},{32,40}... | collective-permute-start | bytes 442376 | tf_op jit(solution)/shard_map/ppermute | solution.py:238
  29.4 5.5 %collective-permute-start.16 = (f32[288,128]{1,0:T(8,128)S(1)}, f32[288,128]{1,0:T(8,128)S(1)}, u32[]{:S(2)}, u32[]{:S(2)}) collective-permute-start(f32[288,128]{1,0:T(8,128)S(1)} %add.44), channel_id=1, source_target_pairs={{0,8},{4,60},{8,16},{12,4},{16,24},{20,12},{24,32},{28,20},{32,40}... | collective-permute-start | bytes 442376 | tf_op jit(solution)/shard_map/ppermute | solution.py:238
  31.1 5.3 %collective-permute-start.5 = (f32[288,128]{1,0:T(8,128)S(1)}, f32[288,128]{1,0:T(8,128)S(1)}, u32[]{:S(2)}, u32[]{:S(2)}) collective-permute-start(f32[288,128]{1,0:T(8,128)S(1)} %add.34), channel_id=1, source_target_pairs={{0,8},{4,60},{8,16},{12,4},{16,24},{20,12},{24,32},{28,20},{32,40}... | collective-permute-start | bytes 442376 | tf_op jit(solution)/shard_map/ppermute | solution.py:238
  32.5 12.2 %copy-start.2 = (bf16[1,4608]{1,0:T(2,128)(2,1)S(1)}, bf16[1,4608]{1,0:T(2,128)(2,1)}, u32[]{:S(2)}) copy-start(bf16[1,4608]{1,0:T(2,128)(2,1)} %param.7) | copy-start | bytes 27652
  32.6 5.6 %collective-permute-start.9 = (f32[288,128]{1,0:T(8,128)S(1)}, f32[288,128]{1,0:T(8,128)S(1)}, u32[]{:S(2)}, u32[]{:S(2)}) collective-permute-start(f32[288,128]{1,0:T(8,128)S(1)} %add.38), channel_id=1, source_target_pairs={{0,8},{4,60},{8,16},{12,4},{16,24},{20,12},{24,32},{28,20},{32,40}... | collective-permute-start | bytes 442376 | tf_op jit(solution)/shard_map/ppermute | solution.py:238
  34.1 5.6 %collective-permute-start.19 = (f32[288,128]{1,0:T(8,128)S(1)}, f32[288,128]{1,0:T(8,128)S(1)}, u32[]{:S(2)}, u32[]{:S(2)}) collective-permute-start(f32[288,128]{1,0:T(8,128)S(1)} %collective-permute-done.13.r2), channel_id=1, source_target_pairs={{0,4},{4,0},{1,5},{5,1},{2,6},{6,2},{3,7},{7,3},{8,12},{12,8},{9,1... | collective-permute-start | bytes 442376 | tf_op jit(solution)/shard_map/ppermute | solution.py:240
  34.9 4.9 %collective-permute-start.20 = (f32[288,128]{1,0:T(8,128)S(1)}, f32[288,128]{1,0:T(8,128)S(1)}, u32[]{:S(2)}, u32[]{:S(2)}) collective-permute-start(f32[288,128]{1,0:T(8,128)S(1)} %collective-permute-done.16.r3), channel_id=1, source_target_pairs={{0,4},{4,0},{1,5},{5,1},{2,6},{6,2},{3,7},{7,3},{8,12},{12,8},{9,1... | collective-permute-start | bytes 442376 | tf_op jit(solution)/shard_map/ppermute | solution.py:240
  36.4 3.3 %collective-permute-start.17 = (f32[288,128]{1,0:T(8,128)S(1)}, f32[288,128]{1,0:T(8,128)S(1)}, u32[]{:S(2)}, u32[]{:S(2)}) collective-permute-start(f32[288,128]{1,0:T(8,128)S(1)} %collective-permute-done.5.r0), channel_id=1, source_target_pairs={{0,4},{4,0},{1,5},{5,1},{2,6},{6,2},{3,7},{7,3},{8,12},{12,8},{9,1... | collective-permute-start | bytes 442376 | tf_op jit(solution)/shard_map/ppermute | solution.py:240
  38.1 2.6 %collective-permute-start.18 = (f32[288,128]{1,0:T(8,128)S(1)}, f32[288,128]{1,0:T(8,128)S(1)}, u32[]{:S(2)}, u32[]{:S(2)}) collective-permute-start(f32[288,128]{1,0:T(8,128)S(1)} %collective-permute-done.9.r1), channel_id=1, source_target_pairs={{0,4},{4,0},{1,5},{5,1},{2,6},{6,2},{3,7},{7,3},{8,12},{12,8},{9,1... | collective-permute-start | bytes 442376 | tf_op jit(solution)/shard_map/ppermute | solution.py:240
  40.8 4.0 %collective-permute-start.21 = (f32[144,128]{1,0:T(8,128)S(1)}, f32[144,128]{1,0:T(8,128)S(1)}, u32[]{:S(2)}, u32[]{:S(2)}) collective-permute-start(f32[144,128]{1,0:T(8,128)S(1)} %get-tuple-element.25), channel_id=1, source_target_pairs={{0,64},{64,0},{128,192},{192,128},{1,65},{65,1},{129,193},{193,129... | collective-permute-start | bytes 221192 | tf_op jit(solution)/shard_map/ppermute | solution.py:253
  42.1 5.7 %collective-permute-start.22 = (f32[144,128]{1,0:T(8,128)S(1)}, f32[144,128]{1,0:T(8,128)S(1)}, u32[]{:S(2)}, u32[]{:S(2)}) collective-permute-start(f32[144,128]{1,0:T(8,128)S(1)} %get-tuple-element.26), channel_id=1, source_target_pairs={{0,128},{64,192},{128,0},{192,64},{1,129},{65,193},{129,1},{193,65... | collective-permute-start | bytes 221192 | tf_op jit(solution)/shard_map/ppermute | solution.py:253
  44.6 4.9 %collective-permute-start.23 = (f32[144,128]{1,0:T(8,128)S(1)}, f32[144,128]{1,0:T(8,128)S(1)}, u32[]{:S(2)}, u32[]{:S(2)}) collective-permute-start(f32[144,128]{1,0:T(8,128)S(1)} %get-tuple-element.27), channel_id=1, source_target_pairs={{0,192},{64,128},{128,64},{192,0},{1,193},{65,129},{129,65},{193,1... | collective-permute-start | bytes 221192 | tf_op jit(solution)/shard_map/ppermute | solution.py:253
  50.2 2.4 %collective-permute-start.24 = (f32[1,128]{1,0:T(1,128)S(1)}, f32[1,128]{1,0:T(1,128)S(1)}, u32[]{:S(2)}, u32[]{:S(2)}) collective-permute-start(f32[1,128]{1,0:T(1,128)S(1)} %get-tuple-element.29), channel_id=1, source_target_pairs={{0,4},{4,0},{1,5},{5,1},{2,6},{6,2},{3,7},{7,3},{8,12},{12,8},{9,1... | collective-permute-start | bytes 1544 | tf_op jit(solution)/shard_map/ppermute | solution.py:265
